TPU v7x, 256 devices: a whole 4x4x8 slice. The times are simulated.
256 devices in a mesh: seq: 32 (over z, x), tp: 8 (over y, core).
Axes of the slice: x: 4, y: 4, z: 8, core: 2. Of those that a mesh axis runs over, the one named last changes fastest.
Arguments:
- packed_input: int32 [2048, 5120], P('seq', 'tp'), may hold values from -2147483648 to 2147483646
- block_exponent: int32 [40, 16384], P('tp', 'seq'), may hold values from -5 to -1
- gate_input: bfloat16 [16384, 5120], P('seq', 'tp'), may hold values from -80 to 80
- state_write: bfloat16 [16384, 128], P('seq'), may hold values from -6 to 6
- state_read: bfloat16 [16384, 128], P('seq'), may hold values from -6 to 6
- log_decay: float32 [80, 16384], P('tp', 'seq'), may hold values from -1.6 to 0
- skip_weight: float32 [80], P('tp'), may hold values from 0.3 to 3
- norm_gain: float32 [5120], P('tp'), may hold values from 0.5 to 1.5
- out_weight: bfloat16 [5120, 2560], P('tp'), may hold values from -0.078125 to 0.078125
- out_cotangent: bfloat16 [16384, 2560], P('seq', 'tp'), may hold values from -6 to 6
Outputs:
- grad_input: bfloat16 [16384, 5120], P('seq', 'tp')
- grad_gate: bfloat16 [16384, 5120], P('seq', 'tp')
- grad_write: float32 [16384, 128], P('seq')
- grad_read: float32 [16384, 128], P('seq')
- grad_decay: float32 [80, 16384], P('tp', 'seq')
- grad_skip: float32 [80], P('tp')
- grad_gain: float32 [5120], P('tp')
- grad_out_weight: float32 [5120, 2560], P('tp', 'seq')
All inputs are finite; a program needn't handle non-finite values.
Results may differ from a plain program's by a relative error of at most 0.0049.
Values may be sent and summed in bfloat16 or wider, within the bound.
A program may use at most 128 MiB of HBM per device.

v0:
```python
import jax
import jax.numpy as jnp
from jax import lax
from jax.sharding import Mesh
from jax.sharding import PartitionSpec as P

SEQ = ("seq_0", "seq_1")


PRECISE = lax.Precision.HIGHEST


def nothing_yet(shard, identity):
    return jax.tree.map(
        lambda part, zero: jnp.zeros_like(part) + jnp.asarray(zero, part.dtype), shard, identity
    )


def prefix_by_axis(shard, axes, combine, identity, reverse):
    before = start = nothing_yet(shard, identity)
    total = shard
    for axis in reversed(axes):
        size, here = (lax.axis_size(axis), lax.axis_index(axis))
        pieces = jax.tree.map(lambda part: lax.all_gather(part, axis), total)
        inside, total = (start, start)
        for k in reversed(range(size)) if reverse else range(size):
            passed = k > here if reverse else k < here
            total = combine(total, jax.tree.map(lambda part: part[k], pieces))
            inside = jax.tree.map(lambda new, old: jnp.where(passed, new, old), total, inside)
        before = combine(inside, before)
    return before


def sent_to_all(shard, axis):
    copies = jnp.broadcast_to(shard, (lax.axis_size(axis), *shard.shape))
    return lax.all_to_all(copies, axis, split_axis=0, concat_axis=0, tiled=True)


def taken_together(shard, axis):
    return sent_to_all(shard, axis).sum(axis=0)


def laid_out(tiles, dim):
    tiles = jnp.moveaxis(tiles, 0, dim)
    shape = tiles.shape
    return tiles.reshape(*shape[:dim], shape[dim] * shape[dim + 1], *shape[dim + 2 :])


def collect(shard, axis, dim):
    return laid_out(sent_to_all(shard, axis), dim)


def scatter_axes(shard, axes, dim):
    if not axes:
        return shard
    nearer = lax.psum_scatter(shard, axes[0], scatter_dimension=dim, tiled=True)
    return scatter_axes(nearer, axes[1:], dim)


def dequantize(packed_words, exponents):
    shifts = 4 * jnp.arange(8, dtype=jnp.int32)
    fields = (
        jnp.bitwise_and(jnp.right_shift(packed_words[:, None, :], shifts[None, :, None]), 15) - 8
    )
    fields = fields.reshape(packed_words.shape[0] * 8, packed_words.shape[1])
    factors = jnp.exp2(exponents.astype(jnp.float32))
    group_width = fields.shape[1] // exponents.shape[0]
    factors = jnp.repeat(factors.T, group_width, axis=1)
    return (fields.astype(jnp.float32) * factors).astype(jnp.bfloat16)


def lower_decays(seg_sum):
    length = seg_sum.shape[1]
    is_lower = (jnp.arange(length)[:, None] >= jnp.arange(length)[None, :])[None]
    spread = seg_sum[:, :, None] - seg_sum[:, None, :]
    return jnp.where(is_lower, jnp.exp(jnp.where(is_lower, spread, 0.0)), 0.0)


def forward_join(earlier, later):
    return (earlier[0] + later[0], jnp.exp(later[0])[:, None, None] * earlier[1] + later[1])


def backward_join(earlier, later):
    return (earlier[0] + later[0], later[1] + jnp.exp(later[0])[:, None, None] * earlier[1])


def on_device(
    packed_input,
    block_exponent,
    gate_input,
    state_write,
    state_read,
    log_decay,
    skip_weight,
    norm_gain,
    out_weight,
    out_cotangent,
):
    head_count, length = log_decay.shape
    x_values = dequantize(packed_input, block_exponent)
    width = x_values.shape[1]
    head_width = width // head_count
    x_heads = x_values.astype(jnp.float32).reshape(length, head_count, head_width)
    write_rows = state_write.astype(jnp.float32)
    read_rows = state_read.astype(jnp.float32)
    decay_sum = jnp.cumsum(log_decay, axis=1)
    decay_total = decay_sum[:, -1]
    to_end = jnp.exp(decay_total[:, None] - decay_sum)
    local_state = jnp.einsum(
        "lhp,ln->hpn", x_heads * to_end.T[:, :, None], write_rows, precision=PRECISE
    )
    zero_pair = (jnp.zeros_like(decay_total), jnp.zeros_like(local_state))
    state_in = prefix_by_axis((decay_total, local_state), SEQ, forward_join, zero_pair, False)[1]
    block_len = min(256, length)
    block_count = length // block_len
    saved = []
    core_parts = []
    state_now = state_in
    for block_index in range(block_count):
        first_row = block_index * block_len
        x_part = x_heads[first_row : first_row + block_len]
        write_part = write_rows[first_row : first_row + block_len]
        read_part = read_rows[first_row : first_row + block_len]
        seg_sum = jnp.cumsum(log_decay[:, first_row : first_row + block_len], axis=1)
        decay_matrix = lower_decays(seg_sum)
        cross = jnp.dot(read_part, write_part.T, precision=PRECISE)
        mixing = decay_matrix * cross[None]
        read_start = jnp.einsum("in,hpn->ihp", read_part, state_now, precision=PRECISE)
        core_parts.append(
            jnp.einsum("hij,jhp->ihp", mixing, x_part, precision=PRECISE)
            + jnp.exp(seg_sum).T[:, :, None] * read_start
        )
        saved.append((seg_sum, decay_matrix, cross, mixing, read_start, state_now))
        end_weight = jnp.exp(seg_sum[:, -1:] - seg_sum)
        state_now = jnp.exp(seg_sum[:, -1])[:, None, None] * state_now + jnp.einsum(
            "jhp,jn->hpn", x_part * end_weight.T[:, :, None], write_part, precision=PRECISE
        )
    core = jnp.concatenate(core_parts, axis=0)
    y_full = (core + skip_weight[None, :, None] * x_heads).reshape(length, width)
    gate = gate_input.astype(jnp.float32)
    sigma = jax.nn.sigmoid(gate)
    active = gate * sigma
    mixed = y_full * active
    total_width = width * lax.axis_size("tp")
    squares = taken_together(jnp.sum(mixed * mixed, axis=1), "tp")
    scale_row = lax.rsqrt(squares / total_width + 1e-05)[:, None]
    normed = (mixed * scale_row * norm_gain).astype(jnp.bfloat16)
    shard_piece = collect(out_cotangent, "tp", 1)
    project_grad_part = lax.dot_general(
        shard_piece, out_weight, (((1,), (1,)), ((), ())), preferred_element_type=jnp.float32
    )
    product = lax.dot_general(
        normed, shard_piece, (((0,), (0,)), ((), ())), preferred_element_type=jnp.float32
    )
    rounded = lax.optimization_barrier(product.astype(jnp.bfloat16))
    weight_part = rounded.astype(jnp.float32)
    grad_v, weight_part = (project_grad_part, weight_part)
    grad_out_weight = scatter_axes(weight_part, SEQ, 1)
    scaled = grad_v * norm_gain
    gain_part = jnp.sum(grad_v * mixed * scale_row, axis=0)
    inner = taken_together(jnp.sum(scaled * mixed, axis=1), "tp")[:, None]
    grad_mixed = (
        scale_row * scaled - mixed * (scale_row * scale_row * scale_row) * inner / total_width
    )
    grad_gate = (grad_mixed * y_full * sigma * (1.0 + gate * (1.0 - sigma))).astype(jnp.bfloat16)
    grad_y = (grad_mixed * active).reshape(length, head_count, head_width)
    skip_part = jnp.sum(grad_y * x_heads, axis=(0, 2))
    grad_gain, grad_skip = (taken_together(gain_part, SEQ), taken_together(skip_part, SEQ))
    from_start = jnp.exp(decay_sum)
    local_cot = jnp.einsum(
        "lhp,ln->hpn", grad_y * from_start.T[:, :, None], read_rows, precision=PRECISE
    )
    cot_in = prefix_by_axis((decay_total, local_cot), SEQ, backward_join, zero_pair, True)[1]
    grad_x_parts = []
    grad_b_parts = []
    grad_c_parts = []
    grad_a_parts = []
    carry_cot = cot_in
    last_marker = (jnp.arange(block_len) == block_len - 1).astype(jnp.float32)[None, :]
    for block_index in reversed(range(block_count)):
        first_row = block_index * block_len
        x_part = x_heads[first_row : first_row + block_len]
        write_part = write_rows[first_row : first_row + block_len]
        read_part = read_rows[first_row : first_row + block_len]
        grad_part = grad_y[first_row : first_row + block_len]
        seg_sum, decay_matrix, cross, mixing, read_start, state_start = saved[block_index]
        end_weight = jnp.exp(seg_sum[:, -1:] - seg_sum)
        start_weight = jnp.exp(seg_sum)
        pair_dot = jnp.einsum("ihp,jhp->hij", grad_part, x_part, precision=PRECISE)
        weighted = pair_dot * decay_matrix
        summed = jnp.sum(weighted, axis=0)
        cot_write = jnp.einsum("jn,hpn->jhp", write_part, carry_cot, precision=PRECISE)
        grad_x_parts.append(
            skip_weight[None, :, None] * grad_part
            + jnp.einsum("hij,ihp->jhp", mixing, grad_part, precision=PRECISE)
            + end_weight.T[:, :, None] * cot_write
        )
        grad_b_parts.append(
            jnp.dot(summed.T, read_part, precision=PRECISE)
            + jnp.einsum(
                "jhp,hpn->jn", x_part * end_weight.T[:, :, None], carry_cot, precision=PRECISE
            )
        )
        scaled_grad = grad_part * start_weight.T[:, :, None]
        grad_c_parts.append(
            jnp.dot(summed, write_part, precision=PRECISE)
            + jnp.einsum("ihp,hpn->in", scaled_grad, state_start, precision=PRECISE)
        )
        pair_terms = weighted * cross[None]
        seg_grad = jnp.sum(pair_terms, axis=2) - jnp.sum(pair_terms, axis=1)
        seg_grad = seg_grad + jnp.sum(grad_part * read_start, axis=2).T * start_weight
        leaving = jnp.sum(x_part * cot_write, axis=2).T * end_weight
        seg_grad = seg_grad - leaving
        final_term = jnp.sum(leaving, axis=1) + jnp.exp(seg_sum[:, -1]) * jnp.sum(
            carry_cot * state_start, axis=(1, 2)
        )
        seg_grad = seg_grad + final_term[:, None] * last_marker
        grad_a_parts.append(jnp.flip(jnp.cumsum(jnp.flip(seg_grad, 1), axis=1), 1))
        carry_cot = jnp.exp(seg_sum[:, -1])[:, None, None] * carry_cot + jnp.einsum(
            "ihp,in->hpn", scaled_grad, read_part, precision=PRECISE
        )
    grad_input = (
        jnp.concatenate(grad_x_parts[::-1], axis=0).reshape(length, width).astype(jnp.bfloat16)
    )
    grad_write, grad_read = (
        taken_together(jnp.concatenate(grad_b_parts[::-1], axis=0), "tp"),
        taken_together(jnp.concatenate(grad_c_parts[::-1], axis=0), "tp"),
    )
    grad_decay = jnp.concatenate(grad_a_parts[::-1], axis=1)
    return (
        grad_input,
        grad_gate,
        grad_write,
        grad_read,
        grad_decay,
        grad_skip,
        grad_gain,
        grad_out_weight,
    )


def solution(mesh):
    torus = Mesh(mesh.devices.reshape(8, 4, mesh.shape["tp"]), ("seq_0", "seq_1", "tp"))
    in_specs = (
        P(SEQ, "tp"),
        P("tp", SEQ),
        P(SEQ, "tp"),
        P(SEQ, None),
        P(SEQ, None),
        P("tp", SEQ),
        P("tp"),
        P("tp"),
        P("tp", None),
        P(SEQ, "tp"),
    )
    out_specs = (
        P(SEQ, "tp"),
        P(SEQ, "tp"),
        P(SEQ, None),
        P(SEQ, None),
        P("tp", SEQ),
        P("tp"),
        P("tp"),
        P("tp", SEQ),
    )
    return jax.shard_map(
        on_device, mesh=torus, in_specs=in_specs, out_specs=out_specs, check_vma=False
    )
```

profile of v0, /device:TPU:1, one launch (start us, length us, event | category | flops | bytes accessed | tf_op | source)
XLA Modules:
  0.0 384.4 jit_solution(11967336934109624141)
XLA Ops:
  13.5 3.7 shift_right_arithmetic.39
  17.2 3.8 copy.263
  21.0 3.0 fusion.31
  25.6 9.3 %all-reduce = f32[40]{0:T(128)S(1)} all-reduce(f32[40]{0:T(128)S(1)} %dynamic-update-slice), channel_id=2, replica_groups=mesh['seq_0'=8,'seq_1'=4,'tp'=8] {'seq_1'}, use_global_device_ids=true, to_apply=%add | all-reduce | flops 40 | bytes 320
  36.0 18.1 %all-gather.14.cloned.1.call-done = f32[40,64,128]{2,1,0:T(8,128)} async-done(((f32[10,64,128]{2,1,0:T(8,128)}), f32[40,64,128]{2,1,0:T(8,128)}) %all-gather.14.cloned.1.call-update) | async-done | bytes 1310736 | tf_op jit(solution)/shard_map/all_gather | solution.py:24
  78.5 14.6 %all-gather.3 = f32[8,1,10]{2,1,0:T(1,128)S(1)} all-gather(f32[1,1,10]{2,1,0:T(1,128)S(1)} %get-tuple-element.132), channel_id=1, replica_groups=mesh['seq_0'=8,'seq_1'=4,'tp'=8] {'seq_0'}, dimensions={0}, use_global_device_ids=true | all-gather | bytes 360 | tf_op jit(solution)/shard_map/all_gather | solution.py:24
  98.8 2.9 fusion.105
  105.3 2.9 fusion.63
  110.4 4.2 %fusion.69 = f32[256,10,64]{0,2,1:T(8,128)} fusion(bf16[256,10,64]{0,2,1:T(8,128)(2,1)} %bitcast.439, f32[256,256]{1,0:T(8,128)} %fusion.244, f32[10,256]{1,0:T(8,128)} %bitcast.430, pred[256,256]{1,0:T(8,128)(4,1)} %iota_compare_fusion, f32[256,10,64]{0,2,1:T(8,128)} %convolution_bitcast_fusion.2, f32[256,10]{0,1:T(8,128)} %exponential_bitcast_fusion.3), kind=kOutput, calls=%fused_computation.70 | convolution fusion | flops 506265600 | bytes 1986560 | tf_op jit(solution)/shard_map/hij,jhp->ihp/dot_general | solution.py:130
  116.8 3.4 multiply_reduce_fusion.7
  120.2 12.8 %all_to_all.39 = f32[8,1,512]{2,1,0:T(1,128)} all-to-all(f32[8,1,512]{2,1,0:T(1,128)S(1)} %broadcast_in_dim.63), channel_id=1, replica_groups=mesh['seq_0'=8,'seq_1'=4,'tp'=8] {'tp'}, dimensions={0} | all-to-all | bytes 32768 | tf_op jit(solution)/shard_map/all_to_all | solution.py:36
  134.7 5.0 %all-to-all-start.1 = ((bf16[8,512,320]{1,2,0:T(8,128)(2,1)}), bf16[8,512,320]{1,2,0:T(8,128)(2,1)}, u32[]{:S(2)}, u32[]{:S(2)}) async-start(bf16[8,512,320]{1,2,0:T(8,128)(2,1)} %broadcast_in_dim.64), calls=%async_computation.1 | async-start | bytes 5242880 | tf_op jit(solution)/shard_map/all_to_all | solution.py:36
  142.3 29.4 %all-to-all-done.1 = bf16[8,512,320]{1,2,0:T(8,128)(2,1)} async-done(((bf16[8,512,320]{1,2,0:T(8,128)(2,1)}), bf16[8,512,320]{1,2,0:T(8,128)(2,1)}, u32[]{:S(2)}, u32[]{:S(2)}) %all-to-all-start.1) | async-done | bytes 2621472 | tf_op jit(solution)/shard_map/all_to_all | solution.py:36
  171.7 6.0 %multiply_reduce_fusion.4 = (f32[640]{0:T(1024)}, f32[512]{0:T(512)S(1)}, f32[512,640]{1,0:T(8,128)}) fusion(f32[512,640]{1,0:T(8,128)} %get-tuple-element.87, f32[512]{0:T(512)} %get-tuple-element.121, f32[640]{0:T(1024)} %param.17, bf16[512,2560]{0,1:T(8,128)(2,1)} %bitcast.47, bf16[640,2560]{1,0:T(8,128)(2,1)S(1)} %copy-done), kind=kOutput, calls=%fused_computation.32 | convolution fusion | flops 1679686528 | bytes 8528896 | tf_op jit(solution)/shard_map/dot_general | solution.py:149
  177.7 8.2 %all_to_all.40 = f32[8,1,512]{2,1,0:T(1,128)S(1)} all-to-all(f32[8,1,512]{2,1,0:T(1,128)S(1)} %broadcast_in_dim.65), channel_id=1, replica_groups=mesh['seq_0'=8,'seq_1'=4,'tp'=8] {'tp'}, dimensions={0} | all-to-all | bytes 32768 | tf_op jit(solution)/shard_map/all_to_all | solution.py:36
  185.9 5.1 %multiply_reduce_fusion.5 = (f32[640]{0:T(1024)}, f32[512,640]{1,0:T(8,128)S(1)}, bf16[512,640]{1,0:T(8,128)(2,1)}) fusion(bf16[512,640]{1,0:T(8,128)(2,1)} %copy-done.2, bf16[512,640]{1,0:T(8,128)(2,1)} %param.12, f32[512]{0:T(512)S(1)} %reduce_sum.234, f32[512,640]{1,0:T(8,128)} %get-tuple-element.87, f32[512]{0:T(512)} %get-tuple-element.120, ...), kind=kLoop, calls=%fused_computation.33 | loop fusion | flops 8191360 | bytes 7222784 | tf_op jit(solution)/shard_map/reduce_sum | solution.py:167
  193.3 22.7 %all-gather.16.cloned.1.call-done = f32[40,64,128]{2,1,0:T(8,128)} async-done(((f32[10,64,128]{2,1,0:T(8,128)}), f32[40,64,128]{2,1,0:T(8,128)}) %all-gather.16.cloned.1.call-update) | async-done | bytes 1310736 | tf_op jit(solution)/shard_map/all_gather | solution.py:24
  218.3 5.6 %convolution_convert_fusion = bf16[640,2560]{1,0:T(8,128)(2,1)} fusion(bf16[512,2560]{0,1:T(8,128)(2,1)} %bitcast.47, f32[512,640]{1,0:T(8,128)S(1)} %copy-done.8, f32[640]{0:T(1024)S(1)} %copy-done.81, f32[512]{0:T(512)S(1)} %copy-done.72), kind=kOutput, calls=%fused_computation | convolution fusion | flops 1680343040 | bytes 7213568 | tf_op jit(solution)/shard_map/dot_general | solution.py:152
  223.8 6.1 %copy.292 = f32[640,2560]{0,1:T(8,128)} copy(bf16[640,2560]{1,0:T(8,128)(2,1)} %convolution_convert_fusion) | data formatting | bytes 9830400
  233.3 13.9 %all-gather.4 = f32[8,1,10]{2,1,0:T(1,128)S(1)} all-gather(f32[1,1,10]{2,1,0:T(1,128)S(1)} %copy-done.92), channel_id=1, replica_groups=mesh['seq_0'=8,'seq_1'=4,'tp'=8] {'seq_0'}, dimensions={0}, use_global_device_ids=true | all-gather | bytes 360 | tf_op jit(solution)/shard_map/all_gather | solution.py:24
  249.2 7.2 %all-to-all-start.5 = ((f32[32,1,10]{2,1,0:T(1,128)}), f32[32,1,10]{2,1,0:T(1,128)}, u32[]{:S(2)}, u32[]{:S(2)}) async-start(f32[32,1,10]{2,1,0:T(1,128)} %broadcast_in_dim.69), calls=%async_computation.5 | async-start | bytes 32768 | tf_op jit(solution)/shard_map/all_to_all | solution.py:36
  261.9 4.1 %multiply_reduce_fusion = (f32[10,256]{1,0:T(8,128)}, f32[10,256]{1,0:T(8,128)}, f32[256,256]{1,0:T(8,128)S(1)}) fusion(f32[256,256]{1,0:T(8,128)} %fusion.244, f32[10,256]{1,0:T(8,128)S(1)} %bitcast.432, pred[256,256]{1,0:T(8,128)(4,1)S(1)} %copy-done.48, f32[256,10,64]{0,2,1:T(8,128)S(1)} %bitcast.404, bf16[256,10,64]{0,2,1:T(8,128)(2,1)} %bitcast.440), kind=kOutput, calls=%fused_computation.11 | convolution fusion | flops 508488704 | bytes 1603584 | tf_op jit(solution)/shard_map/ihp,jhp->hij/dot_general | solution.py:189
  266.5 3.6 convolution_bitcast_fusion.5
  270.1 3.1 multiply_reduce_fusion.2
  276.1 2.9 multiply_reduce_fusion.12
  284.1 9.5 %all-to-all-start.6 = ((f32[32,1,640]{2,1,0:T(1,128)}), f32[32,1,640]{2,1,0:T(1,128)}, u32[]{:S(2)}, u32[]{:S(2)}) async-start(f32[32,1,640]{2,1,0:T(1,128)} %broadcast_in_dim.70), calls=%async_computation.6 | async-start | bytes 163840 | tf_op jit(solution)/shard_map/all_to_all | solution.py:36
  294.9 8.6 %all-to-all-done.6 = f32[32,1,640]{2,1,0:T(1,128)} async-done(((f32[32,1,640]{2,1,0:T(1,128)}), f32[32,1,640]{2,1,0:T(1,128)}, u32[]{:S(2)}, u32[]{:S(2)}) %all-to-all-start.6) | async-done | bytes 81952 | tf_op jit(solution)/shard_map/all_to_all | solution.py:36
  305.0 10.6 %all-to-all-start.4 = ((f32[8,512,128]{2,1,0:T(8,128)}), f32[8,512,128]{2,1,0:T(8,128)}, u32[]{:S(2)}, u32[]{:S(2)}) async-start(f32[8,512,128]{2,1,0:T(8,128)} %broadcast_in_dim.68), calls=%async_computation.4 | async-start | bytes 4194304 | tf_op jit(solution)/shard_map/all_to_all | solution.py:36
  327.3 3.3 convolution_bitcast_fusion.6
  331.0 10.9 %all-to-all-done.4 = f32[8,512,128]{2,1,0:T(8,128)} async-done(((f32[8,512,128]{2,1,0:T(8,128)}), f32[8,512,128]{2,1,0:T(8,128)}, u32[]{:S(2)}, u32[]{:S(2)}) %all-to-all-start.4) | async-done | bytes 2097184 | tf_op jit(solution)/shard_map/all_to_all | solution.py:36
  343.4 5.2 %all-to-all-start.3 = ((f32[8,512,128]{2,1,0:T(8,128)}), f32[8,512,128]{2,1,0:T(8,128)}, u32[]{:S(2)}, u32[]{:S(2)}) async-start(f32[8,512,128]{2,1,0:T(8,128)} %broadcast_in_dim.67), calls=%async_computation.3 | async-start | bytes 4194304 | tf_op jit(solution)/shard_map/all_to_all | solution.py:36
  363.6 11.3 %all-to-all-done.3 = f32[8,512,128]{2,1,0:T(8,128)} async-done(((f32[8,512,128]{2,1,0:T(8,128)}), f32[8,512,128]{2,1,0:T(8,128)}, u32[]{:S(2)}, u32[]{:S(2)}) %all-to-all-start.3) | async-done | bytes 2097184 | tf_op jit(solution)/shard_map/all_to_all | solution.py:36
  (386 shorter events, 107.1 us)
Async XLA Ops:
  7.2 164.5 %copy-start = (bf16[640,2560]{1,0:T(8,128)(2,1)S(1)}, bf16[640,2560]{1,0:T(8,128)(2,1)}, u32[]{:S(2)}) copy-start(bf16[640,2560]{1,0:T(8,128)(2,1)} %param.18) | copy-start | bytes 9830404
  7.2 46.9 %all-gather.14.cloned.1.call-start = ((), (), s32[]{:S(2)}) async-start(), calls=%async_computation.11 | async-start | bytes 1638400 | tf_op jit(solution)/shard_map/all_gather | solution.py:24
  24.0 32.4 %copy-start.105 = (f32[10]{0:T(128)S(1)}, f32[10]{0:T(128)}, u32[]{:S(2)}) copy-start(f32[10]{0:T(128)} %param.16) | copy-start | bytes 124
  24.0 33.2 %copy-start.46 = (f32[10,512]{1,0:T(8,128)S(1)}, f32[10,512]{1,0:T(8,128)}, u32[]{:S(2)}) copy-start(f32[10,512]{1,0:T(8,128)} %param.15) | copy-start | bytes 61444
  24.0 74.8 %all-gather.10.cloned.1.call-start = ((), (), s32[]{:S(2)}) async-start(), calls=%async_computation.9 | async-start | bytes 2949120 | tf_op jit(solution)/shard_map/all_gather | solution.py:24
  34.8 21.6 %copy-start.56 = (f32[40]{0:T(128)}, f32[40]{0:T(128)S(1)}, u32[]{:S(2)}) copy-start(f32[40]{0:T(128)S(1)} %all-reduce) | copy-start | bytes 484
  35.3 21.0 %copy-start.66 = (f32[10]{0:T(128)}, f32[10]{0:T(128)S(1)}, u32[]{:S(2)}) copy-start(f32[10]{0:T(128)S(1)} %get-tuple-element.129) | copy-start | bytes 124
  35.3 26.2 %copy-start.80 = (f32[10]{0:T(128)}, f32[10]{0:T(128)S(1)}, u32[]{:S(2)}) copy-start(f32[10]{0:T(128)S(1)} %get-tuple-element.130) | copy-start | bytes 124
  36.0 20.4 %copy-start.62 = (f32[10]{0:T(128)}, f32[10]{0:T(128)S(1)}, u32[]{:S(2)}) copy-start(f32[10]{0:T(128)S(1)} %get-tuple-element.127) | copy-start | bytes 124
  36.0 21.7 %copy-start.78 = (f32[10]{0:T(128)}, f32[10]{0:T(128)S(1)}, u32[]{:S(2)}) copy-start(f32[10]{0:T(128)S(1)} %get-tuple-element.124) | copy-start | bytes 124
  74.8 22.2 %copy-start.11 = (bf16[512,128]{1,0:T(8,128)(2,1)S(1)}, bf16[512,128]{1,0:T(8,128)(2,1)}, u32[]{:S(2)}) copy-start(bf16[512,128]{1,0:T(8,128)(2,1)} %param.14) | copy-start | bytes 393220
  116.8 16.2 %copy-start.35 = (bf16[512,320]{0,1:T(8,128)(2,1)S(1)}, bf16[512,320]{0,1:T(8,128)(2,1)}, u32[]{:S(2)}) copy-start(bf16[512,320]{0,1:T(8,128)(2,1)} %param.19) | copy-start | bytes 983044
  134.7 36.9 %all-to-all-start.1 = ((bf16[8,512,320]{1,2,0:T(8,128)(2,1)}), bf16[8,512,320]{1,2,0:T(8,128)(2,1)}, u32[]{:S(2)}, u32[]{:S(2)}) async-start(bf16[8,512,320]{1,2,0:T(8,128)(2,1)} %broadcast_in_dim.64), calls=%async_computation.1 | async-start | bytes 5242880 | tf_op jit(solution)/shard_map/all_to_all | solution.py:36
  139.7 76.3 %all-gather.16.cloned.1.call-start = ((), (), s32[]{:S(2)}) async-start(), calls=%async_computation.12 | async-start | bytes 1638400 | tf_op jit(solution)/shard_map/all_gather | solution.py:24
  191.4 24.6 %copy-start.63 = (f32[10]{0:T(128)S(1)}, f32[10]{0:T(128)}, u32[]{:S(2)}) copy-start(f32[10]{0:T(128)} %copy-done.62) | copy-start | bytes 124
  191.4 24.6 %copy-start.67 = (f32[10]{0:T(128)S(1)}, f32[10]{0:T(128)}, u32[]{:S(2)}) copy-start(f32[10]{0:T(128)} %copy-done.66) | copy-start | bytes 124
  191.4 24.6 %copy-start.73 = (f32[10]{0:T(128)S(1)}, f32[10]{0:T(128)}, u32[]{:S(2)}) copy-start(f32[10]{0:T(128)} %get-tuple-element.125) | copy-start | bytes 124
  191.4 24.6 %copy-start.75 = (f32[10]{0:T(128)S(1)}, f32[10]{0:T(128)}, u32[]{:S(2)}) copy-start(f32[10]{0:T(128)} %get-tuple-element.128) | copy-start | bytes 124
  193.2 25.0 %copy-start.8 = (f32[512,640]{1,0:T(8,128)S(1)}, f32[512,640]{1,0:T(8,128)}, u32[]{:S(2)}) copy-start(f32[512,640]{1,0:T(8,128)} %get-tuple-element.87) | copy-start | bytes 3932164
  193.2 25.0 %copy-start.72 = (f32[512]{0:T(512)S(1)}, f32[512]{0:T(512)}, u32[]{:S(2)}) copy-start(f32[512]{0:T(512)} %get-tuple-element.121) | copy-start | bytes 6148
  193.2 25.0 %copy-start.81 = (f32[640]{0:T(1024)S(1)}, f32[640]{0:T(1024)}, u32[]{:S(2)}) copy-start(f32[640]{0:T(1024)} %param.17) | copy-start | bytes 7684
  193.3 82.0 %all-gather.12.cloned.1.call-start = ((), (), s32[]{:S(2)}) async-start(), calls=%async_computation.10 | async-start | bytes 2949120 | tf_op jit(solution)/shard_map/all_gather | solution.py:24
  218.2 130.4 %reduce-scatter.7.cloned.1.call-start = ((), (), s32[]{:S(2)}) async-start(), calls=%async_computation.13 | async-start | bytes 7372800
  232.2 16.2 %copy-start.57 = (f32[640]{0:T(1024)S(1)}, f32[640]{0:T(1024)}, u32[]{:S(2)}) copy-start(f32[640]{0:T(1024)} %get-tuple-element.80) | copy-start | bytes 7684
  249.2 33.6 %all-to-all-start.5 = ((f32[32,1,10]{2,1,0:T(1,128)}), f32[32,1,10]{2,1,0:T(1,128)}, u32[]{:S(2)}, u32[]{:S(2)}) async-start(f32[32,1,10]{2,1,0:T(1,128)} %broadcast_in_dim.69), calls=%async_computation.5 | async-start | bytes 32768 | tf_op jit(solution)/shard_map/all_to_all | solution.py:36
  260.0 14.2 %copy-start.14 = (f32[256,640]{0,1:T(8,128)}, f32[256,640]{0,1:T(8,128)S(1)}, u32[]{:S(2)}) copy-start(f32[256,640]{0,1:T(8,128)S(1)} %copy.272) | copy-start | bytes 1966084
  282.0 21.5 %copy-start.22 = (f32[512,128]{1,0:T(8,128)S(1)}, f32[512,128]{1,0:T(8,128)}, u32[]{:S(2)}) copy-start(f32[512,128]{1,0:T(8,128)} %pad_maximum_fusion.2) | copy-start | bytes 786436
  284.1 19.4 %all-to-all-start.6 = ((f32[32,1,640]{2,1,0:T(1,128)}), f32[32,1,640]{2,1,0:T(1,128)}, u32[]{:S(2)}, u32[]{:S(2)}) async-start(f32[32,1,640]{2,1,0:T(1,128)} %broadcast_in_dim.70), calls=%async_computation.6 | async-start | bytes 163840 | tf_op jit(solution)/shard_map/all_to_all | solution.py:36
  305.0 36.9 %all-to-all-start.4 = ((f32[8,512,128]{2,1,0:T(8,128)}), f32[8,512,128]{2,1,0:T(8,128)}, u32[]{:S(2)}, u32[]{:S(2)}) async-start(f32[8,512,128]{2,1,0:T(8,128)} %broadcast_in_dim.68), calls=%async_computation.4 | async-start | bytes 4194304 | tf_op jit(solution)/shard_map/all_to_all | solution.py:36
  343.4 31.5 %all-to-all-start.3 = ((f32[8,512,128]{2,1,0:T(8,128)}), f32[8,512,128]{2,1,0:T(8,128)}, u32[]{:S(2)}, u32[]{:S(2)}) async-start(f32[8,512,128]{2,1,0:T(8,128)} %broadcast_in_dim.67), calls=%async_computation.3 | async-start | bytes 4194304 | tf_op jit(solution)/shard_map/all_to_all | solution.py:36
  348.6 28.8 %reduce-scatter.9.cloned.1.call-start = ((), (), s32[]{:S(2)}) async-start(), calls=%async_computation.14 | async-start | bytes 1024000
  361.9 15.5 %copy-start.1 = (bf16[640,2560]{1,0:T(8,128)(2,1)S(1)}, bf16[640,2560]{1,0:T(8,128)(2,1)}, u32[]{:S(2)}) copy-start(bf16[640,2560]{1,0:T(8,128)(2,1)} %param.18) | copy-start | bytes 9830404
  (87 other events, 410.3 us)
Sparse Core Ops, SparseCore 0:
  24.1 29.9 all-gather.13
  56.5 40.7 all-gather.9
  193.4 22.5 all-gather.15
  218.3 40.7 all-gather.11
  261.6 80.9 reduce-scatter.6
  352.2 18.0 reduce-scatter.8
where the time goes:
time: 391 us; the launch traced here: 384 us
  waiting for transfers between devices  102 us (26%)
  local copies, waits for them, and re-layouts  65.6 us (17%)
  blocking collectives  58.7 us (15%)
  matrix products  55 us (14%)
  other arithmetic  49.4 us (13%)
  starting transfers between devices  37.6 us (10%)
  between operations  16.4 us (4%)
    all_to_all x5, waiting for transfers between devices, sent_to_all(): return lax.all_to_all(copies, axis, split_axis=0, concat_axis=0, tiled=True)  60.2 us
    all_gather x4, waiting for transfers between devices, prefix_by_axis(): pieces = jax.tree.map(lambda part: lax.all_gather(part, axis), total)  40.8 us
    all_to_all x5, starting transfers between devices, sent_to_all(): return lax.all_to_all(copies, axis, split_axis=0, concat_axis=0, tiled=True)  37.5 us
    all_gather x2, blocking collectives, prefix_by_axis(): pieces = jax.tree.map(lambda part: lax.all_gather(part, axis), total)  28.5 us
    all_to_all x2, blocking collectives, sent_to_all(): return lax.all_to_all(copies, axis, split_axis=0, concat_axis=0, tiled=True)  21 us
    unnamed x231, local copies, waits for them, and re-layouts  14.3 us
    slice x6, local copies, waits for them, and re-layouts, on_device(): x_part = x_heads[first_row:first_row + block_len]  10.2 us
    shift_right_arithmetic x5, local copies, waits for them, and re-layouts, dequantize(): jnp.right_shift(packed_words[:, None, :], shifts[None, :, None])  9.68 us
  transfers between devices with their start and end apart: 11, of which 6 were waited for; matrix products, arithmetic and copies ran while one was open for 28% of the time, Pallas kernels for 0%

commit v1 on v0

v1 whole, which is shorter than its diff:
```python
import functools

import jax
import jax.numpy as jnp
from jax import lax
from jax.experimental import pallas as pl
from jax.experimental.pallas import tpu as pltpu
from jax.sharding import PartitionSpec as P

MESH = pl.DeviceIdType.MESH
F32, BF16 = jnp.float32, jnp.bfloat16
EXACT = lax.Precision.HIGHEST
NX = 4
L = 128
HEAD = 64
SLOT = 16


def dot(a, b, ca=1, cb=0, precision=None):
    return lax.dot_general(
        a, b, (((ca,), (cb,)), ((), ())), preferred_element_type=F32, precision=precision
    )


def iota(shape, dim):
    return lax.broadcasted_iota(jnp.int32, shape, dim)


def rcopy(src, dst, send, recv, dev):
    return pltpu.make_async_remote_copy(
        src_ref=src, dst_ref=dst, send_sem=send, recv_sem=recv, device_id=dev, device_id_type=MESH
    )


def core(nx, nz, ntp, packed, expo, gate_hbm, b_ref, c_ref, ld_ref, skip_ref, gain_ref, w_hbm, cot_hbm,
         gin, ggate, gwrite, gread, gdecay, gskip, ggain, gow, *scratch):
    (gate_v, w_v, cot_all, cot_full, xb, yb, gvb, mixb, dyb, rsb, endb, startb,
     csr, csc, totb, dec, cross, gb, stb, hcb, sumd, segr, segc, dxi,
     sloc, lb, tb, ub, qs, qb, vs, s_in,
     rloc, lb2, tb2, ub2, qs2, qb2, vs2, h_in,
     dxs, dzs, sums, gx, gz, pw, xr, zs, zr, accw, accr, red, redo,
     cp_sem, s_ag, r_ag, s_dx, r_dx, s_dz, r_dz,
     s_p1, r_p1, s_p2, r_p2, s_p3, r_p3, s_p4, r_p4,
     s_h1, r_h1, s_h2, r_h2, s_h3, r_h3, s_h4, r_h4,
     s_tp, r_tp, s_gx, r_gx, s_gz, r_gz, s_rx, r_rx, s_rz, r_rz,
     s_w1, r_w1, s_w2, r_w2, s_c1, r_c1, s_c2, r_c2) = scratch
    tokens, width = xb.shape
    chunks = tokens // L
    pairs = width // 128
    heads = width // HEAD
    total_width = width * ntp
    ny = ntp // 2
    qrows, erows = 128 // nx, 128 // (nx * nz)
    s = lax.axis_index("seq")
    t = lax.axis_index("tp")
    z, x = lax.div(s, nx), lax.rem(s, nx)
    y, half = lax.div(t, 2), lax.rem(t, 2)

    def dev_x(p):
        return {"seq": z * nx + p, "tp": t}

    def dev_z(p):
        return {"seq": p * nx + x, "tp": t}

    def dev_t(p):
        return {"seq": s, "tp": p}

    X, Z, TP = (nx, x, dev_x), (nz, z, dev_z), (ntp, t, dev_t)
    pending = []

    def send(group, src_of, dst, ssem, rsem):
        n, me, dev = group
        for d in range(1, n):
            p = lax.rem(me + d, n)
            copy = rcopy(src_of(p), dst, ssem.at[d], rsem.at[me], dev(p))
            copy.start()
            pending.append(copy)

    def arrive(group, dst_of, ssem, rsem):
        n, me, dev = group
        for d in range(1, n):
            p = lax.rem(me + d, n)
            rcopy(dst_of(p), dst_of(p), ssem.at[d], rsem.at[p], dev(p)).wait_recv()

    load_cot = pltpu.make_async_copy(cot_hbm, cot_all.at[t], cp_sem.at[0])
    load_gate = pltpu.make_async_copy(gate_hbm, gate_v, cp_sem.at[1])
    load_w = pltpu.make_async_copy(w_hbm, w_v, cp_sem.at[2])
    load_cot.start()
    load_gate.start()
    load_w.start()

    barrier = pltpu.get_barrier_semaphore()
    for n, me, dev in (X, Z, TP):
        for d in range(1, n):
            pl.semaphore_signal(
                barrier, inc=1, device_id=dev(lax.rem(me + d, n)), device_id_type=MESH
            )

    spread = (iota((SLOT, width), 1) // HEAD == iota((SLOT, width), 0)).astype(F32)
    gather = (iota((width, SLOT), 0) // HEAD == iota((width, SLOT), 1)).astype(F32)
    upper = (iota((L, L), 0) <= iota((L, L), 1)).astype(F32)
    lower = (iota((L, L), 0) <= iota((L, L), 1)).astype(F32)
    causal = iota((L, L), 0) >= iota((L, L), 1)
    left = iota((L, 128), 1) < HEAD

    csr[...] = jnp.zeros_like(csr)
    segr[...] = jnp.zeros_like(segr)
    log_total = jnp.zeros((1, SLOT), F32)
    for k in range(chunks):
        csr[k, 0:heads, :] = ld_ref[:, k * L : (k + 1) * L]
        rows = dot(csr[k], upper, precision=EXACT)
        csr[k] = rows
        cols = rows.T
        csc[k] = cols
        last = cols[L - 1 : L, :]
        log_total = log_total + last
        totb[k] = dot(jnp.broadcast_to(jnp.exp(last), (8, SLOT)), spread, precision=EXACT)[0:1]
        endb[k * L : (k + 1) * L, :] = dot(jnp.exp(last - cols), spread, precision=EXACT)
        startb[k * L : (k + 1) * L, :] = dot(jnp.exp(cols), spread, precision=EXACT)
    decay_all = dot(jnp.broadcast_to(jnp.exp(log_total), (8, SLOT)), spread, precision=EXACT)[0:1]
    dxs[x] = decay_all

    pl.semaphore_wait(barrier, (nx - 1) + (nz - 1) + (ntp - 1))
    send(X, lambda p: dxs.at[x], dxs.at[x], s_dx, r_dx)

    load_cot.wait()
    sibling = dev_t(2 * y + 1 - half)
    copy = rcopy(cot_all.at[t], cot_all.at[t], s_ag.at[ny], r_ag.at[t], sibling)
    copy.start()
    pending.append(copy)
    for d in range(1, ny):
        p = 2 * lax.rem(y + d, ny) + half
        copy = rcopy(cot_all.at[t], cot_all.at[t], s_ag.at[d], r_ag.at[t], dev_t(p))
        copy.start()
        pending.append(copy)

    def share_cot(d):
        p = 2 * lax.rem(y + d, ny) + half
        rcopy(cot_all.at[p], cot_all.at[p], s_ag.at[d], r_ag.at[p], dev_t(p)).wait_recv()
        copy = rcopy(cot_all.at[p], cot_all.at[p], s_ag.at[ny + d], r_ag.at[p], sibling)
        copy.start()
        pending.append(copy)

    def sibling_cot():
        for d in range(ny):
            p = 2 * lax.rem(y + d, ny) + 1 - half
            rcopy(cot_all.at[p], cot_all.at[p], s_ag.at[d], r_ag.at[p], sibling).wait_recv()

    powers = lax.shift_left(jnp.ones_like(expo[...]), expo[...] + 5).astype(F32) * (1.0 / 32.0)
    nibble = 4 * iota((8, width), 0)
    for k in range(chunks):
        factor_rows = jnp.concatenate(
            [powers[:, k * L : (k + 1) * L], jnp.zeros((8 - pairs, L), F32)], axis=0
        )
        factor = factor_rows.T
        wide = jnp.concatenate(
            [jnp.broadcast_to(factor[:, p : p + 1], (L, 128)) for p in range(pairs)], axis=1
        )
        words = packed[k * (L // 8) : (k + 1) * (L // 8), :]
        fields = jnp.concatenate(
            [
                lax.bitwise_and(
                    lax.shift_right_arithmetic(
                        jnp.broadcast_to(words[r : r + 1, :], (8, width)), nibble
                    ),
                    15,
                )
                - 8
                for r in range(L // 8)
            ],
            axis=0,
        )
        xb[k * L : (k + 1) * L, :] = (fields.astype(F32) * wide).astype(BF16)

    run = jnp.zeros((128, width), F32)
    for k in range(chunks):
        rows = slice(k * L, (k + 1) * L)
        weighted = (xb[rows, :].astype(F32) * endb[rows, :]).astype(BF16)
        gb[k] = dot(b_ref[rows, :], weighted, 0, 0)
        run = totb[k] * run + gb[k]
    sloc[...] = run

    def take_rows(ref, at, count):
        return ref[pl.ds(pl.multiple_of(at * count, count), count), :]

    def exchange_1(own, lbuf, ssem, rsem):
        send(
            X,
            lambda p: own.at[pl.ds(pl.multiple_of(p * qrows, qrows), qrows)],
            lbuf.at[x],
            ssem,
            rsem,
        )
        lbuf[x] = take_rows(own, x, qrows)

    def exchange_2(lbuf, tbuf, ubuf, s1, r1, ssem, rsem, backward):
        arrive(X, lambda p: lbuf.at[p], s1, r1)
        order = range(nx - 1, -1, -1) if backward else range(nx)
        row = None
        for k in order:
            row = lbuf[k] if row is None else dxs[k] * row + lbuf[k]
        for k in range(nz):
            tbuf[k] = row[k * erows : (k + 1) * erows, :]
        send(Z, lambda p: tbuf.at[p], ubuf.at[z], ssem, rsem)
        ubuf[z] = tbuf[z]

    def exchange_3(ubuf, qsend, qbuf, s2, r2, ssem, rsem, backward):
        arrive(Z, lambda p: ubuf.at[p], s2, r2)
        order = range(nz - 1, -1, -1) if backward else range(nz)
        row = jnp.zeros((erows, width), F32)
        for k in order:
            qsend[k] = row
            row = dzs[k] * row + ubuf[k]
        send(Z, lambda p: qsend.at[p], qbuf.at[z], ssem, rsem)
        qbuf[z] = qsend[z]

    def exchange_4(qbuf, lbuf, vsend, result, s3, r3, ssem, rsem, backward):
        arrive(Z, lambda p: qbuf.at[p], s3, r3)
        first = nx - 1 if backward else 0
        for k in range(nz):
            vsend[first, k * erows : (k + 1) * erows, :] = qbuf[k]
        order = range(nx - 1, -1, -1) if backward else range(nx)
        row = vsend[first]
        for k in order:
            if k != first:
                vsend[k] = row
            row = dxs[k] * row + lbuf[k]
        mine = result.at[pl.ds(pl.multiple_of(x * qrows, qrows), qrows)]
        send(X, lambda p: vsend.at[p], mine, ssem, rsem)
        result[pl.ds(pl.multiple_of(x * qrows, qrows), qrows), :] = vsend[x]

    def exchange_5(result, s4, r4):
        arrive(X, lambda p: result.at[pl.ds(pl.multiple_of(p * qrows, qrows), qrows)], s4, r4)

    exchange_1(sloc, lb, s_p1, r_p1)

    arrive(X, lambda p: dxs.at[p], s_dx, r_dx)
    row = dxs[0]
    for k in range(1, nx):
        row = row * dxs[k]
    dzs[z] = row
    send(Z, lambda p: dzs.at[z], dzs.at[z], s_dz, r_dz)

    skip_row = dot(
        jnp.concatenate(
            [jnp.broadcast_to(skip_ref[...], (8, heads)), jnp.zeros((8, SLOT - heads), F32)], axis=1
        ),
        spread,
        precision=EXACT,
    )[0:1]

    def at_chunk(k):
        return pl.ds(pl.multiple_of(k * L, L), L)

    def split_pair(v):
        zero = jnp.zeros_like(v)
        return jnp.concatenate([jnp.where(left, v, zero), jnp.where(left, zero, v)], axis=0)

    def inside(k, _):
        rows = at_chunk(k)
        both = dot(c_ref[rows, :], b_ref[rows, :], 1, 1)
        cross[k] = both
        for p in range(pairs):
            mixing = []
            for h in (2 * p, 2 * p + 1):
                spread_log = csc[k][:, h : h + 1] - csr[k][h : h + 1, :]
                decay = jnp.where(causal, jnp.exp(jnp.minimum(spread_log, 0.0)), 0.0)
                dec[k, h] = decay
                mixing.append((decay * both).astype(BF16))
            lanes = slice(128 * p, 128 * (p + 1))
            x_pair = xb[rows, lanes]
            yb[rows, lanes] = (
                dot(jnp.concatenate(mixing, axis=1), split_pair(x_pair))
                + skip_row[:, lanes] * x_pair.astype(F32)
            )
        return 0

    lax.fori_loop(0, chunks // 2, inside, 0)
    exchange_2(lb, tb, ub, s_p1, r_p1, s_p2, r_p2, False)
    lax.fori_loop(chunks // 2, chunks, inside, 0)
    arrive(Z, lambda p: dzs.at[p], s_dz, r_dz)
    exchange_3(ub, qs, qb, s_p2, r_p2, s_p3, r_p3, False)
    exchange_4(qb, lb, vs, s_in, s_p3, r_p3, s_p4, r_p4, False)
    for d in range(1, ny):
        share_cot(d)
    sibling_cot()
    shard = cot_all.shape[2]
    for p in range(ntp):
        cot_full[:, p * shard : (p + 1) * shard] = cot_all[p]
    load_w.wait()

    def project(k, _):
        rows = at_chunk(k)
        gvb[rows, :] = dot(cot_full[rows, :], w_v[...], 1, 1)
        return 0

    lax.fori_loop(0, chunks, project, 0)
    load_gate.wait()
    exchange_5(s_in, s_p4, r_p4)

    gain_row = gain_ref[...]
    stb[0] = s_in[...]
    for k in range(1, chunks):
        stb[k] = totb[k - 1] * stb[k - 1] + gb[k - 1]

    def outputs_of(k, _):
        rows = at_chunk(k)
        start = dot(c_ref[rows, :], stb[k].astype(BF16))
        rsb[rows, :] = start
        y_now = yb[rows, :] + startb[rows, :] * start
        yb[rows, :] = y_now
        gate = gate_v[rows, :].astype(F32)
        mixed = y_now * gate * jax.nn.sigmoid(gate)
        mixb[rows, :] = mixed
        square = jnp.sum(mixed * mixed, axis=1, keepdims=True)
        inner = jnp.sum(gvb[rows, :] * gain_row * mixed, axis=1, keepdims=True)
        lane = iota((L, 128), 1)
        packed_sums = jnp.where(lane == 0, square, jnp.where(lane == 1, inner, 0.0))
        sums[t, k] = packed_sums.T[0:8, :]
        return 0

    lax.fori_loop(0, chunks, outputs_of, 0)
    send(TP, lambda p: sums.at[t], sums.at[t], s_tp, r_tp)
    arrive(TP, lambda p: sums.at[p], s_tp, r_tp)

    def gradients(k, carry):
        gain_sum, skip_sum = carry
        rows = at_chunk(k)
        both = sums[0, k]
        for p in range(1, ntp):
            both = both + sums[p, k]
        both = jnp.concatenate([both, jnp.zeros((120, L), F32)], axis=0).T
        scale = lax.rsqrt(both[:, 0:1] / total_width + 1e-05)
        inner = both[:, 1:2]
        mixed = mixb[rows, :]
        grad_v = gvb[rows, :]
        gate = gate_v[rows, :].astype(F32)
        sigma = jax.nn.sigmoid(gate)
        grad_mixed = scale * (grad_v * gain_row) - mixed * (
            (scale * scale * scale) * inner / total_width
        )
        ggate[rows, :] = (
            grad_mixed * yb[rows, :] * sigma * (1.0 + gate * (1.0 - sigma))
        ).astype(BF16)
        grad_y = grad_mixed * gate * sigma
        dyb[rows, :] = grad_y
        gain_sum = gain_sum + jnp.sum(grad_v * mixed * scale, axis=0, keepdims=True)
        skip_sum = skip_sum + jnp.sum(
            grad_y * xb[rows, :].astype(F32), axis=0, keepdims=True
        )
        hcb[k] = dot(c_ref[rows, :], (grad_y * startb[rows, :]).astype(BF16), 0, 0)
        mixb[rows, :] = mixed * scale * gain_row
        return gain_sum, skip_sum

    zero_row = jnp.zeros((1, width), F32)
    gain_sum, skip_sum = lax.fori_loop(0, chunks, gradients, (zero_row, zero_row))
    run = hcb[chunks - 1]
    for k in range(chunks - 2, -1, -1):
        run = totb[k] * run + hcb[k]
    rloc[...] = run
    exchange_1(rloc, lb2, s_h1, r_h1)
    gx[x, 0:1, :] = gain_sum
    gx[x, 1:2, :] = skip_sum
    send(X, lambda p: gx.at[x], gx.at[x], s_gx, r_gx)

    columns = shard // nx

    def weight_block(k):
        normed = mixb[...].astype(BF16)
        pw[k] = dot(cot_all[k], normed, 0, 0).astype(BF16)
        for d in range(1, nx):
            p = lax.rem(x + d, nx)
            copy = rcopy(
                pw.at[k, pl.ds(pl.multiple_of(p * columns, columns), columns)],
                xr.at[x, k],
                s_rx.at[d, k],
                r_rx.at[x, k],
                dev_x(p),
            )
            copy.start()
            pending.append(copy)

    def weight_rows(k):
        out = pw[k, pl.ds(pl.multiple_of(x * columns, columns), columns), :].astype(F32)
        for d in range(1, nx):
            p = lax.rem(x + d, nx)
            rcopy(xr.at[p, k], xr.at[p, k], s_rx.at[d, k], r_rx.at[p, k], dev_x(p)).wait_recv()
            out = out + xr[p, k].astype(F32)
        zs[k] = out.astype(BF16)

        @pl.when(z != k)
        def _():
            rcopy(zs.at[k], zr.at[z], s_rz.at[k], r_rz.at[z], dev_z(k)).start()

    first_blocks = nz // 2
    for k in range(first_blocks):
        weight_block(k)
    exchange_2(lb2, tb2, ub2, s_h1, r_h1, s_h2, r_h2, True)
    arrive(X, lambda p: gx.at[p], s_gx, r_gx)
    row = gx[0]
    for k in range(1, nx):
        row = row + gx[k]
    gz[z] = row
    send(Z, lambda p: gz.at[z], gz.at[z], s_gz, r_gz)

    def inside_back(k, _):
        rows = at_chunk(k)
        both = cross[k]
        summed = jnp.zeros((L, L), F32)
        lane = iota((L, SLOT), 1)
        row_sums = jnp.zeros((L, SLOT), F32)
        for p in range(pairs):
            lanes = slice(128 * p, 128 * (p + 1))
            x_pair = xb[rows, lanes]
            grads = split_pair(dyb[rows, lanes].astype(BF16))
            dots = dot(grads, x_pair, 1, 1)
            mixing = []
            for i in range(2):
                h = 2 * p + i
                decay = dec[k, h]
                weighted = dots[i * L : (i + 1) * L, :] * decay
                summed = summed + weighted
                terms = weighted * both
                row_sums = row_sums + jnp.where(
                    lane == h, jnp.sum(terms, axis=1, keepdims=True), 0.0
                )
                segr[k, h : h + 1, :] = jnp.sum(terms, axis=0, keepdims=True)
                mixing.append((decay * both).astype(BF16))
            dxi[rows, lanes] = dot(jnp.concatenate(mixing, axis=0), grads, 0, 0)
        sumd[k] = summed
        segc[k] = row_sums - segr[k].T
        scaled = dyb[rows, :] * startb[rows, :]
        accr[rows, :] = dot(summed.astype(BF16), b_ref[rows, :]) + dot(
            scaled.astype(BF16), stb[k].astype(BF16), 1, 1
        )
        return 0

    lax.fori_loop(0, chunks // 2, inside_back, 0)
    exchange_3(ub2, qs2, qb2, s_h2, r_h2, s_h3, r_h3, True)
    lax.fori_loop(chunks // 2, chunks, inside_back, 0)
    exchange_4(qb2, lb2, vs2, h_in, s_h3, r_h3, s_h4, r_h4, True)

    share = tokens // ntp

    def reduce_1(acc, which, ssem, rsem):
        send(
            TP,
            lambda p: acc.at[pl.ds(pl.multiple_of(p * share, share), share)],
            red.at[which, t],
            ssem,
            rsem,
        )
        red[which, t] = take_rows(acc, t, share)

    def reduce_2(which, s1, r1, ssem, rsem):
        arrive(TP, lambda p: red.at[which, p], s1, r1)
        out = red[which, 0]
        for p in range(1, ntp):
            out = out + red[which, p]
        redo[which, t] = out
        send(TP, lambda p: redo.at[which, t], redo.at[which, t], ssem, rsem)

    def reduce_3(out_ref, which, ssem, rsem):
        arrive(TP, lambda p: redo.at[which, p], ssem, rsem)
        for p in range(ntp):
            out_ref[p * share : (p + 1) * share, :] = redo[which, p]

    reduce_1(accr, 0, s_c1, r_c1)
    for k in range(first_blocks, nz):
        weight_block(k)
    for k in range(first_blocks):
        weight_rows(k)
    exchange_5(h_in, s_h4, r_h4)

    def finish(i, run):
        k = chunks - 1 - i
        rows = at_chunk(k)
        h_low = run.astype(BF16)
        end = endb[rows, :]
        grad_y = dyb[rows, :]
        x_now = xb[rows, :].astype(F32)
        write = end * dot(b_ref[rows, :], h_low)
        gin[rows, :] = (skip_row * grad_y + dxi[rows, :] + write).astype(BF16)
        accw[rows, :] = dot(sumd[k].astype(BF16), c_ref[rows, :], 0, 0) + dot(
            (x_now * end).astype(BF16), h_low, 1, 1
        )
        leaving = dot(x_now * write, gather, precision=EXACT)
        arriving = dot(grad_y * startb[rows, :] * rsb[rows, :], gather, precision=EXACT)
        seg = segc[k] + arriving - leaving
        across = totb[k] * jnp.sum(run * stb[k], axis=0, keepdims=True)
        final = jnp.sum(leaving, axis=0, keepdims=True) + dot(
            jnp.broadcast_to(across, (8, width)), gather, precision=EXACT
        )[0:1]
        whole = dot(lower, seg, precision=EXACT) + final
        sumd[k, 0:SLOT, :] = whole.T
        return totb[k] * run + hcb[k]

    lax.fori_loop(0, chunks, finish, h_in[...])
    reduce_1(accw, 1, s_w1, r_w1)
    for k in range(chunks):
        gdecay[:, k * L : (k + 1) * L] = sumd[k, 0:heads, :]
    reduce_2(0, s_c1, r_c1, s_c2, r_c2)
    arrive(Z, lambda p: gz.at[p], s_gz, r_gz)
    row = gz[0]
    for k in range(1, nz):
        row = row + gz[k]
    ggain[...] = row[0:1]
    gskip[...] = dot(row, gather, precision=EXACT)[1:2, 0:heads]
    reduce_2(1, s_w1, r_w1, s_w2, r_w2)
    reduce_3(gread, 0, s_c2, r_c2)
    for k in range(first_blocks, nz):
        weight_rows(k)
    reduce_3(gwrite, 1, s_w2, r_w2)
    zr[z] = zs[z]
    arrive(Z, lambda p: zr.at[p], s_rz, r_rz)
    out = zr[0].astype(F32)
    for k in range(1, nz):
        out = out + zr[k].astype(F32)
    gow[...] = out.T
    for copy in pending:
        copy.wait_send()
    for k in range(nz):

        @pl.when(z != k)
        def _():
            rcopy(zs.at[k], zr.at[z], s_rz.at[k], r_rz.at[z], dev_z(k)).wait_send()


def on_device(nx, nz, ntp, packed, expo, gate, write, read, decay, skip, gain, weight, cot):
    tokens, width = gate.shape
    heads = decay.shape[0]
    model = weight.shape[1]
    shard = cot.shape[1]
    chunks = tokens // L
    n = write.shape[1]
    columns = model // (nx * nz)
    qrows, erows = n // nx, n // (nx * nz)
    ny = ntp // 2
    share = tokens // ntp

    def wide(kind=F32):
        return pltpu.VMEM((tokens, width), kind)

    def exchange():
        return [
            pltpu.VMEM((n, width), F32),
            pltpu.VMEM((nx, qrows, width), F32),
            pltpu.VMEM((nz, erows, width), F32),
            pltpu.VMEM((nz, erows, width), F32),
            pltpu.VMEM((nz, erows, width), F32),
            pltpu.VMEM((nz, erows, width), F32),
            pltpu.VMEM((nx, qrows, width), F32),
            pltpu.VMEM((n, width), F32),
        ]

    def sems(*shape):
        return [pltpu.SemaphoreType.DMA(shape), pltpu.SemaphoreType.DMA(shape)]

    scratch = [
        pltpu.VMEM((tokens, width), BF16),
        pltpu.VMEM((width, model), BF16),
        pltpu.VMEM((ntp, tokens, shard), BF16),
        pltpu.VMEM((tokens, model), BF16),
        wide(BF16),
        *[wide() for _ in range(7)],
        pltpu.VMEM((chunks, SLOT, L), F32),
        pltpu.VMEM((chunks, L, SLOT), F32),
        pltpu.VMEM((chunks, 1, width), F32),
        pltpu.VMEM((chunks, heads, L, L), F32),
        pltpu.VMEM((chunks, L, L), F32),
        pltpu.VMEM((chunks, n, width), F32),
        pltpu.VMEM((chunks, n, width), F32),
        pltpu.VMEM((chunks, n, width), F32),
        pltpu.VMEM((chunks, L, L), F32),
        pltpu.VMEM((chunks, SLOT, L), F32),
        pltpu.VMEM((chunks, L, SLOT), F32),
        wide(),
        *exchange(),
        *exchange(),
        pltpu.VMEM((nx, 1, width), F32),
        pltpu.VMEM((nz, 1, width), F32),
        pltpu.VMEM((ntp, chunks, 8, L), F32),
        pltpu.VMEM((nx, 2, width), F32),
        pltpu.VMEM((nz, 2, width), F32),
        pltpu.VMEM((nz, shard, width), BF16),
        pltpu.VMEM((nx, nz, columns, width), BF16),
        pltpu.VMEM((nz, columns, width), BF16),
        pltpu.VMEM((nz, columns, width), BF16),
        pltpu.VMEM((tokens, n), F32),
        pltpu.VMEM((tokens, n), F32),
        pltpu.VMEM((2, ntp, share, n), F32),
        pltpu.VMEM((2, ntp, share, n), F32),
        pltpu.SemaphoreType.DMA((3,)),
        pltpu.SemaphoreType.DMA((2 * ny,)),
        pltpu.SemaphoreType.DMA((ntp,)),
        *sems(nx),
        *sems(nz),
        *(sems(nx) + sems(nz) + sems(nz) + sems(nx)),
        *(sems(nx) + sems(nz) + sems(nz) + sems(nx)),
        *sems(ntp),
        *sems(nx),
        *sems(nz),
        *sems(nx, nz),
        *sems(nz),
        *(sems(ntp) * 4),
    ]
    vmem = pl.BlockSpec(memory_space=pltpu.VMEM)
    hbm = pl.BlockSpec(memory_space=pl.ANY)
    outs = pl.pallas_call(
        functools.partial(core, nx, nz, ntp),
        out_shape=(
            jax.ShapeDtypeStruct((tokens, width), BF16),
            jax.ShapeDtypeStruct((tokens, width), BF16),
            jax.ShapeDtypeStruct((tokens, n), F32),
            jax.ShapeDtypeStruct((tokens, n), F32),
            jax.ShapeDtypeStruct((heads, tokens), F32),
            jax.ShapeDtypeStruct((1, heads), F32),
            jax.ShapeDtypeStruct((1, width), F32),
            jax.ShapeDtypeStruct((width, columns), F32),
        ),
        in_specs=[vmem, vmem, hbm, vmem, vmem, vmem, vmem, vmem, hbm, hbm],
        out_specs=(vmem,) * 8,
        scratch_shapes=scratch,
        compiler_params=pltpu.CompilerParams(
            collective_id=0, has_side_effects=True, vmem_limit_bytes=60 * 1024 * 1024
        ),
        name="layer_backward",
    )(packed, expo, gate, write, read, decay, skip[None, :], gain[None, :], weight, cot)
    return (*outs[:5], outs[5][0], outs[6][0], outs[7])


def solution(mesh):
    ntp = mesh.shape["tp"]
    nz = mesh.shape["seq"] // NX
    return jax.shard_map(
        functools.partial(on_device, NX, nz, ntp),
        mesh=mesh,
        in_specs=(
            P("seq", "tp"),
            P("tp", "seq"),
            P("seq", "tp"),
            P("seq", None),
            P("seq", None),
            P("tp", "seq"),
            P("tp"),
            P("tp"),
            P("tp", None),
            P("seq", "tp"),
        ),
        out_specs=(
            P("seq", "tp"),
            P("seq", "tp"),
            P("seq", None),
            P("seq", None),
            P("tp", "seq"),
            P("tp"),
            P("tp"),
            P("tp", "seq"),
        ),
        check_vma=False,
    )
```

time: 391 us -> 122 us (0.31); the launches traced: 384 us -> 122 us
  Pallas kernels: 0 us -> 109 us
  waiting for transfers between devices: 102 us -> 0 us
  blocking collectives: 58.7 us -> 0 us
  matrix products: 55 us -> 0 us
  local copies, waits for them, and re-layouts: 65.6 us -> 11.5 us
  other arithmetic: 49.4 us -> 1.32 us
  starting transfers between devices: 37.6 us -> 0 us
  between operations: 16.4 us -> 0.68 us
    pallas_call x0 -> x1, Pallas kernels: none -> 109 us  [on_device(): pl.pallas_call(functools.partial(core, nx, nz, ntp), out_shape=(jax.Shape...]
    all_to_all x5 -> x0, waiting for transfers between devices: 60.2 us -> none  [sent_to_all(): return lax.all_to_all(copies, axis, split_axis=0, concat_axis=0, tiled=True)]
    dot_general x26 -> x0, matrix products: 55 us -> none  [the longest x2 7.27 us: on_device(): pair_dot = jnp.einsum('ihp,jhp->hij', grad_part, x_part, precision=PRECISE)]
    all_gather x4 -> x0, waiting for transfers between devices: 40.8 us -> none  [prefix_by_axis(): pieces = jax.tree.map(lambda part: lax.all_gather(part, axis), total)]
    all_to_all x5 -> x0, starting transfers between devices: 37.5 us -> none  [sent_to_all(): return lax.all_to_all(copies, axis, split_axis=0, concat_axis=0, tiled=True)]
    all_gather x2 -> x0, blocking collectives: 28.5 us -> none  [prefix_by_axis(): pieces = jax.tree.map(lambda part: lax.all_gather(part, axis), total)]
    reduce_sum x13 -> x0, other arithmetic: 21.8 us -> none  [the longest x6 9.12 us: taken_together(): return sent_to_all(shard, axis).sum(axis=0)]
    all_to_all x2 -> x0, blocking collectives: 21 us -> none  [sent_to_all(): return lax.all_to_all(copies, axis, split_axis=0, concat_axis=0, tiled=True)]
  transfers between devices with their start and end apart: 11 -> 0, of which waited for: 6 -> 0; matrix products, arithmetic and copies ran while one was open for 28% -> 0% of each run, Pallas kernels for 0% -> 0%
where the time goes in v1:
time: 122 us
  Pallas kernels  109 us (89%)
  local copies, waits for them, and re-layouts  11.5 us (9%)
  other arithmetic  1.32 us (1%)
    pallas_call x1, Pallas kernels, on_device(): pl.pallas_call(functools.partial(core, nx, nz, ntp), out_shape=(jax.Shape...  109 us
    unnamed x16, local copies, waits for them, and re-layouts  10.2 us

profile of v1, /device:TPU:1, one launch (start us, length us, event | category | flops | bytes accessed | tf_op | source)
XLA Modules:
  0.0 122.2 jit_solution(11748709091738518503)
XLA Ops:
  0.6 1.3 %broadcast_in_dim.7.gain_ref = f32[1,640]{1,0:T(1,128)} reshape(f32[640]{0:T(1024)} %param.17) | data formatting | bytes 5120 | tf_op jit(solution)/shard_map/broadcast_in_dim | solution.py:628
  1.9 1.9 %copy.18.cot_hbm = bf16[512,320]{1,0:T(8,128)(2,1)} copy(bf16[512,320]{0,1:T(8,128)(2,1)} %param.19) | data formatting | bytes 655360 | tf_op args[9]
  3.8 108.7 %layer_backward.1 = (bf16[512,640]{1,0:T(8,128)(2,1)}, bf16[512,640]{1,0:T(8,128)(2,1)}, f32[512,128]{1,0:T(8,128)}, f32[512,128]{1,0:T(8,128)}, f32[10,512]{1,0...) custom-call(s32[64,640]{1,0:T(8,128)} %packed.1, s32[5,512]{1,0:T(8,128)} %expo.1, ...), custom_call_target="tpu_custom_call" | custom-call | tf_op jit(solution)/shard_map/layer_backward/pallas_call | solution.py:609
  112.5 0.0 copy-start.1
  112.5 0.0 copy-start
  112.5 0.0 copy-start.2
  112.5 0.0 copy-start.3
  112.5 1.3 %reduce = f32[640]{0:T(1024)} reduce(f32[1,640]{1,0:T(1,128)} %get-tuple-element.22, f32[]{:T(128)} %constant.3), dimensions={0}, to_apply=%get-tuple-element.22.reduce_sub_computation | reduce | bytes 5124 | tf_op jit(solution)/shard_map/layer_backward/pallas_call | solution.py:609
  113.9 1.8 %copy.19 = f32[640,80]{0,1:T(8,128)} copy(f32[640,80]{1,0:T(8,128)} %get-tuple-element.31) | data formatting | bytes 409600
  115.7 2.0 %copy.26 = bf16[512,640]{1,0:T(8,128)(2,1)} copy(bf16[512,640]{1,0:T(8,128)(2,1)} %get-tuple-element.40) | data formatting | bytes 1310720
  117.6 2.0 %copy.27 = bf16[512,640]{1,0:T(8,128)(2,1)} copy(bf16[512,640]{1,0:T(8,128)(2,1)} %get-tuple-element.41) | data formatting | bytes 1310720
  119.6 0.0 copy-done.1
  119.6 0.7 copy.28
  120.3 0.0 copy-done
  120.3 0.7 copy.29
  121.0 0.0 copy-done.2
  121.0 0.6 copy.30
  121.7 0.0 copy-done.3
  121.7 0.5 copy.31
Async XLA Ops:
  112.5 7.1 %copy-start.1 = (f32[512,128]{1,0:T(8,128)S(1)}, f32[512,128]{1,0:T(8,128)}, u32[]{:S(2)}) copy-start(f32[512,128]{1,0:T(8,128)} %get-tuple-element.42) | copy-start | bytes 786436
  112.5 7.8 %copy-start = (f32[512,128]{1,0:T(8,128)S(1)}, f32[512,128]{1,0:T(8,128)}, u32[]{:S(2)}) copy-start(f32[512,128]{1,0:T(8,128)} %get-tuple-element.43) | copy-start | bytes 786436
  112.5 8.5 %copy-start.2 = (f32[10,512]{1,0:T(8,128)S(1)}, f32[10,512]{1,0:T(8,128)}, u32[]{:S(2)}) copy-start(f32[10,512]{1,0:T(8,128)} %get-tuple-element.44) | copy-start | bytes 61444
  112.5 9.1 %copy-start.3 = (f32[1,10]{1,0:T(1,128)S(1)}, f32[1,10]{1,0:T(1,128)}, u32[]{:S(2)}) copy-start(f32[1,10]{1,0:T(1,128)} %get-tuple-element.21) | copy-start | bytes 124

commit v2 on v1

--- a/solution.py
+++ b/solution.py
@@ -22,6 +22,15 @@
     )
 
 
+def pieces(v, count):
+    out = []
+    for _ in range(count):
+        part = v.astype(BF16)
+        out.append(part)
+        v = v - part.astype(F32)
+    return out
+
+
 def iota(shape, dim):
     return lax.broadcasted_iota(jnp.int32, shape, dim)
 
@@ -34,11 +43,11 @@
 
 def core(nx, nz, ntp, packed, expo, gate_hbm, b_ref, c_ref, ld_ref, skip_ref, gain_ref, w_hbm, cot_hbm,
          gin, ggate, gwrite, gread, gdecay, gskip, ggain, gow, *scratch):
-    (gate_v, w_v, cot_all, cot_full, xb, yb, gvb, mixb, dyb, rsb, endb, startb,
-     csr, csc, totb, dec, cross, gb, stb, hcb, sumd, segr, segc, dxi,
+    (gate_v, w_v, cot, xb, yb, gvb, mixb, dyb, rsb, endb, startb,
+     normed, csr, csc, totb, dec, cross, gb, stb, hcb, hst, sumd, segr, segc, dxi,
      sloc, lb, tb, ub, qs, qb, vs, s_in,
      rloc, lb2, tb2, ub2, qs2, qb2, vs2, h_in,
-     dxs, dzs, sums, gx, gz, pw, xr, zs, zr, accw, accr, red, redo,
+     vtop, dxs, dzs, sums, gx, gz, pw, xa, xd, xm, xc, zs, zr, accw, accr, red, redo,
      cp_sem, s_ag, r_ag, s_dx, r_dx, s_dz, r_dz,
      s_p1, r_p1, s_p2, r_p2, s_p3, r_p3, s_p4, r_p4,
      s_h1, r_h1, s_h2, r_h2, s_h3, r_h3, s_h4, r_h4,
@@ -55,6 +64,7 @@
     t = lax.axis_index("tp")
     z, x = lax.div(s, nx), lax.rem(s, nx)
     y, half = lax.div(t, 2), lax.rem(t, 2)
+    shard = cot.shape[0] // ntp
 
     def dev_x(p):
         return {"seq": z * nx + p, "tp": t}
@@ -82,7 +92,10 @@
             p = lax.rem(me + d, n)
             rcopy(dst_of(p), dst_of(p), ssem.at[d], rsem.at[p], dev(p)).wait_recv()
 
-    load_cot = pltpu.make_async_copy(cot_hbm, cot_all.at[t], cp_sem.at[0])
+    def cot_rows(p, first=0, count=shard):
+        return cot.at[pl.ds(pl.multiple_of(p * shard + first, 16), count)]
+
+    load_cot = pltpu.make_async_copy(cot_hbm, cot_rows(t), cp_sem.at[0])
     load_gate = pltpu.make_async_copy(gate_hbm, gate_v, cp_sem.at[1])
     load_w = pltpu.make_async_copy(w_hbm, w_v, cp_sem.at[2])
     load_cot.start()
@@ -96,55 +109,101 @@
                 barrier, inc=1, device_id=dev(lax.rem(me + d, n)), device_id_type=MESH
             )
 
-    spread = (iota((SLOT, width), 1) // HEAD == iota((SLOT, width), 0)).astype(F32)
-    gather = (iota((width, SLOT), 0) // HEAD == iota((width, SLOT), 1)).astype(F32)
-    upper = (iota((L, L), 0) <= iota((L, L), 1)).astype(F32)
-    lower = (iota((L, L), 0) <= iota((L, L), 1)).astype(F32)
+    spread = (iota((SLOT, width), 1) // HEAD == iota((SLOT, width), 0)).astype(BF16)
+    gather = (iota((width, SLOT), 0) // HEAD == iota((width, SLOT), 1)).astype(BF16)
+    upper = (iota((L, L), 0) <= iota((L, L), 1)).astype(BF16)
     causal = iota((L, L), 0) >= iota((L, L), 1)
     left = iota((L, 128), 1) < HEAD
 
+    def spread_heads(v):
+        return sum(dot(part, spread) for part in pieces(v, 3))
+
+    def head_sums(v):
+        return sum(dot(part, gather) for part in pieces(v, 2))
+
     csr[...] = jnp.zeros_like(csr)
     segr[...] = jnp.zeros_like(segr)
-    log_total = jnp.zeros((1, SLOT), F32)
     for k in range(chunks):
         csr[k, 0:heads, :] = ld_ref[:, k * L : (k + 1) * L]
-        rows = dot(csr[k], upper, precision=EXACT)
-        csr[k] = rows
-        cols = rows.T
+    rows = csr[...].reshape(chunks * SLOT, L)
+    rows = sum(dot(part, upper) for part in pieces(rows, 3))
+    log_total = jnp.zeros((1, width), F32)
+    for k in range(chunks):
+        csr[k] = rows[k * SLOT : (k + 1) * SLOT, :]
+        cols = rows[k * SLOT : (k + 1) * SLOT, :].T
         csc[k] = cols
-        last = cols[L - 1 : L, :]
+        logs = spread_heads(cols)
+        last = logs[L - 1 : L, :]
         log_total = log_total + last
-        totb[k] = dot(jnp.broadcast_to(jnp.exp(last), (8, SLOT)), spread, precision=EXACT)[0:1]
-        endb[k * L : (k + 1) * L, :] = dot(jnp.exp(last - cols), spread, precision=EXACT)
-        startb[k * L : (k + 1) * L, :] = dot(jnp.exp(cols), spread, precision=EXACT)
-    decay_all = dot(jnp.broadcast_to(jnp.exp(log_total), (8, SLOT)), spread, precision=EXACT)[0:1]
-    dxs[x] = decay_all
+        totb[k] = jnp.exp(last)
+        endb[k * L : (k + 1) * L, :] = jnp.exp(last - logs)
+        startb[k * L : (k + 1) * L, :] = jnp.exp(logs)
+    dxs[x] = jnp.exp(log_total)
 
     pl.semaphore_wait(barrier, (nx - 1) + (nz - 1) + (ntp - 1))
     send(X, lambda p: dxs.at[x], dxs.at[x], s_dx, r_dx)
 
     load_cot.wait()
-    sibling = dev_t(2 * y + 1 - half)
-    copy = rcopy(cot_all.at[t], cot_all.at[t], s_ag.at[ny], r_ag.at[t], sibling)
-    copy.start()
-    pending.append(copy)
-    for d in range(1, ny):
-        p = 2 * lax.rem(y + d, ny) + half
-        copy = rcopy(cot_all.at[t], cot_all.at[t], s_ag.at[d], r_ag.at[t], dev_t(p))
+    part = shard // 2
+    sibling = 2 * y + 1 - half
+    after = 2 * lax.rem(y + 1, ny) + half
+    before = 2 * lax.rem(y + ny - 1, ny) + half
+    across = 2 * lax.rem(y + 2, ny) + half
+
+    def cot_copy(i, j, p, to, first=0, count=shard):
+        return rcopy(cot_rows(p, first, count), cot_rows(p, first, count), s_ag.at[i], r_ag.at[j], dev_t(to))
+
+    def cot_send(i, j, p, to, *rows):
+        copy = cot_copy(i, j, p, to, *rows)
         copy.start()
         pending.append(copy)
 
-    def share_cot(d):
-        p = 2 * lax.rem(y + d, ny) + half
-        rcopy(cot_all.at[p], cot_all.at[p], s_ag.at[d], r_ag.at[p], dev_t(p)).wait_recv()
-        copy = rcopy(cot_all.at[p], cot_all.at[p], s_ag.at[ny + d], r_ag.at[p], sibling)
-        copy.start()
-        pending.append(copy)
-
-    def sibling_cot():
-        for d in range(ny):
-            p = 2 * lax.rem(y + d, ny) + 1 - half
-            rcopy(cot_all.at[p], cot_all.at[p], s_ag.at[d], r_ag.at[p], sibling).wait_recv()
+    def cot_wait(j, p, *rows):
+        cot_copy(0, j, p, sibling, *rows).wait_recv()
+
+    cot_send(0, 0, t, sibling)
+    if ny == 2:
+        cot_send(1, 1, t, after)
+    elif ny == 4:
+        cot_send(1, 1, t, after, 0, part)
+        cot_send(2, 3, t, before, part, part)
+        cot_send(3, 2, t, after, part, part)
+        cot_send(4, 4, t, before, 0, part)
+
+    def relay_cot():
+        if ny == 4:
+            cot_wait(1, before, 0, part)
+            cot_send(5, 5, before, after, 0, part)
+            cot_wait(3, after, part, part)
+            cot_send(6, 6, after, before, part, part)
+
+    def near_cot():
+        if ny == 2:
+            cot_wait(1, after)
+            cot_send(2, 7, after, sibling)
+        elif ny == 4:
+            cot_wait(2, before, part, part)
+            cot_send(7, 7, before, sibling)
+            cot_wait(4, after, 0, part)
+            cot_send(8, 8, after, sibling)
+
+    def far_cot():
+        if ny == 4:
+            cot_wait(5, across, 0, part)
+            cot_wait(6, across, part, part)
+            cot_send(9, 9, across, sibling)
+
+    def project(chip, first=False):
+        terms = dot(
+            cot[pl.ds(pl.multiple_of(chip * 2 * shard, 128), 2 * shard), :],
+            w_v[:, pl.ds(pl.multiple_of(chip * 2 * shard, 128), 2 * shard)],
+            0,
+            1,
+        )
+        gvb[...] = terms if first else gvb[...] + terms
+
+    def other(p):
+        return p + 1 - 2 * half
 
     powers = lax.shift_left(jnp.ones_like(expo[...]), expo[...] + 5).astype(F32) * (1.0 / 32.0)
     nibble = 4 * iota((8, width), 0)
@@ -175,8 +234,8 @@
     run = jnp.zeros((128, width), F32)
     for k in range(chunks):
         rows = slice(k * L, (k + 1) * L)
-        weighted = (xb[rows, :].astype(F32) * endb[rows, :]).astype(BF16)
-        gb[k] = dot(b_ref[rows, :], weighted, 0, 0)
+        weighted = xb[rows, :].astype(F32) * endb[rows, :]
+        gb[k] = sum(dot(b_ref[rows, :], part, 0, 0) for part in pieces(weighted, 2))
         run = totb[k] * run + gb[k]
     sloc[...] = run
 
@@ -198,7 +257,8 @@
         order = range(nx - 1, -1, -1) if backward else range(nx)
         row = None
         for k in order:
-            row = lbuf[k] if row is None else dxs[k] * row + lbuf[k]
+            add = lbuf[k].astype(F32)
+            row = add if row is None else dxs[k] * row + add
         for k in range(nz):
             tbuf[k] = row[k * erows : (k + 1) * erows, :]
         send(Z, lambda p: tbuf.at[p], ubuf.at[z], ssem, rsem)
@@ -216,15 +276,13 @@
 
     def exchange_4(qbuf, lbuf, vsend, result, s3, r3, ssem, rsem, backward):
         arrive(Z, lambda p: qbuf.at[p], s3, r3)
-        first = nx - 1 if backward else 0
         for k in range(nz):
-            vsend[first, k * erows : (k + 1) * erows, :] = qbuf[k]
+            vtop[k * erows : (k + 1) * erows, :] = qbuf[k]
         order = range(nx - 1, -1, -1) if backward else range(nx)
-        row = vsend[first]
+        row = vtop[...]
         for k in order:
-            if k != first:
-                vsend[k] = row
-            row = dxs[k] * row + lbuf[k]
+            vsend[k] = row.astype(vsend.dtype)
+            row = dxs[k] * row + lbuf[k].astype(F32)
         mine = result.at[pl.ds(pl.multiple_of(x * qrows, qrows), qrows)]
         send(X, lambda p: vsend.at[p], mine, ssem, rsem)
         result[pl.ds(pl.multiple_of(x * qrows, qrows), qrows), :] = vsend[x]
@@ -241,13 +299,10 @@
     dzs[z] = row
     send(Z, lambda p: dzs.at[z], dzs.at[z], s_dz, r_dz)
 
-    skip_row = dot(
-        jnp.concatenate(
-            [jnp.broadcast_to(skip_ref[...], (8, heads)), jnp.zeros((8, SLOT - heads), F32)], axis=1
-        ),
-        spread,
-        precision=EXACT,
-    )[0:1]
+    skip_row = jnp.zeros((1, width), F32)
+    head_of = iota((1, width), 1) // HEAD
+    for h in range(heads):
+        skip_row = jnp.where(head_of == h, skip_ref[0, h], skip_row)
 
     def at_chunk(k):
         return pl.ds(pl.multiple_of(k * L, L), L)
@@ -266,52 +321,63 @@
                 spread_log = csc[k][:, h : h + 1] - csr[k][h : h + 1, :]
                 decay = jnp.where(causal, jnp.exp(jnp.minimum(spread_log, 0.0)), 0.0)
                 dec[k, h] = decay
-                mixing.append((decay * both).astype(BF16))
+                mixing.append(pieces(decay * both, 2))
             lanes = slice(128 * p, 128 * (p + 1))
             x_pair = xb[rows, lanes]
+            x_split = split_pair(x_pair)
             yb[rows, lanes] = (
-                dot(jnp.concatenate(mixing, axis=1), split_pair(x_pair))
+                dot(jnp.concatenate([m[0] for m in mixing], axis=1), x_split)
+                + dot(jnp.concatenate([m[1] for m in mixing], axis=1), x_split)
                 + skip_row[:, lanes] * x_pair.astype(F32)
             )
         return 0
 
     lax.fori_loop(0, chunks // 2, inside, 0)
+    load_w.wait()
+    cot_wait(0, sibling)
+    project(y, True)
     exchange_2(lb, tb, ub, s_p1, r_p1, s_p2, r_p2, False)
+    relay_cot()
     lax.fori_loop(chunks // 2, chunks, inside, 0)
     arrive(Z, lambda p: dzs.at[p], s_dz, r_dz)
     exchange_3(ub, qs, qb, s_p2, r_p2, s_p3, r_p3, False)
+    near_cot()
     exchange_4(qb, lb, vs, s_in, s_p3, r_p3, s_p4, r_p4, False)
-    for d in range(1, ny):
-        share_cot(d)
-    sibling_cot()
-    shard = cot_all.shape[2]
-    for p in range(ntp):
-        cot_full[:, p * shard : (p + 1) * shard] = cot_all[p]
-    load_w.wait()
-
-    def project(k, _):
-        rows = at_chunk(k)
-        gvb[rows, :] = dot(cot_full[rows, :], w_v[...], 1, 1)
-        return 0
-
-    lax.fori_loop(0, chunks, project, 0)
+    if ny == 2:
+        cot_wait(7, other(after))
+        project(lax.rem(y + 1, ny))
+    elif ny == 4:
+        cot_wait(7, other(before))
+        project(lax.rem(y + 3, ny))
+        cot_wait(8, other(after))
+        project(lax.rem(y + 1, ny))
+    far_cot()
     load_gate.wait()
     exchange_5(s_in, s_p4, r_p4)
-
-    gain_row = gain_ref[...]
-    stb[0] = s_in[...]
+    gain_row = gain_ref[...].reshape(1, width)
+    stb[0] = s_in[...].astype(F32)
     for k in range(1, chunks):
         stb[k] = totb[k - 1] * stb[k - 1] + gb[k - 1]
 
     def outputs_of(k, _):
         rows = at_chunk(k)
-        start = dot(c_ref[rows, :], stb[k].astype(BF16))
+        start = sum(dot(c_ref[rows, :], part) for part in pieces(stb[k], 2))
         rsb[rows, :] = start
         y_now = yb[rows, :] + startb[rows, :] * start
         yb[rows, :] = y_now
         gate = gate_v[rows, :].astype(F32)
         mixed = y_now * gate * jax.nn.sigmoid(gate)
         mixb[rows, :] = mixed
+        return 0
+
+    lax.fori_loop(0, chunks, outputs_of, 0)
+    if ny == 4:
+        cot_wait(9, other(across))
+        project(lax.rem(y + 2, ny))
+
+    def sums_of(k, _):
+        rows = at_chunk(k)
+        mixed = mixb[rows, :]
         square = jnp.sum(mixed * mixed, axis=1, keepdims=True)
         inner = jnp.sum(gvb[rows, :] * gain_row * mixed, axis=1, keepdims=True)
         lane = iota((L, 128), 1)
@@ -319,7 +385,7 @@
         sums[t, k] = packed_sums.T[0:8, :]
         return 0
 
-    lax.fori_loop(0, chunks, outputs_of, 0)
+    lax.fori_loop(0, chunks, sums_of, 0)
     send(TP, lambda p: sums.at[t], sums.at[t], s_tp, r_tp)
     arrive(TP, lambda p: sums.at[p], s_tp, r_tp)
 
@@ -348,8 +414,9 @@
         skip_sum = skip_sum + jnp.sum(
             grad_y * xb[rows, :].astype(F32), axis=0, keepdims=True
         )
-        hcb[k] = dot(c_ref[rows, :], (grad_y * startb[rows, :]).astype(BF16), 0, 0)
-        mixb[rows, :] = mixed * scale * gain_row
+        scaled = grad_y * startb[rows, :]
+        hcb[k] = sum(dot(c_ref[rows, :], part, 0, 0) for part in pieces(scaled, 2))
+        normed[rows, :] = (mixed * scale * gain_row).astype(BF16)
         return gain_sum, skip_sum
 
     zero_row = jnp.zeros((1, width), F32)
@@ -357,44 +424,77 @@
     run = hcb[chunks - 1]
     for k in range(chunks - 2, -1, -1):
         run = totb[k] * run + hcb[k]
-    rloc[...] = run
+    rloc[...] = run.astype(BF16)
     exchange_1(rloc, lb2, s_h1, r_h1)
     gx[x, 0:1, :] = gain_sum
     gx[x, 1:2, :] = skip_sum
     send(X, lambda p: gx.at[x], gx.at[x], s_gx, r_gx)
 
     columns = shard // nx
-
-    def weight_block(k):
-        normed = mixb[...].astype(BF16)
-        pw[k] = dot(cot_all[k], normed, 0, 0).astype(BF16)
-        for d in range(1, nx):
-            p = lax.rem(x + d, nx)
-            copy = rcopy(
-                pw.at[k, pl.ds(pl.multiple_of(p * columns, columns), columns)],
-                xr.at[x, k],
-                s_rx.at[d, k],
-                r_rx.at[x, k],
-                dev_x(p),
-            )
+    steps = sorted(range(1, nz), key=lambda i: -min(i, nz - i)) + [nz]
+
+    def block_of(i):
+        return lax.rem(z + i, nz)
+
+    def mine_of(i, p):
+        return pw.at[block_of(i), pl.ds(pl.multiple_of(p * columns, columns), columns)]
+
+    def sides(i):
+        one, two = lax.rem(x + 1, nx), lax.rem(x + nx - 1, nx)
+        return (one, two) if steps.index(i) % 2 == 0 else (two, one)
+
+    def weight_copy(kind, i, to):
+        source = (mine_of(i, lax.rem(x + 2, nx)), mine_of(i, to), xm.at[i - 1])[kind]
+        target = (xa, xd, xc)[kind].at[i - 1]
+        return rcopy(source, target, s_rx.at[kind, i - 1], r_rx.at[kind, i - 1], dev_x(to))
+
+    def weight_send(kind, i, to):
+        copy = weight_copy(kind, i, to)
+        copy.start()
+        pending.append(copy)
+
+    def weight_block(i):
+        k = block_of(i)
+        pw[k] = dot(cot[pl.ds(pl.multiple_of(k * shard, shard), shard), :], normed[...]).astype(BF16)
+        near, far = sides(i)
+        if nx == 4:
+            weight_send(0, i, near)
+        if nx > 1:
+            weight_send(1, i, far)
+
+    def weight_relay(i):
+        near, _ = sides(i)
+        if nx == 4:
+            weight_copy(0, i, near).wait_recv()
+            xm[i - 1] = (xa[i - 1].astype(F32) + mine_of(i, near)[...].astype(F32)).astype(BF16)
+            weight_send(2, i, near)
+
+    def weight_rows(i):
+        near, far = sides(i)
+        out = mine_of(i, x)[...].astype(F32)
+        if nx > 1:
+            weight_copy(1, i, far).wait_recv()
+            out = out + xd[i - 1].astype(F32)
+        if nx == 4:
+            weight_copy(2, i, near).wait_recv()
+            out = out + xc[i - 1].astype(F32)
+        zs[i - 1] = out.astype(BF16)
+        if i < nz:
+            copy = rcopy(zs.at[i - 1], zr.at[i - 1], s_rz.at[i - 1], r_rz.at[i - 1], dev_z(block_of(i)))
             copy.start()
             pending.append(copy)
 
-    def weight_rows(k):
-        out = pw[k, pl.ds(pl.multiple_of(x * columns, columns), columns), :].astype(F32)
-        for d in range(1, nx):
-            p = lax.rem(x + d, nx)
-            rcopy(xr.at[p, k], xr.at[p, k], s_rx.at[d, k], r_rx.at[p, k], dev_x(p)).wait_recv()
-            out = out + xr[p, k].astype(F32)
-        zs[k] = out.astype(BF16)
-
-        @pl.when(z != k)
-        def _():
-            rcopy(zs.at[k], zr.at[z], s_rz.at[k], r_rz.at[z], dev_z(k)).start()
-
-    first_blocks = nz // 2
-    for k in range(first_blocks):
-        weight_block(k)
+    def weight_finish():
+        out = zs[nz - 1].astype(F32)
+        for i in steps[:-1]:
+            rcopy(zs.at[i - 1], zr.at[i - 1], s_rz.at[i - 1], r_rz.at[i - 1], dev_z(block_of(i))).wait_recv()
+            out = out + zr[i - 1].astype(F32)
+        gow[...] = out
+
+    early = steps[: (3 * nz) // 8]
+    later = steps[(3 * nz) // 8 :]
+    for i in early:
+        weight_block(i)
     exchange_2(lb2, tb2, ub2, s_h1, r_h1, s_h2, r_h2, True)
     arrive(X, lambda p: gx.at[p], s_gx, r_gx)
     row = gx[0]
@@ -438,6 +538,8 @@
     lax.fori_loop(0, chunks // 2, inside_back, 0)
     exchange_3(ub2, qs2, qb2, s_h2, r_h2, s_h3, r_h3, True)
     lax.fori_loop(chunks // 2, chunks, inside_back, 0)
+    for i in early[:-1]:
+        weight_relay(i)
     exchange_4(qb2, lb2, vs2, h_in, s_h3, r_h3, s_h4, r_h4, True)
 
     share = tokens // ntp
@@ -466,91 +568,145 @@
             out_ref[p * share : (p + 1) * share, :] = redo[which, p]
 
     reduce_1(accr, 0, s_c1, r_c1)
-    for k in range(first_blocks, nz):
-        weight_block(k)
-    for k in range(first_blocks):
-        weight_rows(k)
+    for i in early[-1:]:
+        weight_relay(i)
+    for i in later:
+        weight_block(i)
     exchange_5(h_in, s_h4, r_h4)
 
-    def finish(i, run):
+    def states_back(i, run):
         k = chunks - 1 - i
         rows = at_chunk(k)
-        h_low = run.astype(BF16)
-        end = endb[rows, :]
+        hst[k] = run
+        accw[rows, :] = dot(sumd[k].astype(BF16), c_ref[rows, :], 0, 0) + dot(
+            (xb[rows, :].astype(F32) * endb[rows, :]).astype(BF16), run.astype(BF16), 1, 1
+        )
+        return totb[k] * run + hcb[k]
+
+    lax.fori_loop(0, chunks, states_back, h_in[...].astype(F32))
+    reduce_1(accw, 1, s_w1, r_w1)
+    def finish(k, _):
+        rows = at_chunk(k)
         grad_y = dyb[rows, :]
-        x_now = xb[rows, :].astype(F32)
-        write = end * dot(b_ref[rows, :], h_low)
+        run = hst[k]
+        write = endb[rows, :] * sum(dot(b_ref[rows, :], part) for part in pieces(run, 2))
         gin[rows, :] = (skip_row * grad_y + dxi[rows, :] + write).astype(BF16)
-        accw[rows, :] = dot(sumd[k].astype(BF16), c_ref[rows, :], 0, 0) + dot(
-            (x_now * end).astype(BF16), h_low, 1, 1
-        )
-        leaving = dot(x_now * write, gather, precision=EXACT)
-        arriving = dot(grad_y * startb[rows, :] * rsb[rows, :], gather, precision=EXACT)
-        seg = segc[k] + arriving - leaving
-        across = totb[k] * jnp.sum(run * stb[k], axis=0, keepdims=True)
-        final = jnp.sum(leaving, axis=0, keepdims=True) + dot(
-            jnp.broadcast_to(across, (8, width)), gather, precision=EXACT
-        )[0:1]
-        whole = dot(lower, seg, precision=EXACT) + final
+        leaving = xb[rows, :].astype(F32) * write
+        arriving = grad_y * startb[rows, :] * rsb[rows, :]
+        seg = segc[k] + head_sums(arriving - leaving)
+        final = jnp.sum(leaving, axis=0, keepdims=True) + totb[k] * jnp.sum(
+            run * stb[k], axis=0, keepdims=True
+        )
+        final = head_sums(jnp.broadcast_to(final, (8, width)))[0:1]
+        whole = sum(dot(upper, part) for part in pieces(seg, 2)) + final
         sumd[k, 0:SLOT, :] = whole.T
-        return totb[k] * run + hcb[k]
-
-    lax.fori_loop(0, chunks, finish, h_in[...])
-    reduce_1(accw, 1, s_w1, r_w1)
+        return 0
+
+    lax.fori_loop(0, chunks, finish, 0)
     for k in range(chunks):
         gdecay[:, k * L : (k + 1) * L] = sumd[k, 0:heads, :]
+    for i in later[:2]:
+        weight_relay(i)
     reduce_2(0, s_c1, r_c1, s_c2, r_c2)
+    reduce_2(1, s_w1, r_w1, s_w2, r_w2)
+    for i in early:
+        weight_rows(i)
+    for i in later[2:3]:
+        weight_relay(i)
     arrive(Z, lambda p: gz.at[p], s_gz, r_gz)
     row = gz[0]
     for k in range(1, nz):
         row = row + gz[k]
     ggain[...] = row[0:1]
-    gskip[...] = dot(row, gather, precision=EXACT)[1:2, 0:heads]
-    reduce_2(1, s_w1, r_w1, s_w2, r_w2)
+    gskip[...] = head_sums(jnp.concatenate([row, jnp.zeros((6, width), F32)], axis=0))[1:2, 0:heads]
+    for i in later[3:4]:
+        weight_relay(i)
+    for i in later[:2]:
+        weight_rows(i)
+    for i in later[4:]:
+        weight_relay(i)
+    for i in later[2:]:
+        weight_rows(i)
     reduce_3(gread, 0, s_c2, r_c2)
-    for k in range(first_blocks, nz):
-        weight_rows(k)
     reduce_3(gwrite, 1, s_w2, r_w2)
-    zr[z] = zs[z]
-    arrive(Z, lambda p: zr.at[p], s_rz, r_rz)
-    out = zr[0].astype(F32)
-    for k in range(1, nz):
-        out = out + zr[k].astype(F32)
-    gow[...] = out.T
+    weight_finish()
     for copy in pending:
         copy.wait_send()
-    for k in range(nz):
-
-        @pl.when(z != k)
-        def _():
-            rcopy(zs.at[k], zr.at[z], s_rz.at[k], r_rz.at[z], dev_z(k)).wait_send()
-
-
-def on_device(nx, nz, ntp, packed, expo, gate, write, read, decay, skip, gain, weight, cot):
+
+
+def copy_out(*refs):
+    count = 8
+    sources, targets, scratch, sem_in, sem_out = (
+        refs[:count],
+        refs[count : 2 * count],
+        refs[2 * count : -2],
+        refs[-2],
+        refs[-1],
+    )
+    large = [k for k in range(count) if k not in (5, 6)]
+    loads = [
+        pltpu.make_async_copy(sources[k], scratch[i], sem_in.at[i]) for i, k in enumerate(large)
+    ]
+    stores = [
+        pltpu.make_async_copy(scratch[i], targets[k], sem_out.at[i]) for i, k in enumerate(large)
+    ]
+    for load in loads:
+        load.start()
+    for k in (5, 6):
+        targets[k][...] = sources[k][...].reshape(targets[k].shape)
+    for load, store in zip(loads, stores):
+        load.wait()
+        store.start()
+    for store in stores:
+        store.wait()
+
+
+def hand_out(outs):
+    vmem = pl.BlockSpec(memory_space=pltpu.VMEM)
+    hbm = pl.BlockSpec(memory_space=pl.ANY)
+    specs = [vmem if k in (5, 6) else hbm for k in range(8)]
+    shapes = [
+        jax.ShapeDtypeStruct(o.shape[1:] if k in (5, 6) else o.shape, o.dtype)
+        for k, o in enumerate(outs)
+    ]
+    large = [o for k, o in enumerate(outs) if k not in (5, 6)]
+    done = pl.pallas_call(
+        copy_out,
+        out_shape=shapes,
+        in_specs=specs,
+        out_specs=specs,
+        scratch_shapes=[pltpu.VMEM(o.shape, o.dtype) for o in large]
+        + [pltpu.SemaphoreType.DMA((6,)), pltpu.SemaphoreType.DMA((6,))],
+        name="hand_out",
+    )(*outs)
+    return (*done[:7], done[7].T)
+
+
+def on_device(nx, nz, ntp, packed, expo, gate, write, read, decay, skip, gain, weight, cotangent):
+    cot = cotangent.T
     tokens, width = gate.shape
     heads = decay.shape[0]
     model = weight.shape[1]
-    shard = cot.shape[1]
+    shard = cot.shape[0]
     chunks = tokens // L
     n = write.shape[1]
     columns = model // (nx * nz)
     qrows, erows = n // nx, n // (nx * nz)
-    ny = ntp // 2
     share = tokens // ntp
 
     def wide(kind=F32):
         return pltpu.VMEM((tokens, width), kind)
 
-    def exchange():
+    def exchange(kind):
         return [
-            pltpu.VMEM((n, width), F32),
-            pltpu.VMEM((nx, qrows, width), F32),
+            pltpu.VMEM((n, width), kind),
+            pltpu.VMEM((nx, qrows, width), kind),
             pltpu.VMEM((nz, erows, width), F32),
             pltpu.VMEM((nz, erows, width), F32),
             pltpu.VMEM((nz, erows, width), F32),
             pltpu.VMEM((nz, erows, width), F32),
-            pltpu.VMEM((nx, qrows, width), F32),
-            pltpu.VMEM((n, width), F32),
+            pltpu.VMEM((nx, qrows, width), kind),
+            pltpu.VMEM((n, width), kind),
         ]
 
     def sems(*shape):
@@ -559,10 +715,10 @@
     scratch = [
         pltpu.VMEM((tokens, width), BF16),
         pltpu.VMEM((width, model), BF16),
-        pltpu.VMEM((ntp, tokens, shard), BF16),
-        pltpu.VMEM((tokens, model), BF16),
+        pltpu.VMEM((model, tokens), BF16),
         wide(BF16),
         *[wide() for _ in range(7)],
+        wide(BF16),
         pltpu.VMEM((chunks, SLOT, L), F32),
         pltpu.VMEM((chunks, L, SLOT), F32),
         pltpu.VMEM((chunks, 1, width), F32),
@@ -571,28 +727,27 @@
         pltpu.VMEM((chunks, n, width), F32),
         pltpu.VMEM((chunks, n, width), F32),
         pltpu.VMEM((chunks, n, width), F32),
+        pltpu.VMEM((chunks, n, width), F32),
         pltpu.VMEM((chunks, L, L), F32),
         pltpu.VMEM((chunks, SLOT, L), F32),
         pltpu.VMEM((chunks, L, SLOT), F32),
         wide(),
-        *exchange(),
-        *exchange(),
+        *exchange(F32),
+        *exchange(BF16),
+        pltpu.VMEM((qrows, width), F32),
         pltpu.VMEM((nx, 1, width), F32),
         pltpu.VMEM((nz, 1, width), F32),
         pltpu.VMEM((ntp, chunks, 8, L), F32),
         pltpu.VMEM((nx, 2, width), F32),
         pltpu.VMEM((nz, 2, width), F32),
         pltpu.VMEM((nz, shard, width), BF16),
-        pltpu.VMEM((nx, nz, columns, width), BF16),
-        pltpu.VMEM((nz, columns, width), BF16),
-        pltpu.VMEM((nz, columns, width), BF16),
+        *[pltpu.VMEM((nz, columns, width), BF16) for _ in range(6)],
         pltpu.VMEM((tokens, n), F32),
         pltpu.VMEM((tokens, n), F32),
         pltpu.VMEM((2, ntp, share, n), F32),
         pltpu.VMEM((2, ntp, share, n), F32),
         pltpu.SemaphoreType.DMA((3,)),
-        pltpu.SemaphoreType.DMA((2 * ny,)),
-        pltpu.SemaphoreType.DMA((ntp,)),
+        *sems(10),
         *sems(nx),
         *sems(nz),
         *(sems(nx) + sems(nz) + sems(nz) + sems(nx)),
@@ -600,7 +755,7 @@
         *sems(ntp),
         *sems(nx),
         *sems(nz),
-        *sems(nx, nz),
+        *sems(3, nz),
         *sems(nz),
         *(sems(ntp) * 4),
     ]
@@ -616,17 +771,17 @@
             jax.ShapeDtypeStruct((heads, tokens), F32),
             jax.ShapeDtypeStruct((1, heads), F32),
             jax.ShapeDtypeStruct((1, width), F32),
-            jax.ShapeDtypeStruct((width, columns), F32),
+            jax.ShapeDtypeStruct((columns, width), F32),
         ),
-        in_specs=[vmem, vmem, hbm, vmem, vmem, vmem, vmem, vmem, hbm, hbm],
+        in_specs=[vmem, vmem, hbm, vmem, vmem, vmem, pl.BlockSpec(memory_space=pltpu.SMEM), vmem, hbm, hbm],
         out_specs=(vmem,) * 8,
         scratch_shapes=scratch,
         compiler_params=pltpu.CompilerParams(
             collective_id=0, has_side_effects=True, vmem_limit_bytes=60 * 1024 * 1024
         ),
         name="layer_backward",
-    )(packed, expo, gate, write, read, decay, skip[None, :], gain[None, :], weight, cot)
-    return (*outs[:5], outs[5][0], outs[6][0], outs[7])
+    )(packed, expo, gate, write, read, decay, skip[None, :], gain, weight, cot)
+    return hand_out(outs)
 
 
 def solution(mesh):

time: 122 us -> 97.5 us (0.80)
  Pallas kernels: 109 us -> 96.7 us
  local copies, waits for them, and re-layouts: 11.5 us -> 0 us
  other arithmetic: 1.32 us -> 0 us
    pallas_call x1, Pallas kernels: 109 us -> 93 us  [on_device(): pl.pallas_call(functools.partial(core, nx, nz, ntp), out_shape=(jax.Shape...]
    unnamed x16 -> x0, local copies, waits for them, and re-layouts: 10.2 us -> none
    pallas_call x0 -> x1, Pallas kernels: none -> 3.74 us  [hand_out(): pl.pallas_call(copy_out, out_shape=shapes, in_specs=specs, out_specs=spec...]
    pallas_call x1 -> x0, other arithmetic: 1.32 us -> none  [on_device(): pl.pallas_call(functools.partial(core, nx, nz, ntp), out_shape=(jax.Shape...]
    broadcast_in_dim x1 -> x0, local copies, waits for them, and re-layouts: 1.27 us -> none  [on_device(): gain[None, :]]
where the time goes in v2:
time: 97.5 us; the launch traced here: 97.4 us
  Pallas kernels  96.7 us (99%)
    pallas_call x1, Pallas kernels, on_device(): pl.pallas_call(functools.partial(core, nx, nz, ntp), out_shape=(jax.Shape...  93 us
    pallas_call x1, Pallas kernels, hand_out(): pl.pallas_call(copy_out, out_shape=shapes, in_specs=specs, out_specs=spec...  3.74 us

profile of v2, /device:TPU:1, one launch (start us, length us, event | category | flops | bytes accessed | tf_op | source)
XLA Modules:
  0.0 97.4 jit_solution(1639635894298493888)
XLA Ops:
  0.6 93.0 %layer_backward.1 = (bf16[512,640]{1,0:T(8,128)(2,1)}, bf16[512,640]{1,0:T(8,128)(2,1)}, f32[512,128]{1,0:T(8,128)}, f32[512,128]{1,0:T(8,128)}, f32[10,512]{1,0...) custom-call(s32[64,640]{1,0:T(8,128)} %packed.1, s32[5,512]{1,0:T(8,128)} %expo.1, ...), custom_call_target="tpu_custom_call" | custom-call | tf_op jit(solution)/shard_map/layer_backward/pallas_call | solution.py:764
  93.6 3.7 %hand_out.1 = (bf16[512,640]{1,0:T(8,128)(2,1)}, bf16[512,640]{1,0:T(8,128)(2,1)}, f32[512,128]{1,0:T(8,128)}, f32[512,128]{1,0:T(8,128)}, f32[10,512]{1,0:T(8,1...) custom-call(bf16[512,640]{1,0:T(8,128)(2,1)} %get-tuple-element.24.refs_0_, ...), custom_call_target="tpu_custom_call" | custom-call | tf_op jit(solution)/shard_map/hand_out/pallas_call | solution.py:673

commit v3 on v2

--- a/solution.py
+++ b/solution.py
@@ -47,7 +47,7 @@
      normed, csr, csc, totb, dec, cross, gb, stb, hcb, hst, sumd, segr, segc, dxi,
      sloc, lb, tb, ub, qs, qb, vs, s_in,
      rloc, lb2, tb2, ub2, qs2, qb2, vs2, h_in,
-     vtop, dxs, dzs, sums, gx, gz, pw, xa, xd, xm, xc, zs, zr, accw, accr, red, redo,
+     vtop, dxs, dzs, sums, totc, gx, gz, pw, xa, xd, xm, xc, zs, zr, accw, accr, red, redo,
      cp_sem, s_ag, r_ag, s_dx, r_dx, s_dz, r_dz,
      s_p1, r_p1, s_p2, r_p2, s_p3, r_p3, s_p4, r_p4,
      s_h1, r_h1, s_h2, r_h2, s_h3, r_h3, s_h4, r_h4,
@@ -140,71 +140,6 @@
         startb[k * L : (k + 1) * L, :] = jnp.exp(logs)
     dxs[x] = jnp.exp(log_total)
 
-    pl.semaphore_wait(barrier, (nx - 1) + (nz - 1) + (ntp - 1))
-    send(X, lambda p: dxs.at[x], dxs.at[x], s_dx, r_dx)
-
-    load_cot.wait()
-    part = shard // 2
-    sibling = 2 * y + 1 - half
-    after = 2 * lax.rem(y + 1, ny) + half
-    before = 2 * lax.rem(y + ny - 1, ny) + half
-    across = 2 * lax.rem(y + 2, ny) + half
-
-    def cot_copy(i, j, p, to, first=0, count=shard):
-        return rcopy(cot_rows(p, first, count), cot_rows(p, first, count), s_ag.at[i], r_ag.at[j], dev_t(to))
-
-    def cot_send(i, j, p, to, *rows):
-        copy = cot_copy(i, j, p, to, *rows)
-        copy.start()
-        pending.append(copy)
-
-    def cot_wait(j, p, *rows):
-        cot_copy(0, j, p, sibling, *rows).wait_recv()
-
-    cot_send(0, 0, t, sibling)
-    if ny == 2:
-        cot_send(1, 1, t, after)
-    elif ny == 4:
-        cot_send(1, 1, t, after, 0, part)
-        cot_send(2, 3, t, before, part, part)
-        cot_send(3, 2, t, after, part, part)
-        cot_send(4, 4, t, before, 0, part)
-
-    def relay_cot():
-        if ny == 4:
-            cot_wait(1, before, 0, part)
-            cot_send(5, 5, before, after, 0, part)
-            cot_wait(3, after, part, part)
-            cot_send(6, 6, after, before, part, part)
-
-    def near_cot():
-        if ny == 2:
-            cot_wait(1, after)
-            cot_send(2, 7, after, sibling)
-        elif ny == 4:
-            cot_wait(2, before, part, part)
-            cot_send(7, 7, before, sibling)
-            cot_wait(4, after, 0, part)
-            cot_send(8, 8, after, sibling)
-
-    def far_cot():
-        if ny == 4:
-            cot_wait(5, across, 0, part)
-            cot_wait(6, across, part, part)
-            cot_send(9, 9, across, sibling)
-
-    def project(chip, first=False):
-        terms = dot(
-            cot[pl.ds(pl.multiple_of(chip * 2 * shard, 128), 2 * shard), :],
-            w_v[:, pl.ds(pl.multiple_of(chip * 2 * shard, 128), 2 * shard)],
-            0,
-            1,
-        )
-        gvb[...] = terms if first else gvb[...] + terms
-
-    def other(p):
-        return p + 1 - 2 * half
-
     powers = lax.shift_left(jnp.ones_like(expo[...]), expo[...] + 5).astype(F32) * (1.0 / 32.0)
     nibble = 4 * iota((8, width), 0)
     for k in range(chunks):
@@ -238,6 +173,71 @@
         gb[k] = sum(dot(b_ref[rows, :], part, 0, 0) for part in pieces(weighted, 2))
         run = totb[k] * run + gb[k]
     sloc[...] = run
+
+    pl.semaphore_wait(barrier, (nx - 1) + (nz - 1) + (ntp - 1))
+    send(X, lambda p: dxs.at[x], dxs.at[x], s_dx, r_dx)
+
+    load_cot.wait()
+    part = shard // 2
+    sibling = 2 * y + 1 - half
+    after = 2 * lax.rem(y + 1, ny) + half
+    before = 2 * lax.rem(y + ny - 1, ny) + half
+    across = 2 * lax.rem(y + 2, ny) + half
+
+    def cot_copy(i, j, p, to, first=0, count=shard):
+        return rcopy(cot_rows(p, first, count), cot_rows(p, first, count), s_ag.at[i], r_ag.at[j], dev_t(to))
+
+    def cot_send(i, j, p, to, *rows):
+        copy = cot_copy(i, j, p, to, *rows)
+        copy.start()
+        pending.append(copy)
+
+    def cot_wait(j, p, *rows):
+        cot_copy(0, j, p, sibling, *rows).wait_recv()
+
+    cot_send(0, 0, t, sibling)
+    if ny == 2:
+        cot_send(1, 1, t, after)
+    elif ny == 4:
+        cot_send(1, 1, t, after, 0, part)
+        cot_send(2, 3, t, before, part, part)
+        cot_send(3, 2, t, after, part, part)
+        cot_send(4, 4, t, before, 0, part)
+
+    def relay_cot():
+        if ny == 4:
+            cot_wait(1, before, 0, part)
+            cot_send(5, 5, before, after, 0, part)
+            cot_wait(3, after, part, part)
+            cot_send(6, 6, after, before, part, part)
+
+    def near_cot():
+        if ny == 2:
+            cot_wait(1, after)
+            cot_send(2, 7, after, sibling)
+        elif ny == 4:
+            cot_wait(2, before, part, part)
+            cot_send(7, 7, before, sibling)
+            cot_wait(4, after, 0, part)
+            cot_send(8, 8, after, sibling)
+
+    def far_cot():
+        if ny == 4:
+            cot_wait(5, across, 0, part)
+            cot_wait(6, across, part, part)
+            cot_send(9, 9, across, sibling)
+
+    def project(chip, first=False):
+        terms = dot(
+            cot[pl.ds(pl.multiple_of(chip * 2 * shard, 128), 2 * shard), :],
+            w_v[:, pl.ds(pl.multiple_of(chip * 2 * shard, 128), 2 * shard)],
+            0,
+            1,
+        )
+        gvb[...] = terms if first else gvb[...] + terms
+
+    def other(p):
+        return p + 1 - 2 * half
 
     def take_rows(ref, at, count):
         return ref[pl.ds(pl.multiple_of(at * count, count), count), :]
@@ -343,6 +343,7 @@
     exchange_3(ub, qs, qb, s_p2, r_p2, s_p3, r_p3, False)
     near_cot()
     exchange_4(qb, lb, vs, s_in, s_p3, r_p3, s_p4, r_p4, False)
+    far_cot()
     if ny == 2:
         cot_wait(7, other(after))
         project(lax.rem(y + 1, ny))
@@ -351,7 +352,6 @@
         project(lax.rem(y + 3, ny))
         cot_wait(8, other(after))
         project(lax.rem(y + 1, ny))
-    far_cot()
     load_gate.wait()
     exchange_5(s_in, s_p4, r_p4)
     gain_row = gain_ref[...].reshape(1, width)
@@ -375,57 +375,75 @@
         cot_wait(9, other(across))
         project(lax.rem(y + 2, ny))
 
-    def sums_of(k, _):
+    lane = iota((L, 128), 1)
+
+    def sums_of(k, acc):
         rows = at_chunk(k)
         mixed = mixb[rows, :]
         square = jnp.sum(mixed * mixed, axis=1, keepdims=True)
         inner = jnp.sum(gvb[rows, :] * gain_row * mixed, axis=1, keepdims=True)
-        lane = iota((L, 128), 1)
-        packed_sums = jnp.where(lane == 0, square, jnp.where(lane == 1, inner, 0.0))
-        sums[t, k] = packed_sums.T[0:8, :]
-        return 0
-
-    lax.fori_loop(0, chunks, sums_of, 0)
+        return jnp.where(lane == 2 * k, square, jnp.where(lane == 2 * k + 1, inner, acc))
+
+    packed_sums = lax.fori_loop(0, chunks, sums_of, jnp.zeros((L, 128), F32))
+    sums[t] = packed_sums.T[0:8, :]
     send(TP, lambda p: sums.at[t], sums.at[t], s_tp, r_tp)
     arrive(TP, lambda p: sums.at[p], s_tp, r_tp)
 
-    def gradients(k, carry):
-        gain_sum, skip_sum = carry
+    both = sums[0]
+    for p in range(1, ntp):
+        both = both + sums[p]
+    totc[...] = jnp.concatenate([both, jnp.zeros((120, L), F32)], axis=0).T
+
+    def token_scales(k):
+        both = totc[...]
+        square = jnp.sum(jnp.where(lane == 2 * k, both, 0.0), axis=1, keepdims=True)
+        inner = jnp.sum(jnp.where(lane == 2 * k + 1, both, 0.0), axis=1, keepdims=True)
+        return lax.rsqrt(square / total_width + 1e-05), inner
+
+    def gradients(k, _):
         rows = at_chunk(k)
-        both = sums[0, k]
-        for p in range(1, ntp):
-            both = both + sums[p, k]
-        both = jnp.concatenate([both, jnp.zeros((120, L), F32)], axis=0).T
-        scale = lax.rsqrt(both[:, 0:1] / total_width + 1e-05)
-        inner = both[:, 1:2]
-        mixed = mixb[rows, :]
-        grad_v = gvb[rows, :]
+        scale, inner = token_scales(k)
         gate = gate_v[rows, :].astype(F32)
-        sigma = jax.nn.sigmoid(gate)
-        grad_mixed = scale * (grad_v * gain_row) - mixed * (
+        grad_mixed = scale * (gvb[rows, :] * gain_row) - mixb[rows, :] * (
             (scale * scale * scale) * inner / total_width
         )
-        ggate[rows, :] = (
-            grad_mixed * yb[rows, :] * sigma * (1.0 + gate * (1.0 - sigma))
-        ).astype(BF16)
-        grad_y = grad_mixed * gate * sigma
+        grad_y = grad_mixed * gate * jax.nn.sigmoid(gate)
         dyb[rows, :] = grad_y
-        gain_sum = gain_sum + jnp.sum(grad_v * mixed * scale, axis=0, keepdims=True)
-        skip_sum = skip_sum + jnp.sum(
-            grad_y * xb[rows, :].astype(F32), axis=0, keepdims=True
-        )
         scaled = grad_y * startb[rows, :]
         hcb[k] = sum(dot(c_ref[rows, :], part, 0, 0) for part in pieces(scaled, 2))
-        normed[rows, :] = (mixed * scale * gain_row).astype(BF16)
-        return gain_sum, skip_sum
-
-    zero_row = jnp.zeros((1, width), F32)
-    gain_sum, skip_sum = lax.fori_loop(0, chunks, gradients, (zero_row, zero_row))
+        return 0
+
+    lax.fori_loop(0, chunks, gradients, 0)
     run = hcb[chunks - 1]
     for k in range(chunks - 2, -1, -1):
         run = totb[k] * run + hcb[k]
     rloc[...] = run.astype(BF16)
     exchange_1(rloc, lb2, s_h1, r_h1)
+
+    def gate_gradients(k, carry):
+        gain_sum, skip_sum = carry
+        rows = at_chunk(k)
+        scale, inner = token_scales(k)
+        mixed = mixb[rows, :]
+        grad_v = gvb[rows, :]
+        gate = gate_v[rows, :].astype(F32)
+        sigma = jax.nn.sigmoid(gate)
+        scaled_mixed = mixed * scale
+        normed[rows, :] = (scaled_mixed * gain_row).astype(BF16)
+        grad_mixed = scale * (grad_v * gain_row) - mixed * (
+            (scale * scale * scale) * inner / total_width
+        )
+        ggate[rows, :] = (
+            grad_mixed * yb[rows, :] * sigma * (1.0 + gate * (1.0 - sigma))
+        ).astype(BF16)
+        gain_sum = gain_sum + jnp.sum(grad_v * scaled_mixed, axis=0, keepdims=True)
+        skip_sum = skip_sum + jnp.sum(
+            dyb[rows, :] * xb[rows, :].astype(F32), axis=0, keepdims=True
+        )
+        return gain_sum, skip_sum
+
+    zero_row = jnp.zeros((1, width), F32)
+    gain_sum, skip_sum = lax.fori_loop(0, chunks, gate_gradients, (zero_row, zero_row))
     gx[x, 0:1, :] = gain_sum
     gx[x, 1:2, :] = skip_sum
     send(X, lambda p: gx.at[x], gx.at[x], s_gx, r_gx)
@@ -478,18 +496,48 @@
         if nx == 4:
             weight_copy(2, i, near).wait_recv()
             out = out + xc[i - 1].astype(F32)
+        away = i % nz
+        if away < middle:
+            ring_copy(away + 1, True).wait_recv()
+            out = add_part(out, away + 1, True)
+        if i > middle:
+            ring_copy(i - 1, False).wait_recv()
+            out = add_part(out, i - 1, False)
+        if i == nz:
+            gow[...] = out
+            return
         zs[i - 1] = out.astype(BF16)
-        if i < nz:
-            copy = rcopy(zs.at[i - 1], zr.at[i - 1], s_rz.at[i - 1], r_rz.at[i - 1], dev_z(block_of(i)))
-            copy.start()
-            pending.append(copy)
-
-    def weight_finish():
-        out = zs[nz - 1].astype(F32)
-        for i in steps[:-1]:
-            rcopy(zs.at[i - 1], zr.at[i - 1], s_rz.at[i - 1], r_rz.at[i - 1], dev_z(block_of(i))).wait_recv()
-            out = out + zr[i - 1].astype(F32)
-        gow[...] = out
+        for up in (True, False):
+            if i == middle or (i < middle) == up:
+                copy = ring_copy(i, up)
+                copy.start()
+                pending.append(copy)
+
+    middle = nz // 2
+    cut = 16 * (3 * columns // 80)
+
+    def ring_rows(i, up):
+        return (0, columns) if i != middle else (0, cut) if up else (cut, columns)
+
+    def ring_copy(i, up):
+        first, end = ring_rows(i, up)
+        slot = i - 1 if i != middle or up else nz - 1
+        return rcopy(
+            zs.at[i - 1, pl.ds(first, end - first)],
+            zr.at[i - 1, pl.ds(first, end - first)],
+            s_rz.at[slot],
+            r_rz.at[slot],
+            dev_z(lax.rem(z + (1 if up else nz - 1), nz)),
+        )
+
+    def add_part(out, i, up):
+        first, end = ring_rows(i, up)
+        part = zr[i - 1, first:end, :].astype(F32)
+        parts = [out[:first]] if first else []
+        parts.append(out[first:end] + part)
+        if end < columns:
+            parts.append(out[end:])
+        return jnp.concatenate(parts, axis=0) if len(parts) > 1 else parts[0]
 
     early = steps[: (3 * nz) // 8]
     later = steps[(3 * nz) // 8 :]
@@ -536,10 +584,14 @@
         return 0
 
     lax.fori_loop(0, chunks // 2, inside_back, 0)
+    for i in early[:1]:
+        weight_relay(i)
     exchange_3(ub2, qs2, qb2, s_h2, r_h2, s_h3, r_h3, True)
     lax.fori_loop(chunks // 2, chunks, inside_back, 0)
-    for i in early[:-1]:
+    for i in early[1:]:
         weight_relay(i)
+    for i in early[:1]:
+        weight_rows(i)
     exchange_4(qb2, lb2, vs2, h_in, s_h3, r_h3, s_h4, r_h4, True)
 
     share = tokens // ntp
@@ -567,11 +619,11 @@
         for p in range(ntp):
             out_ref[p * share : (p + 1) * share, :] = redo[which, p]
 
-    reduce_1(accr, 0, s_c1, r_c1)
-    for i in early[-1:]:
-        weight_relay(i)
     for i in later:
         weight_block(i)
+    reduce_1(accr, 0, s_c1, r_c1)
+    for i in early[1:]:
+        weight_rows(i)
     exchange_5(h_in, s_h4, r_h4)
 
     def states_back(i, run):
@@ -585,6 +637,9 @@
 
     lax.fori_loop(0, chunks, states_back, h_in[...].astype(F32))
     reduce_1(accw, 1, s_w1, r_w1)
+    for i in later[:1]:
+        weight_relay(i)
+
     def finish(k, _):
         rows = at_chunk(k)
         grad_y = dyb[rows, :]
@@ -602,34 +657,35 @@
         sumd[k, 0:SLOT, :] = whole.T
         return 0
 
-    lax.fori_loop(0, chunks, finish, 0)
+    lax.fori_loop(0, chunks // 2, finish, 0)
+    for i in later[1:2]:
+        weight_relay(i)
+    lax.fori_loop(chunks // 2, chunks, finish, 0)
     for k in range(chunks):
         gdecay[:, k * L : (k + 1) * L] = sumd[k, 0:heads, :]
-    for i in later[:2]:
+    for i in later[:1]:
+        weight_rows(i)
+    for i in later[2:3]:
         weight_relay(i)
     reduce_2(0, s_c1, r_c1, s_c2, r_c2)
     reduce_2(1, s_w1, r_w1, s_w2, r_w2)
-    for i in early:
+    for i in later[3:4]:
+        weight_relay(i)
+    for i in later[1:2]:
         weight_rows(i)
-    for i in later[2:3]:
-        weight_relay(i)
     arrive(Z, lambda p: gz.at[p], s_gz, r_gz)
     row = gz[0]
     for k in range(1, nz):
         row = row + gz[k]
     ggain[...] = row[0:1]
     gskip[...] = head_sums(jnp.concatenate([row, jnp.zeros((6, width), F32)], axis=0))[1:2, 0:heads]
-    for i in later[3:4]:
-        weight_relay(i)
-    for i in later[:2]:
-        weight_rows(i)
     for i in later[4:]:
         weight_relay(i)
-    for i in later[2:]:
+    for i in later[2:-1]:
         weight_rows(i)
     reduce_3(gread, 0, s_c2, r_c2)
     reduce_3(gwrite, 1, s_w2, r_w2)
-    weight_finish()
+    weight_rows(nz)
     for copy in pending:
         copy.wait_send()
 
@@ -737,7 +793,8 @@
         pltpu.VMEM((qrows, width), F32),
         pltpu.VMEM((nx, 1, width), F32),
         pltpu.VMEM((nz, 1, width), F32),
-        pltpu.VMEM((ntp, chunks, 8, L), F32),
+        pltpu.VMEM((ntp, 8, L), F32),
+        pltpu.VMEM((L, 128), F32),
         pltpu.VMEM((nx, 2, width), F32),
         pltpu.VMEM((nz, 2, width), F32),
         pltpu.VMEM((nz, shard, width), BF16),

time: 97.5 us -> 87.5 us (0.90)
  the two profiles are of different devices: /device:TPU:1 before, /device:TPU:32 now
where the time goes in v3:
time: 87.5 us; the launch traced here: 87.4 us
  Pallas kernels  86.7 us (99%)
    pallas_call x1, Pallas kernels, on_device(): pl.pallas_call(functools.partial(core, nx, nz, ntp), out_shape=(jax.Shape...  83 us
    pallas_call x1, Pallas kernels, hand_out(): pl.pallas_call(copy_out, out_shape=shapes, in_specs=specs, out_specs=spec...  3.74 us

profile of v3, /device:TPU:32, one launch (start us, length us, event | category | flops | bytes accessed | tf_op | source)
XLA Modules:
  0.0 87.4 jit_solution(3775185820030810072)
XLA Ops:
  0.6 83.0 %layer_backward.1 = (bf16[512,640]{1,0:T(8,128)(2,1)}, bf16[512,640]{1,0:T(8,128)(2,1)}, f32[512,128]{1,0:T(8,128)}, f32[512,128]{1,0:T(8,128)}, f32[10,512]{1,0...) custom-call(s32[64,640]{1,0:T(8,128)} %packed.1, s32[5,512]{1,0:T(8,128)} %expo.1, ...), custom_call_target="tpu_custom_call" | custom-call | tf_op jit(solution)/shard_map/layer_backward/pallas_call | solution.py:821
  83.6 3.7 %hand_out.1 = (bf16[512,640]{1,0:T(8,128)(2,1)}, bf16[512,640]{1,0:T(8,128)(2,1)}, f32[512,128]{1,0:T(8,128)}, f32[512,128]{1,0:T(8,128)}, f32[10,512]{1,0:T(8,1...) custom-call(bf16[512,640]{1,0:T(8,128)(2,1)} %get-tuple-element.24.refs_0_, ...), custom_call_target="tpu_custom_call" | custom-call | tf_op jit(solution)/shard_map/hand_out/pallas_call | solution.py:729

commit v4 on v3

--- a/solution.py
+++ b/solution.py
@@ -14,6 +14,7 @@
 L = 128
 HEAD = 64
 SLOT = 16
+FRONT = 384
 
 
 def dot(a, b, ca=1, cb=0, precision=None):
@@ -47,11 +48,11 @@
      normed, csr, csc, totb, dec, cross, gb, stb, hcb, hst, sumd, segr, segc, dxi,
      sloc, lb, tb, ub, qs, qb, vs, s_in,
      rloc, lb2, tb2, ub2, qs2, qb2, vs2, h_in,
-     vtop, dxs, dzs, sums, totc, gx, gz, pw, xa, xd, xm, xc, zs, zr, accw, accr, red, redo,
+     vtop, dxs, dzs, sums, totc, gx, gz, pwa, pwb, xa, xd, xm, xc, zsa, zra, zsb, zrb, xsb, xrb, accw, accr, red, redo,
      cp_sem, s_ag, r_ag, s_dx, r_dx, s_dz, r_dz,
      s_p1, r_p1, s_p2, r_p2, s_p3, r_p3, s_p4, r_p4,
      s_h1, r_h1, s_h2, r_h2, s_h3, r_h3, s_h4, r_h4,
-     s_tp, r_tp, s_gx, r_gx, s_gz, r_gz, s_rx, r_rx, s_rz, r_rz,
+     s_tp, r_tp, s_gx, r_gx, s_gz, r_gz, s_rx, r_rx, s_za, r_za, s_zb, r_zb, s_xb, r_xb,
      s_w1, r_w1, s_w2, r_w2, s_c1, r_c1, s_c2, r_c2) = scratch
     tokens, width = xb.shape
     chunks = tokens // L
@@ -291,13 +292,6 @@
         arrive(X, lambda p: result.at[pl.ds(pl.multiple_of(p * qrows, qrows), qrows)], s4, r4)
 
     exchange_1(sloc, lb, s_p1, r_p1)
-
-    arrive(X, lambda p: dxs.at[p], s_dx, r_dx)
-    row = dxs[0]
-    for k in range(1, nx):
-        row = row * dxs[k]
-    dzs[z] = row
-    send(Z, lambda p: dzs.at[z], dzs.at[z], s_dz, r_dz)
 
     skip_row = jnp.zeros((1, width), F32)
     head_of = iota((1, width), 1) // HEAD
@@ -336,6 +330,13 @@
     load_w.wait()
     cot_wait(0, sibling)
     project(y, True)
+    arrive(X, lambda p: dxs.at[p], s_dx, r_dx)
+    row = dxs[0]
+    for k in range(1, nx):
+        row = row * dxs[k]
+    dzs[z] = row
+    send(Z, lambda p: dzs.at[z], dzs.at[z], s_dz, r_dz)
+
     exchange_2(lb, tb, ub, s_p1, r_p1, s_p2, r_p2, False)
     relay_cot()
     lax.fori_loop(chunks // 2, chunks, inside, 0)
@@ -449,13 +450,15 @@
     send(X, lambda p: gx.at[x], gx.at[x], s_gx, r_gx)
 
     columns = shard // nx
+    front = pwa.shape[2]
+    middle = nz // 2
     steps = sorted(range(1, nz), key=lambda i: -min(i, nz - i)) + [nz]
 
     def block_of(i):
         return lax.rem(z + i, nz)
 
     def mine_of(i, p):
-        return pw.at[block_of(i), pl.ds(pl.multiple_of(p * columns, columns), columns)]
+        return pwa.at[block_of(i), pl.ds(pl.multiple_of(p * columns, columns), columns)]
 
     def sides(i):
         one, two = lax.rem(x + 1, nx), lax.rem(x + nx - 1, nx)
@@ -473,7 +476,9 @@
 
     def weight_block(i):
         k = block_of(i)
-        pw[k] = dot(cot[pl.ds(pl.multiple_of(k * shard, shard), shard), :], normed[...]).astype(BF16)
+        terms = dot(cot[pl.ds(pl.multiple_of(k * shard, shard), shard), :], normed[...]).astype(BF16)
+        pwa[k] = terms[:, :front]
+        pwb[k] = terms[:, front:]
         near, far = sides(i)
         if nx == 4:
             weight_send(0, i, near)
@@ -486,6 +491,47 @@
             weight_copy(0, i, near).wait_recv()
             xm[i - 1] = (xa[i - 1].astype(F32) + mine_of(i, near)[...].astype(F32)).astype(BF16)
             weight_send(2, i, near)
+
+    def ring_part(kind, i, up):
+        rows = (columns, shard)[kind]
+        cut = 16 * (3 * rows // 80)
+        return (0, rows) if i != middle else (0, cut) if up else (cut, rows)
+
+    def ring_copy(kind, i, up):
+        first, end = ring_part(kind, i, up)
+        slot = i - 1 if i != middle or up else nz - 1
+        sends, lands, s_z, r_z = ((zsa, zra, s_za, r_za), (zsb, zrb, s_zb, r_zb))[kind]
+        return rcopy(
+            sends.at[i - 1, pl.ds(first, end - first)],
+            lands.at[i - 1, pl.ds(first, end - first)],
+            s_z.at[slot],
+            r_z.at[slot],
+            dev_z(lax.rem(z + (1 if up else nz - 1), nz)),
+        )
+
+    def ring_add(kind, out, i, up):
+        ring_copy(kind, i, up).wait_recv()
+        first, end = ring_part(kind, i, up)
+        part = (zra, zrb)[kind][i - 1, first:end, :].astype(F32)
+        parts = [out[:first]] if first else []
+        parts.append(out[first:end] + part)
+        if end < out.shape[0]:
+            parts.append(out[end:])
+        return jnp.concatenate(parts, axis=0) if len(parts) > 1 else parts[0]
+
+    def ring_step(kind, i, out):
+        if i % nz < middle:
+            out = ring_add(kind, out, i % nz + 1, True)
+        if i > middle:
+            out = ring_add(kind, out, i - 1, False)
+        if i < nz:
+            (zsa, zsb)[kind][i - 1] = out.astype(BF16)
+            for up in (True, False):
+                if i == middle or (i < middle) == up:
+                    copy = ring_copy(kind, i, up)
+                    copy.start()
+                    pending.append(copy)
+        return out
 
     def weight_rows(i):
         near, far = sides(i)
@@ -496,53 +542,39 @@
         if nx == 4:
             weight_copy(2, i, near).wait_recv()
             out = out + xc[i - 1].astype(F32)
-        away = i % nz
-        if away < middle:
-            ring_copy(away + 1, True).wait_recv()
-            out = add_part(out, away + 1, True)
-        if i > middle:
-            ring_copy(i - 1, False).wait_recv()
-            out = add_part(out, i - 1, False)
+        out = ring_step(0, i, out)
         if i == nz:
-            gow[...] = out
-            return
-        zs[i - 1] = out.astype(BF16)
-        for up in (True, False):
-            if i == middle or (i < middle) == up:
-                copy = ring_copy(i, up)
-                copy.start()
-                pending.append(copy)
-
-    middle = nz // 2
-    cut = 16 * (3 * columns // 80)
-
-    def ring_rows(i, up):
-        return (0, columns) if i != middle else (0, cut) if up else (cut, columns)
-
-    def ring_copy(i, up):
-        first, end = ring_rows(i, up)
-        slot = i - 1 if i != middle or up else nz - 1
-        return rcopy(
-            zs.at[i - 1, pl.ds(first, end - first)],
-            zr.at[i - 1, pl.ds(first, end - first)],
-            s_rz.at[slot],
-            r_rz.at[slot],
-            dev_z(lax.rem(z + (1 if up else nz - 1), nz)),
-        )
-
-    def add_part(out, i, up):
-        first, end = ring_rows(i, up)
-        part = zr[i - 1, first:end, :].astype(F32)
-        parts = [out[:first]] if first else []
-        parts.append(out[first:end] + part)
-        if end < columns:
-            parts.append(out[end:])
-        return jnp.concatenate(parts, axis=0) if len(parts) > 1 else parts[0]
-
-    early = steps[: (3 * nz) // 8]
-    later = steps[(3 * nz) // 8 :]
-    for i in early:
+            gow[:, :front] = out
+
+    def back_rows(i):
+        out = ring_step(1, i, pwb[block_of(i)].astype(F32))
+        if i == nz:
+            for p in range(nx):
+                xsb[p] = out[p * columns : (p + 1) * columns, :].astype(BF16)
+            send(X, lambda p: xsb.at[p], xrb.at[x], s_xb, r_xb)
+            xrb[x] = xsb[x]
+
+    def back_finish():
+        arrive(X, lambda p: xrb.at[p], s_xb, r_xb)
+        out = xrb[0].astype(F32)
+        for p in range(1, nx):
+            out = out + xrb[p].astype(F32)
+        gow[:, front:] = out
+
+    early = steps[: (5 * nz) // 8]
+    later = steps[(5 * nz) // 8 :]
+    order = iter(steps)
+
+    def back_steps(count):
+        for _ in range(count):
+            i = next(order, None)
+            if i is not None:
+                back_rows(i)
+
+    for n, i in enumerate(early):
         weight_block(i)
+        if n == 0:
+            back_steps(1)
     exchange_2(lb2, tb2, ub2, s_h1, r_h1, s_h2, r_h2, True)
     arrive(X, lambda p: gx.at[p], s_gx, r_gx)
     row = gx[0]
@@ -586,9 +618,10 @@
     lax.fori_loop(0, chunks // 2, inside_back, 0)
     for i in early[:1]:
         weight_relay(i)
+    back_steps(2 if nz == 8 else 0)
     exchange_3(ub2, qs2, qb2, s_h2, r_h2, s_h3, r_h3, True)
     lax.fori_loop(chunks // 2, chunks, inside_back, 0)
-    for i in early[1:]:
+    for i in early[1:3]:
         weight_relay(i)
     for i in early[:1]:
         weight_rows(i)
@@ -622,8 +655,11 @@
     for i in later:
         weight_block(i)
     reduce_1(accr, 0, s_c1, r_c1)
-    for i in early[1:]:
+    for i in early[3:4]:
+        weight_relay(i)
+    for i in early[1:3]:
         weight_rows(i)
+    back_steps(2 if nz == 8 else 0)
     exchange_5(h_in, s_h4, r_h4)
 
     def states_back(i, run):
@@ -637,7 +673,7 @@
 
     lax.fori_loop(0, chunks, states_back, h_in[...].astype(F32))
     reduce_1(accw, 1, s_w1, r_w1)
-    for i in later[:1]:
+    for i in early[4:]:
         weight_relay(i)
 
     def finish(k, _):
@@ -658,34 +694,35 @@
         return 0
 
     lax.fori_loop(0, chunks // 2, finish, 0)
-    for i in later[1:2]:
+    for i in later[:1]:
         weight_relay(i)
+    for i in early[3:4]:
+        weight_rows(i)
+    back_steps(2 if nz == 8 else 0)
     lax.fori_loop(chunks // 2, chunks, finish, 0)
     for k in range(chunks):
         gdecay[:, k * L : (k + 1) * L] = sumd[k, 0:heads, :]
-    for i in later[:1]:
+    for i in later[1:2]:
+        weight_relay(i)
+    for i in early[4:]:
         weight_rows(i)
-    for i in later[2:3]:
-        weight_relay(i)
     reduce_2(0, s_c1, r_c1, s_c2, r_c2)
     reduce_2(1, s_w1, r_w1, s_w2, r_w2)
-    for i in later[3:4]:
+    for i in later[2:]:
         weight_relay(i)
-    for i in later[1:2]:
-        weight_rows(i)
     arrive(Z, lambda p: gz.at[p], s_gz, r_gz)
     row = gz[0]
     for k in range(1, nz):
         row = row + gz[k]
     ggain[...] = row[0:1]
     gskip[...] = head_sums(jnp.concatenate([row, jnp.zeros((6, width), F32)], axis=0))[1:2, 0:heads]
-    for i in later[4:]:
-        weight_relay(i)
-    for i in later[2:-1]:
+    back_steps(nz)
+    for i in later[:-1]:
         weight_rows(i)
     reduce_3(gread, 0, s_c2, r_c2)
     reduce_3(gwrite, 1, s_w2, r_w2)
     weight_rows(nz)
+    back_finish()
     for copy in pending:
         copy.wait_send()
 
@@ -749,6 +786,7 @@
     columns = model // (nx * nz)
     qrows, erows = n // nx, n // (nx * nz)
     share = tokens // ntp
+    front = FRONT
 
     def wide(kind=F32):
         return pltpu.VMEM((tokens, width), kind)
@@ -797,8 +835,11 @@
         pltpu.VMEM((L, 128), F32),
         pltpu.VMEM((nx, 2, width), F32),
         pltpu.VMEM((nz, 2, width), F32),
-        pltpu.VMEM((nz, shard, width), BF16),
-        *[pltpu.VMEM((nz, columns, width), BF16) for _ in range(6)],
+        pltpu.VMEM((nz, shard, front), BF16),
+        pltpu.VMEM((nz, shard, width - front), BF16),
+        *[pltpu.VMEM((nz, columns, front), BF16) for _ in range(6)],
+        *[pltpu.VMEM((nz, shard, width - front), BF16) for _ in range(2)],
+        *[pltpu.VMEM((nx, columns, width - front), BF16) for _ in range(2)],
         pltpu.VMEM((tokens, n), F32),
         pltpu.VMEM((tokens, n), F32),
         pltpu.VMEM((2, ntp, share, n), F32),
@@ -814,6 +855,8 @@
         *sems(nz),
         *sems(3, nz),
         *sems(nz),
+        *sems(nz),
+        *sems(nx),
         *(sems(ntp) * 4),
     ]
     vmem = pl.BlockSpec(memory_space=pltpu.VMEM)

time: 87.5 us -> 82.9 us (0.947)
  the two profiles are of different devices: /device:TPU:32 before, /device:TPU:1 now
where the time goes in v4:
time: 82.9 us; the launch traced here: 82.7 us
  Pallas kernels  82.1 us (99%)
    pallas_call x1, Pallas kernels, on_device(): pl.pallas_call(functools.partial(core, nx, nz, ntp), out_shape=(jax.Shape...  78.3 us
    pallas_call x1, Pallas kernels, hand_out(): pl.pallas_call(copy_out, out_shape=shapes, in_specs=specs, out_specs=spec...  3.74 us

profile of v4, /device:TPU:1, one launch (start us, length us, event | category | flops | bytes accessed | tf_op | source)
XLA Modules:
  0.0 82.7 jit_solution(5371687026932188864)
XLA Ops:
  0.6 78.3 %layer_backward.1 = (bf16[512,640]{1,0:T(8,128)(2,1)}, bf16[512,640]{1,0:T(8,128)(2,1)}, f32[512,128]{1,0:T(8,128)}, f32[512,128]{1,0:T(8,128)}, f32[10,512]{1,0...) custom-call(s32[64,640]{1,0:T(8,128)} %packed.1, s32[5,512]{1,0:T(8,128)} %expo.1, ...), custom_call_target="tpu_custom_call" | custom-call | tf_op jit(solution)/shard_map/layer_backward/pallas_call | solution.py:864
  79.0 3.7 %hand_out.1 = (bf16[512,640]{1,0:T(8,128)(2,1)}, bf16[512,640]{1,0:T(8,128)(2,1)}, f32[512,128]{1,0:T(8,128)}, f32[512,128]{1,0:T(8,128)}, f32[10,512]{1,0:T(8,1...) custom-call(bf16[512,640]{1,0:T(8,128)(2,1)} %get-tuple-element.24.refs_0_, ...), custom_call_target="tpu_custom_call" | custom-call | tf_op jit(solution)/shard_map/hand_out/pallas_call | solution.py:766

commit v5 on v4

--- a/solution.py
+++ b/solution.py
@@ -45,7 +45,7 @@
 def core(nx, nz, ntp, packed, expo, gate_hbm, b_ref, c_ref, ld_ref, skip_ref, gain_ref, w_hbm, cot_hbm,
          gin, ggate, gwrite, gread, gdecay, gskip, ggain, gow, *scratch):
     (gate_v, w_v, cot, xb, yb, gvb, mixb, dyb, rsb, endb, startb,
-     normed, csr, csc, totb, dec, cross, gb, stb, hcb, hst, sumd, segr, segc, dxi,
+     normed, act, gvg, xe, accp, csr, csc, totb, dec, cross, gb, stb, hcb, hst, sumd, segr, segc, dxi,
      sloc, lb, tb, ub, qs, qb, vs, s_in,
      rloc, lb2, tb2, ub2, qs2, qb2, vs2, h_in,
      vtop, dxs, dzs, sums, totc, gx, gz, pwa, pwb, xa, xd, xm, xc, zsa, zra, zsb, zrb, xsb, xrb, accw, accr, red, redo,
@@ -79,19 +79,21 @@
     X, Z, TP = (nx, x, dev_x), (nz, z, dev_z), (ntp, t, dev_t)
     pending = []
 
-    def send(group, src_of, dst, ssem, rsem):
+    def send(group, src_of, dst, whole, ssem, rsem):
         n, me, dev = group
         for d in range(1, n):
             p = lax.rem(me + d, n)
-            copy = rcopy(src_of(p), dst, ssem.at[d], rsem.at[me], dev(p))
-            copy.start()
-            pending.append(copy)
-
-    def arrive(group, dst_of, ssem, rsem):
+            rcopy(src_of(p), dst, ssem.at[0], rsem.at[0], dev(p)).start()
+        if n > 1:
+            pending.append(rcopy(whole, whole, ssem.at[0], rsem.at[0], dev(me)))
+
+    def arrive(group, whole, ssem, rsem):
         n, me, dev = group
-        for d in range(1, n):
-            p = lax.rem(me + d, n)
-            rcopy(dst_of(p), dst_of(p), ssem.at[d], rsem.at[p], dev(p)).wait_recv()
+        if n > 1:
+            rcopy(whole, whole, ssem.at[0], rsem.at[0], dev(me)).wait_recv()
+
+    def slots(ref, n):
+        return ref.at[pl.ds(0, n - 1)]
 
     def cot_rows(p, first=0, count=shard):
         return cot.at[pl.ds(pl.multiple_of(p * shard + first, 16), count)]
@@ -171,12 +173,29 @@
     for k in range(chunks):
         rows = slice(k * L, (k + 1) * L)
         weighted = xb[rows, :].astype(F32) * endb[rows, :]
-        gb[k] = sum(dot(b_ref[rows, :], part, 0, 0) for part in pieces(weighted, 2))
+        parts = pieces(weighted, 2)
+        xe[rows, :] = parts[0]
+        gb[k] = sum(dot(b_ref[rows, :], part, 0, 0) for part in parts)
         run = totb[k] * run + gb[k]
     sloc[...] = run
 
+    def take_rows(ref, at, count):
+        return ref[pl.ds(pl.multiple_of(at * count, count), count), :]
+
+    def exchange_1(own, lbuf, ssem, rsem):
+        send(
+            X,
+            lambda p: own.at[pl.ds(pl.multiple_of(p * qrows, qrows), qrows)],
+            lbuf.at[x],
+            slots(lbuf, nx),
+            ssem,
+            rsem,
+        )
+        lbuf[x] = take_rows(own, x, qrows)
+
     pl.semaphore_wait(barrier, (nx - 1) + (nz - 1) + (ntp - 1))
-    send(X, lambda p: dxs.at[x], dxs.at[x], s_dx, r_dx)
+    send(X, lambda p: dxs.at[x], dxs.at[x], slots(dxs, nx), s_dx, r_dx)
+    exchange_1(sloc, lb, s_p1, r_p1)
 
     load_cot.wait()
     part = shard // 2
@@ -185,48 +204,46 @@
     before = 2 * lax.rem(y + ny - 1, ny) + half
     across = 2 * lax.rem(y + 2, ny) + half
 
-    def cot_copy(i, j, p, to, first=0, count=shard):
-        return rcopy(cot_rows(p, first, count), cot_rows(p, first, count), s_ag.at[i], r_ag.at[j], dev_t(to))
-
-    def cot_send(i, j, p, to, *rows):
-        copy = cot_copy(i, j, p, to, *rows)
-        copy.start()
-        pending.append(copy)
+    def cot_copy(j, p, to, first=0, count=shard):
+        return rcopy(cot_rows(p, first, count), cot_rows(p, first, count), s_ag.at[0], r_ag.at[j], dev_t(to))
+
+    def cot_send(j, p, to, *rows):
+        cot_copy(j, p, to, *rows).start()
 
     def cot_wait(j, p, *rows):
-        cot_copy(0, j, p, sibling, *rows).wait_recv()
-
-    cot_send(0, 0, t, sibling)
+        cot_copy(j, p, sibling, *rows).wait_recv()
+
+    cot_send(0, t, sibling)
     if ny == 2:
-        cot_send(1, 1, t, after)
+        cot_send(1, t, after)
     elif ny == 4:
-        cot_send(1, 1, t, after, 0, part)
-        cot_send(2, 3, t, before, part, part)
-        cot_send(3, 2, t, after, part, part)
-        cot_send(4, 4, t, before, 0, part)
+        cot_send(1, t, after, 0, part)
+        cot_send(3, t, before, part, part)
+        cot_send(2, t, after, part, part)
+        cot_send(4, t, before, 0, part)
 
     def relay_cot():
         if ny == 4:
             cot_wait(1, before, 0, part)
-            cot_send(5, 5, before, after, 0, part)
+            cot_send(5, before, after, 0, part)
             cot_wait(3, after, part, part)
-            cot_send(6, 6, after, before, part, part)
+            cot_send(6, after, before, part, part)
 
     def near_cot():
         if ny == 2:
             cot_wait(1, after)
-            cot_send(2, 7, after, sibling)
+            cot_send(7, after, sibling)
         elif ny == 4:
             cot_wait(2, before, part, part)
-            cot_send(7, 7, before, sibling)
+            cot_send(7, before, sibling)
             cot_wait(4, after, 0, part)
-            cot_send(8, 8, after, sibling)
+            cot_send(8, after, sibling)
 
     def far_cot():
         if ny == 4:
             cot_wait(5, across, 0, part)
             cot_wait(6, across, part, part)
-            cot_send(9, 9, across, sibling)
+            cot_send(9, across, sibling)
 
     def project(chip, first=False):
         terms = dot(
@@ -240,21 +257,8 @@
     def other(p):
         return p + 1 - 2 * half
 
-    def take_rows(ref, at, count):
-        return ref[pl.ds(pl.multiple_of(at * count, count), count), :]
-
-    def exchange_1(own, lbuf, ssem, rsem):
-        send(
-            X,
-            lambda p: own.at[pl.ds(pl.multiple_of(p * qrows, qrows), qrows)],
-            lbuf.at[x],
-            ssem,
-            rsem,
-        )
-        lbuf[x] = take_rows(own, x, qrows)
-
     def exchange_2(lbuf, tbuf, ubuf, s1, r1, ssem, rsem, backward):
-        arrive(X, lambda p: lbuf.at[p], s1, r1)
+        arrive(X, slots(lbuf, nx), s1, r1)
         order = range(nx - 1, -1, -1) if backward else range(nx)
         row = None
         for k in order:
@@ -262,21 +266,21 @@
             row = add if row is None else dxs[k] * row + add
         for k in range(nz):
             tbuf[k] = row[k * erows : (k + 1) * erows, :]
-        send(Z, lambda p: tbuf.at[p], ubuf.at[z], ssem, rsem)
+        send(Z, lambda p: tbuf.at[p], ubuf.at[z], slots(ubuf, nz), ssem, rsem)
         ubuf[z] = tbuf[z]
 
     def exchange_3(ubuf, qsend, qbuf, s2, r2, ssem, rsem, backward):
-        arrive(Z, lambda p: ubuf.at[p], s2, r2)
+        arrive(Z, slots(ubuf, nz), s2, r2)
         order = range(nz - 1, -1, -1) if backward else range(nz)
         row = jnp.zeros((erows, width), F32)
         for k in order:
             qsend[k] = row
             row = dzs[k] * row + ubuf[k]
-        send(Z, lambda p: qsend.at[p], qbuf.at[z], ssem, rsem)
+        send(Z, lambda p: qsend.at[p], qbuf.at[z], slots(qbuf, nz), ssem, rsem)
         qbuf[z] = qsend[z]
 
     def exchange_4(qbuf, lbuf, vsend, result, s3, r3, ssem, rsem, backward):
-        arrive(Z, lambda p: qbuf.at[p], s3, r3)
+        arrive(Z, slots(qbuf, nz), s3, r3)
         for k in range(nz):
             vtop[k * erows : (k + 1) * erows, :] = qbuf[k]
         order = range(nx - 1, -1, -1) if backward else range(nx)
@@ -285,13 +289,12 @@
             vsend[k] = row.astype(vsend.dtype)
             row = dxs[k] * row + lbuf[k].astype(F32)
         mine = result.at[pl.ds(pl.multiple_of(x * qrows, qrows), qrows)]
-        send(X, lambda p: vsend.at[p], mine, ssem, rsem)
+        send(X, lambda p: vsend.at[p], mine, result.at[pl.ds(0, (nx - 1) * qrows)], ssem, rsem)
         result[pl.ds(pl.multiple_of(x * qrows, qrows), qrows), :] = vsend[x]
 
     def exchange_5(result, s4, r4):
-        arrive(X, lambda p: result.at[pl.ds(pl.multiple_of(p * qrows, qrows), qrows)], s4, r4)
-
-    exchange_1(sloc, lb, s_p1, r_p1)
+        arrive(X, result.at[pl.ds(0, (nx - 1) * qrows)], s4, r4)
+
 
     skip_row = jnp.zeros((1, width), F32)
     head_of = iota((1, width), 1) // HEAD
@@ -330,17 +333,17 @@
     load_w.wait()
     cot_wait(0, sibling)
     project(y, True)
-    arrive(X, lambda p: dxs.at[p], s_dx, r_dx)
+    arrive(X, slots(dxs, nx), s_dx, r_dx)
     row = dxs[0]
     for k in range(1, nx):
         row = row * dxs[k]
     dzs[z] = row
-    send(Z, lambda p: dzs.at[z], dzs.at[z], s_dz, r_dz)
+    send(Z, lambda p: dzs.at[z], dzs.at[z], slots(dzs, nz), s_dz, r_dz)
 
     exchange_2(lb, tb, ub, s_p1, r_p1, s_p2, r_p2, False)
     relay_cot()
     lax.fori_loop(chunks // 2, chunks, inside, 0)
-    arrive(Z, lambda p: dzs.at[p], s_dz, r_dz)
+    arrive(Z, slots(dzs, nz), s_dz, r_dz)
     exchange_3(ub, qs, qb, s_p2, r_p2, s_p3, r_p3, False)
     near_cot()
     exchange_4(qb, lb, vs, s_in, s_p3, r_p3, s_p4, r_p4, False)
@@ -354,41 +357,41 @@
         cot_wait(8, other(after))
         project(lax.rem(y + 1, ny))
     load_gate.wait()
+    if ny == 4:
+        cot_wait(9, other(across))
+        project(lax.rem(y + 2, ny))
+    gain_row = gain_ref[...].reshape(1, width)
+
+    def prepare(k, _):
+        rows = at_chunk(k)
+        gate = gate_v[rows, :].astype(F32)
+        act[rows, :] = gate * jax.nn.sigmoid(gate)
+        gvg[rows, :] = gvb[rows, :] * gain_row
+        return 0
+
+    lax.fori_loop(0, chunks, prepare, 0)
     exchange_5(s_in, s_p4, r_p4)
-    gain_row = gain_ref[...].reshape(1, width)
     stb[0] = s_in[...].astype(F32)
     for k in range(1, chunks):
         stb[k] = totb[k - 1] * stb[k - 1] + gb[k - 1]
-
-    def outputs_of(k, _):
+    lane = iota((L, 128), 1)
+
+    def sums_of(k, acc):
         rows = at_chunk(k)
         start = sum(dot(c_ref[rows, :], part) for part in pieces(stb[k], 2))
         rsb[rows, :] = start
         y_now = yb[rows, :] + startb[rows, :] * start
         yb[rows, :] = y_now
-        gate = gate_v[rows, :].astype(F32)
-        mixed = y_now * gate * jax.nn.sigmoid(gate)
+        mixed = y_now * act[rows, :]
         mixb[rows, :] = mixed
-        return 0
-
-    lax.fori_loop(0, chunks, outputs_of, 0)
-    if ny == 4:
-        cot_wait(9, other(across))
-        project(lax.rem(y + 2, ny))
-
-    lane = iota((L, 128), 1)
-
-    def sums_of(k, acc):
-        rows = at_chunk(k)
-        mixed = mixb[rows, :]
         square = jnp.sum(mixed * mixed, axis=1, keepdims=True)
-        inner = jnp.sum(gvb[rows, :] * gain_row * mixed, axis=1, keepdims=True)
+        inner = jnp.sum(gvg[rows, :] * mixed, axis=1, keepdims=True)
         return jnp.where(lane == 2 * k, square, jnp.where(lane == 2 * k + 1, inner, acc))
 
     packed_sums = lax.fori_loop(0, chunks, sums_of, jnp.zeros((L, 128), F32))
     sums[t] = packed_sums.T[0:8, :]
-    send(TP, lambda p: sums.at[t], sums.at[t], s_tp, r_tp)
-    arrive(TP, lambda p: sums.at[p], s_tp, r_tp)
+    send(TP, lambda p: sums.at[t], sums.at[t], slots(sums, ntp), s_tp, r_tp)
+    arrive(TP, slots(sums, ntp), s_tp, r_tp)
 
     both = sums[0]
     for p in range(1, ntp):
@@ -404,11 +407,10 @@
     def gradients(k, _):
         rows = at_chunk(k)
         scale, inner = token_scales(k)
-        gate = gate_v[rows, :].astype(F32)
-        grad_mixed = scale * (gvb[rows, :] * gain_row) - mixb[rows, :] * (
+        grad_mixed = scale * gvg[rows, :] - mixb[rows, :] * (
             (scale * scale * scale) * inner / total_width
         )
-        grad_y = grad_mixed * gate * jax.nn.sigmoid(gate)
+        grad_y = grad_mixed * act[rows, :]
         dyb[rows, :] = grad_y
         scaled = grad_y * startb[rows, :]
         hcb[k] = sum(dot(c_ref[rows, :], part, 0, 0) for part in pieces(scaled, 2))
@@ -426,18 +428,17 @@
         rows = at_chunk(k)
         scale, inner = token_scales(k)
         mixed = mixb[rows, :]
-        grad_v = gvb[rows, :]
         gate = gate_v[rows, :].astype(F32)
         sigma = jax.nn.sigmoid(gate)
         scaled_mixed = mixed * scale
         normed[rows, :] = (scaled_mixed * gain_row).astype(BF16)
-        grad_mixed = scale * (grad_v * gain_row) - mixed * (
+        grad_mixed = scale * gvg[rows, :] - mixed * (
             (scale * scale * scale) * inner / total_width
         )
         ggate[rows, :] = (
             grad_mixed * yb[rows, :] * sigma * (1.0 + gate * (1.0 - sigma))
         ).astype(BF16)
-        gain_sum = gain_sum + jnp.sum(grad_v * scaled_mixed, axis=0, keepdims=True)
+        gain_sum = gain_sum + jnp.sum(gvb[rows, :] * scaled_mixed, axis=0, keepdims=True)
         skip_sum = skip_sum + jnp.sum(
             dyb[rows, :] * xb[rows, :].astype(F32), axis=0, keepdims=True
         )
@@ -447,7 +448,7 @@
     gain_sum, skip_sum = lax.fori_loop(0, chunks, gate_gradients, (zero_row, zero_row))
     gx[x, 0:1, :] = gain_sum
     gx[x, 1:2, :] = skip_sum
-    send(X, lambda p: gx.at[x], gx.at[x], s_gx, r_gx)
+    send(X, lambda p: gx.at[x], gx.at[x], slots(gx, nx), s_gx, r_gx)
 
     columns = shard // nx
     front = pwa.shape[2]
@@ -467,12 +468,10 @@
     def weight_copy(kind, i, to):
         source = (mine_of(i, lax.rem(x + 2, nx)), mine_of(i, to), xm.at[i - 1])[kind]
         target = (xa, xd, xc)[kind].at[i - 1]
-        return rcopy(source, target, s_rx.at[kind, i - 1], r_rx.at[kind, i - 1], dev_x(to))
+        return rcopy(source, target, s_rx.at[kind], r_rx.at[kind, i - 1], dev_x(to))
 
     def weight_send(kind, i, to):
-        copy = weight_copy(kind, i, to)
-        copy.start()
-        pending.append(copy)
+        weight_copy(kind, i, to).start()
 
     def weight_block(i):
         k = block_of(i)
@@ -504,7 +503,7 @@
         return rcopy(
             sends.at[i - 1, pl.ds(first, end - first)],
             lands.at[i - 1, pl.ds(first, end - first)],
-            s_z.at[slot],
+            s_z.at[0],
             r_z.at[slot],
             dev_z(lax.rem(z + (1 if up else nz - 1), nz)),
         )
@@ -528,9 +527,7 @@
             (zsa, zsb)[kind][i - 1] = out.astype(BF16)
             for up in (True, False):
                 if i == middle or (i < middle) == up:
-                    copy = ring_copy(kind, i, up)
-                    copy.start()
-                    pending.append(copy)
+                    ring_copy(kind, i, up).start()
         return out
 
     def weight_rows(i):
@@ -551,18 +548,17 @@
         if i == nz:
             for p in range(nx):
                 xsb[p] = out[p * columns : (p + 1) * columns, :].astype(BF16)
-            send(X, lambda p: xsb.at[p], xrb.at[x], s_xb, r_xb)
+            send(X, lambda p: xsb.at[p], xrb.at[x], slots(xrb, nx), s_xb, r_xb)
             xrb[x] = xsb[x]
 
     def back_finish():
-        arrive(X, lambda p: xrb.at[p], s_xb, r_xb)
+        arrive(X, slots(xrb, nx), s_xb, r_xb)
         out = xrb[0].astype(F32)
         for p in range(1, nx):
             out = out + xrb[p].astype(F32)
         gow[:, front:] = out
 
-    early = steps[: (5 * nz) // 8]
-    later = steps[(5 * nz) // 8 :]
+    early, later = steps[: (5 * nz) // 8], steps[(5 * nz) // 8 :]
     order = iter(steps)
 
     def back_steps(count):
@@ -571,17 +567,17 @@
             if i is not None:
                 back_rows(i)
 
-    for n, i in enumerate(early):
+    for n, i in enumerate(steps):
         weight_block(i)
         if n == 0:
             back_steps(1)
     exchange_2(lb2, tb2, ub2, s_h1, r_h1, s_h2, r_h2, True)
-    arrive(X, lambda p: gx.at[p], s_gx, r_gx)
+    arrive(X, slots(gx, nx), s_gx, r_gx)
     row = gx[0]
     for k in range(1, nx):
         row = row + gx[k]
     gz[z] = row
-    send(Z, lambda p: gz.at[z], gz.at[z], s_gz, r_gz)
+    send(Z, lambda p: gz.at[z], gz.at[z], slots(gz, nz), s_gz, r_gz)
 
     def inside_back(k, _):
         rows = at_chunk(k)
@@ -592,8 +588,9 @@
         for p in range(pairs):
             lanes = slice(128 * p, 128 * (p + 1))
             x_pair = xb[rows, lanes]
-            grads = split_pair(dyb[rows, lanes].astype(BF16))
-            dots = dot(grads, x_pair, 1, 1)
+            high, low = pieces(dyb[rows, lanes], 2)
+            grads = split_pair(high)
+            dots = dot(grads, x_pair, 1, 1) + dot(split_pair(low), x_pair, 1, 1)
             mixing = []
             for i in range(2):
                 h = 2 * p + i
@@ -607,24 +604,22 @@
                 segr[k, h : h + 1, :] = jnp.sum(terms, axis=0, keepdims=True)
                 mixing.append((decay * both).astype(BF16))
             dxi[rows, lanes] = dot(jnp.concatenate(mixing, axis=0), grads, 0, 0)
-        sumd[k] = summed
+        accp[rows, :] = dot(summed.astype(BF16), c_ref[rows, :], 0, 0)
         segc[k] = row_sums - segr[k].T
         scaled = dyb[rows, :] * startb[rows, :]
-        accr[rows, :] = dot(summed.astype(BF16), b_ref[rows, :]) + dot(
-            scaled.astype(BF16), stb[k].astype(BF16), 1, 1
-        )
+        accr[rows, :] = (
+            dot(summed.astype(BF16), b_ref[rows, :])
+            + dot(scaled.astype(BF16), stb[k].astype(BF16), 1, 1)
+        ).astype(BF16)
         return 0
 
     lax.fori_loop(0, chunks // 2, inside_back, 0)
-    for i in early[:1]:
-        weight_relay(i)
     back_steps(2 if nz == 8 else 0)
     exchange_3(ub2, qs2, qb2, s_h2, r_h2, s_h3, r_h3, True)
     lax.fori_loop(chunks // 2, chunks, inside_back, 0)
-    for i in early[1:3]:
+    back_steps(2 if nz == 8 else 0)
+    for i in early[:3]:
         weight_relay(i)
-    for i in early[:1]:
-        weight_rows(i)
     exchange_4(qb2, lb2, vs2, h_in, s_h3, r_h3, s_h4, r_h4, True)
 
     share = tokens // ntp
@@ -634,31 +629,34 @@
             TP,
             lambda p: acc.at[pl.ds(pl.multiple_of(p * share, share), share)],
             red.at[which, t],
+            red.at[which, pl.ds(0, ntp - 1)],
             ssem,
             rsem,
         )
         red[which, t] = take_rows(acc, t, share)
 
     def reduce_2(which, s1, r1, ssem, rsem):
-        arrive(TP, lambda p: red.at[which, p], s1, r1)
-        out = red[which, 0]
+        arrive(TP, red.at[which, pl.ds(0, ntp - 1)], s1, r1)
+        out = red[which, 0].astype(F32)
         for p in range(1, ntp):
-            out = out + red[which, p]
+            out = out + red[which, p].astype(F32)
         redo[which, t] = out
-        send(TP, lambda p: redo.at[which, t], redo.at[which, t], ssem, rsem)
+        send(TP, lambda p: redo.at[which, t], redo.at[which, t], redo.at[which, pl.ds(0, ntp - 1)], ssem, rsem)
 
     def reduce_3(out_ref, which, ssem, rsem):
-        arrive(TP, lambda p: redo.at[which, p], ssem, rsem)
+        arrive(TP, redo.at[which, pl.ds(0, ntp - 1)], ssem, rsem)
         for p in range(ntp):
             out_ref[p * share : (p + 1) * share, :] = redo[which, p]
 
-    for i in later:
-        weight_block(i)
     reduce_1(accr, 0, s_c1, r_c1)
-    for i in early[3:4]:
+    for i in early[:1]:
+        weight_rows(i)
+    for i in early[3:]:
         weight_relay(i)
     for i in early[1:3]:
         weight_rows(i)
+    for i in later:
+        weight_relay(i)
     back_steps(2 if nz == 8 else 0)
     exchange_5(h_in, s_h4, r_h4)
 
@@ -666,15 +664,13 @@
         k = chunks - 1 - i
         rows = at_chunk(k)
         hst[k] = run
-        accw[rows, :] = dot(sumd[k].astype(BF16), c_ref[rows, :], 0, 0) + dot(
-            (xb[rows, :].astype(F32) * endb[rows, :]).astype(BF16), run.astype(BF16), 1, 1
-        )
+        accw[rows, :] = (accp[rows, :] + dot(xe[rows, :], run.astype(BF16), 1, 1)).astype(BF16)
         return totb[k] * run + hcb[k]
 
     lax.fori_loop(0, chunks, states_back, h_in[...].astype(F32))
     reduce_1(accw, 1, s_w1, r_w1)
-    for i in early[4:]:
-        weight_relay(i)
+    for i in early[3:]:
+        weight_rows(i)
 
     def finish(k, _):
         rows = at_chunk(k)
@@ -690,66 +686,54 @@
         )
         final = head_sums(jnp.broadcast_to(final, (8, width)))[0:1]
         whole = sum(dot(upper, part) for part in pieces(seg, 2)) + final
-        sumd[k, 0:SLOT, :] = whole.T
+        sumd[k] = whole.T
         return 0
 
     lax.fori_loop(0, chunks // 2, finish, 0)
-    for i in later[:1]:
-        weight_relay(i)
-    for i in early[3:4]:
-        weight_rows(i)
-    back_steps(2 if nz == 8 else 0)
+    reduce_2(0, s_c1, r_c1, s_c2, r_c2)
+    back_steps(nz)
     lax.fori_loop(chunks // 2, chunks, finish, 0)
     for k in range(chunks):
         gdecay[:, k * L : (k + 1) * L] = sumd[k, 0:heads, :]
-    for i in later[1:2]:
-        weight_relay(i)
-    for i in early[4:]:
+    reduce_2(1, s_w1, r_w1, s_w2, r_w2)
+    for i in later[:-1]:
         weight_rows(i)
-    reduce_2(0, s_c1, r_c1, s_c2, r_c2)
-    reduce_2(1, s_w1, r_w1, s_w2, r_w2)
-    for i in later[2:]:
-        weight_relay(i)
-    arrive(Z, lambda p: gz.at[p], s_gz, r_gz)
+    arrive(Z, slots(gz, nz), s_gz, r_gz)
     row = gz[0]
     for k in range(1, nz):
         row = row + gz[k]
     ggain[...] = row[0:1]
     gskip[...] = head_sums(jnp.concatenate([row, jnp.zeros((6, width), F32)], axis=0))[1:2, 0:heads]
-    back_steps(nz)
-    for i in later[:-1]:
-        weight_rows(i)
     reduce_3(gread, 0, s_c2, r_c2)
+    back_finish()
+    weight_rows(nz)
     reduce_3(gwrite, 1, s_w2, r_w2)
-    weight_rows(nz)
-    back_finish()
     for copy in pending:
         copy.wait_send()
 
+    def all_left(whole, sem):
+        rcopy(whole, whole, sem, r_ag.at[0], dev_t(sibling)).wait_send()
+
+    all_left(cot.at[pl.ds(0, (2 * ny - 1) * shard)], s_ag.at[0])
+    for kind in range(3):
+        if nx == 4 or (nx > 1 and kind == 1):
+            all_left(xa, s_rx.at[kind])
+    all_left(slots(zra, nz), s_za.at[0])
+    all_left(slots(zrb, nz), s_zb.at[0])
+
 
 def copy_out(*refs):
     count = 8
-    sources, targets, scratch, sem_in, sem_out = (
-        refs[:count],
-        refs[count : 2 * count],
-        refs[2 * count : -2],
-        refs[-2],
-        refs[-1],
-    )
-    large = [k for k in range(count) if k not in (5, 6)]
-    loads = [
-        pltpu.make_async_copy(sources[k], scratch[i], sem_in.at[i]) for i, k in enumerate(large)
+    sources, targets, sem = refs[:count], refs[count : 2 * count], refs[-1]
+    stores = [
+        pltpu.make_async_copy(sources[k], targets[k], sem.at[k])
+        for k in range(count)
+        if k not in (5, 6)
     ]
-    stores = [
-        pltpu.make_async_copy(scratch[i], targets[k], sem_out.at[i]) for i, k in enumerate(large)
-    ]
-    for load in loads:
-        load.start()
+    for store in stores:
+        store.start()
     for k in (5, 6):
         targets[k][...] = sources[k][...].reshape(targets[k].shape)
-    for load, store in zip(loads, stores):
-        load.wait()
-        store.start()
     for store in stores:
         store.wait()
 
@@ -757,21 +741,18 @@
 def hand_out(outs):
     vmem = pl.BlockSpec(memory_space=pltpu.VMEM)
     hbm = pl.BlockSpec(memory_space=pl.ANY)
-    specs = [vmem if k in (5, 6) else hbm for k in range(8)]
     shapes = [
         jax.ShapeDtypeStruct(o.shape[1:] if k in (5, 6) else o.shape, o.dtype)
         for k, o in enumerate(outs)
     ]
-    large = [o for k, o in enumerate(outs) if k not in (5, 6)]
     done = pl.pallas_call(
         copy_out,
         out_shape=shapes,
-        in_specs=specs,
-        out_specs=specs,
-        scratch_shapes=[pltpu.VMEM(o.shape, o.dtype) for o in large]
-        + [pltpu.SemaphoreType.DMA((6,)), pltpu.SemaphoreType.DMA((6,))],
+        in_specs=[vmem] * 8,
+        out_specs=[vmem if k in (5, 6) else hbm for k in range(8)],
+        scratch_shapes=[pltpu.SemaphoreType.DMA((8,))],
         name="hand_out",
-    )(*outs)
+    )(*[pltpu.with_memory_space_constraint(o, pltpu.VMEM) for o in outs])
     return (*done[:7], done[7].T)
 
 
@@ -799,12 +780,12 @@
             pltpu.VMEM((nz, erows, width), F32),
             pltpu.VMEM((nz, erows, width), F32),
             pltpu.VMEM((nz, erows, width), F32),
-            pltpu.VMEM((nx, qrows, width), kind),
-            pltpu.VMEM((n, width), kind),
+            pltpu.VMEM((nx, qrows, width), F32),
+            pltpu.VMEM((n, width), F32),
         ]
 
-    def sems(*shape):
-        return [pltpu.SemaphoreType.DMA(shape), pltpu.SemaphoreType.DMA(shape)]
+    def sems(sends, lands):
+        return [pltpu.SemaphoreType.DMA((sends,)), pltpu.SemaphoreType.DMA((lands,))]
 
     scratch = [
         pltpu.VMEM((tokens, width), BF16),
@@ -813,6 +794,10 @@
         wide(BF16),
         *[wide() for _ in range(7)],
         wide(BF16),
+        wide(),
+        wide(),
+        wide(BF16),
+        pltpu.VMEM((tokens, n), F32),
         pltpu.VMEM((chunks, SLOT, L), F32),
         pltpu.VMEM((chunks, L, SLOT), F32),
         pltpu.VMEM((chunks, 1, width), F32),
@@ -822,7 +807,7 @@
         pltpu.VMEM((chunks, n, width), F32),
         pltpu.VMEM((chunks, n, width), F32),
         pltpu.VMEM((chunks, n, width), F32),
-        pltpu.VMEM((chunks, L, L), F32),
+        pltpu.VMEM((chunks, SLOT, L), F32),
         pltpu.VMEM((chunks, SLOT, L), F32),
         pltpu.VMEM((chunks, L, SLOT), F32),
         wide(),
@@ -840,44 +825,39 @@
         *[pltpu.VMEM((nz, columns, front), BF16) for _ in range(6)],
         *[pltpu.VMEM((nz, shard, width - front), BF16) for _ in range(2)],
         *[pltpu.VMEM((nx, columns, width - front), BF16) for _ in range(2)],
-        pltpu.VMEM((tokens, n), F32),
-        pltpu.VMEM((tokens, n), F32),
-        pltpu.VMEM((2, ntp, share, n), F32),
+        pltpu.VMEM((tokens, n), BF16),
+        pltpu.VMEM((tokens, n), BF16),
+        pltpu.VMEM((2, ntp, share, n), BF16),
         pltpu.VMEM((2, ntp, share, n), F32),
         pltpu.SemaphoreType.DMA((3,)),
-        *sems(10),
-        *sems(nx),
-        *sems(nz),
-        *(sems(nx) + sems(nz) + sems(nz) + sems(nx)),
-        *(sems(nx) + sems(nz) + sems(nz) + sems(nx)),
-        *sems(ntp),
-        *sems(nx),
-        *sems(nz),
-        *sems(3, nz),
-        *sems(nz),
-        *sems(nz),
-        *sems(nx),
-        *(sems(ntp) * 4),
+        *sems(1, 10),
+        *(sems(1, 1) * 2),
+        *(sems(1, 1) * 8),
+        *(sems(1, 1) * 3),
+        pltpu.SemaphoreType.DMA((3,)),
+        pltpu.SemaphoreType.DMA((3, nz)),
+        *(sems(1, nz) * 2),
+        *(sems(1, 1) * 5),
     ]
     vmem = pl.BlockSpec(memory_space=pltpu.VMEM)
     hbm = pl.BlockSpec(memory_space=pl.ANY)
     outs = pl.pallas_call(
         functools.partial(core, nx, nz, ntp),
         out_shape=(
-            jax.ShapeDtypeStruct((tokens, width), BF16),
-            jax.ShapeDtypeStruct((tokens, width), BF16),
-            jax.ShapeDtypeStruct((tokens, n), F32),
-            jax.ShapeDtypeStruct((tokens, n), F32),
-            jax.ShapeDtypeStruct((heads, tokens), F32),
-            jax.ShapeDtypeStruct((1, heads), F32),
-            jax.ShapeDtypeStruct((1, width), F32),
-            jax.ShapeDtypeStruct((columns, width), F32),
+            pltpu.VMEM((tokens, width), BF16),
+            pltpu.VMEM((tokens, width), BF16),
+            pltpu.VMEM((tokens, n), F32),
+            pltpu.VMEM((tokens, n), F32),
+            pltpu.VMEM((heads, tokens), F32),
+            pltpu.VMEM((1, heads), F32),
+            pltpu.VMEM((1, width), F32),
+            pltpu.VMEM((columns, width), F32),
         ),
         in_specs=[vmem, vmem, hbm, vmem, vmem, vmem, pl.BlockSpec(memory_space=pltpu.SMEM), vmem, hbm, hbm],
         out_specs=(vmem,) * 8,
         scratch_shapes=scratch,
         compiler_params=pltpu.CompilerParams(
-            collective_id=0, has_side_effects=True, vmem_limit_bytes=60 * 1024 * 1024
+            collective_id=0, has_side_effects=True, vmem_limit_bytes=54 * 1024 * 1024
         ),
         name="layer_backward",
     )(packed, expo, gate, write, read, decay, skip[None, :], gain, weight, cot)

time: 82.9 us -> 77.1 us (0.930)
  Pallas kernels: 82.1 us -> 76.3 us
    pallas_call x2, Pallas kernels: 82.1 us -> 76.3 us  [the longest x1 74.4 us: on_device(): pl.pallas_call(functools.partial(core, nx, nz, ntp), out_shape=(pltpu.VME...]
where the time goes in v5:
time: 77.1 us; the launch traced here: 77 us
  Pallas kernels  76.3 us (99%)
    pallas_call x1, Pallas kernels, on_device(): pl.pallas_call(functools.partial(core, nx, nz, ntp), out_shape=(pltpu.VME...  74.4 us
    pallas_call x1, Pallas kernels, hand_out(): pl.pallas_call(copy_out, out_shape=shapes, in_specs=[vmem] * 8, out_specs...  1.95 us

profile of v5, /device:TPU:1, one launch (start us, length us, event | category | flops | bytes accessed | tf_op | source)
XLA Modules:
  0.0 77.0 jit_solution(15567219799846655798)
XLA Ops:
  0.6 74.4 %layer_backward.1 = (bf16[512,640]{1,0:T(8,128)(2,1)S(1)}, bf16[512,640]{1,0:T(8,128)(2,1)S(1)}, f32[512,128]{1,0:T(8,128)S(1)}, f32[512,128]{1,0:T(8,128)S(1)},...) custom-call(s32[64,640]{1,0:T(8,128)} %packed.1, s32[5,512]{1,0:T(8,128)} %expo.1, ...), custom_call_target="tpu_custom_call" | custom-call | tf_op jit(solution)/shard_map/layer_backward/pallas_call | solution.py:844
  75.0 1.9 %hand_out.1 = (bf16[512,640]{1,0:T(8,128)(2,1)}, bf16[512,640]{1,0:T(8,128)(2,1)}, f32[512,128]{1,0:T(8,128)}, f32[512,128]{1,0:T(8,128)}, f32[10,512]{1,0:T(8,1...) custom-call(bf16[512,640]{1,0:T(8,128)(2,1)S(1)} %get-tuple-element.24.refs_0_, ...), custom_call_target="tpu_custom_call" | custom-call | tf_op jit(solution)/shard_map/hand_out/pallas_call | solution.py:748

commit v6 on v5

--- a/solution.py
+++ b/solution.py
@@ -45,13 +45,13 @@
 def core(nx, nz, ntp, packed, expo, gate_hbm, b_ref, c_ref, ld_ref, skip_ref, gain_ref, w_hbm, cot_hbm,
          gin, ggate, gwrite, gread, gdecay, gskip, ggain, gow, *scratch):
     (gate_v, w_v, cot, xb, yb, gvb, mixb, dyb, rsb, endb, startb,
-     normed, act, gvg, xe, accp, csr, csc, totb, dec, cross, gb, stb, hcb, hst, sumd, segr, segc, dxi,
+     normed, act, gvg, xe, xl, accp, csr, csc, totb, dec, cross, gb, stb, hcb, sumd, segr, segc, dxi,
      sloc, lb, tb, ub, qs, qb, vs, s_in,
-     rloc, lb2, tb2, ub2, qs2, qb2, vs2, h_in,
+     rloc, lb2, tb2, ub2, qs2, qb2, vs2, h_in, vl2, h_low,
      vtop, dxs, dzs, sums, totc, gx, gz, pwa, pwb, xa, xd, xm, xc, zsa, zra, zsb, zrb, xsb, xrb, accw, accr, red, redo,
      cp_sem, s_ag, r_ag, s_dx, r_dx, s_dz, r_dz,
      s_p1, r_p1, s_p2, r_p2, s_p3, r_p3, s_p4, r_p4,
-     s_h1, r_h1, s_h2, r_h2, s_h3, r_h3, s_h4, r_h4,
+     s_h1, r_h1, s_h2, r_h2, s_h3, r_h3, s_h4, r_h4, s_hl, r_hl,
      s_tp, r_tp, s_gx, r_gx, s_gz, r_gz, s_rx, r_rx, s_za, r_za, s_zb, r_zb, s_xb, r_xb,
      s_w1, r_w1, s_w2, r_w2, s_c1, r_c1, s_c2, r_c2) = scratch
     tokens, width = xb.shape
@@ -81,7 +81,7 @@
 
     def send(group, src_of, dst, whole, ssem, rsem):
         n, me, dev = group
-        for d in range(1, n):
+        for d in sorted(range(1, n), key=lambda d: -min(d, n - d)):
             p = lax.rem(me + d, n)
             rcopy(src_of(p), dst, ssem.at[0], rsem.at[0], dev(p)).start()
         if n > 1:
@@ -174,7 +174,7 @@
         rows = slice(k * L, (k + 1) * L)
         weighted = xb[rows, :].astype(F32) * endb[rows, :]
         parts = pieces(weighted, 2)
-        xe[rows, :] = parts[0]
+        xe[rows, :], xl[rows, :] = parts
         gb[k] = sum(dot(b_ref[rows, :], part, 0, 0) for part in parts)
         run = totb[k] * run + gb[k]
     sloc[...] = run
@@ -286,11 +286,18 @@
         order = range(nx - 1, -1, -1) if backward else range(nx)
         row = vtop[...]
         for k in order:
-            vsend[k] = row.astype(vsend.dtype)
+            if backward:
+                vsend[k], vl2[k] = pieces(row, 2)
+            else:
+                vsend[k] = row
             row = dxs[k] * row + lbuf[k].astype(F32)
-        mine = result.at[pl.ds(pl.multiple_of(x * qrows, qrows), qrows)]
-        send(X, lambda p: vsend.at[p], mine, result.at[pl.ds(0, (nx - 1) * qrows)], ssem, rsem)
-        result[pl.ds(pl.multiple_of(x * qrows, qrows), qrows), :] = vsend[x]
+        mine = pl.ds(pl.multiple_of(x * qrows, qrows), qrows)
+        rest = pl.ds(0, (nx - 1) * qrows)
+        send(X, lambda p: vsend.at[p], result.at[mine], result.at[rest], ssem, rsem)
+        result[mine, :] = vsend[x]
+        if backward:
+            send(X, lambda p: vl2.at[p], h_low.at[mine], h_low.at[rest], s_hl, r_hl)
+            h_low[mine, :] = vl2[x]
 
     def exchange_5(result, s4, r4):
         arrive(X, result.at[pl.ds(0, (nx - 1) * qrows)], s4, r4)
@@ -478,6 +485,8 @@
         terms = dot(cot[pl.ds(pl.multiple_of(k * shard, shard), shard), :], normed[...]).astype(BF16)
         pwa[k] = terms[:, :front]
         pwb[k] = terms[:, front:]
+
+    def block_send(i):
         near, far = sides(i)
         if nx == 4:
             weight_send(0, i, near)
@@ -558,7 +567,9 @@
             out = out + xrb[p].astype(F32)
         gow[:, front:] = out
 
-    early, later = steps[: (5 * nz) // 8], steps[(5 * nz) // 8 :]
+    def batch(first, end):
+        return steps[(first * nz) // 8 : (end * nz) // 8]
+
     order = iter(steps)
 
     def back_steps(count):
@@ -569,6 +580,8 @@
 
     for n, i in enumerate(steps):
         weight_block(i)
+        if i in batch(0, 4):
+            block_send(i)
         if n == 0:
             back_steps(1)
     exchange_2(lb2, tb2, ub2, s_h1, r_h1, s_h2, r_h2, True)
@@ -604,22 +617,29 @@
                 segr[k, h : h + 1, :] = jnp.sum(terms, axis=0, keepdims=True)
                 mixing.append((decay * both).astype(BF16))
             dxi[rows, lanes] = dot(jnp.concatenate(mixing, axis=0), grads, 0, 0)
-        accp[rows, :] = dot(summed.astype(BF16), c_ref[rows, :], 0, 0)
+        sum_parts = pieces(summed, 2)
+        accp[rows, :] = sum(dot(part, c_ref[rows, :], 0, 0) for part in sum_parts)
         segc[k] = row_sums - segr[k].T
         scaled = dyb[rows, :] * startb[rows, :]
         accr[rows, :] = (
-            dot(summed.astype(BF16), b_ref[rows, :])
-            + dot(scaled.astype(BF16), stb[k].astype(BF16), 1, 1)
+            sum(dot(part, b_ref[rows, :]) for part in sum_parts)
+            + sum(dot(part, stb[k].astype(BF16), 1, 1) for part in pieces(scaled, 2))
         ).astype(BF16)
         return 0
 
     lax.fori_loop(0, chunks // 2, inside_back, 0)
+    for i in batch(0, 1):
+        weight_relay(i)
     back_steps(2 if nz == 8 else 0)
     exchange_3(ub2, qs2, qb2, s_h2, r_h2, s_h3, r_h3, True)
+    for i in batch(4, 8):
+        block_send(i)
     lax.fori_loop(chunks // 2, chunks, inside_back, 0)
+    for i in batch(1, 3):
+        weight_relay(i)
+    for i in batch(0, 1):
+        weight_rows(i)
     back_steps(2 if nz == 8 else 0)
-    for i in early[:3]:
-        weight_relay(i)
     exchange_4(qb2, lb2, vs2, h_in, s_h3, r_h3, s_h4, r_h4, True)
 
     share = tokens // ntp
@@ -640,22 +660,20 @@
         out = red[which, 0].astype(F32)
         for p in range(1, ntp):
             out = out + red[which, p].astype(F32)
-        redo[which, t] = out
+        redo[which, t] = out.astype(BF16)
         send(TP, lambda p: redo.at[which, t], redo.at[which, t], redo.at[which, pl.ds(0, ntp - 1)], ssem, rsem)
 
     def reduce_3(out_ref, which, ssem, rsem):
         arrive(TP, redo.at[which, pl.ds(0, ntp - 1)], ssem, rsem)
         for p in range(ntp):
-            out_ref[p * share : (p + 1) * share, :] = redo[which, p]
+            out_ref[p * share : (p + 1) * share, :] = redo[which, p].astype(F32)
 
     reduce_1(accr, 0, s_c1, r_c1)
-    for i in early[:1]:
+    for i in batch(3, 4):
+        weight_relay(i)
+    for i in batch(1, 3):
         weight_rows(i)
-    for i in early[3:]:
-        weight_relay(i)
-    for i in early[1:3]:
-        weight_rows(i)
-    for i in later:
+    for i in batch(4, 6):
         weight_relay(i)
     back_steps(2 if nz == 8 else 0)
     exchange_5(h_in, s_h4, r_h4)
@@ -663,19 +681,17 @@
     def states_back(i, run):
         k = chunks - 1 - i
         rows = at_chunk(k)
-        hst[k] = run
-        accw[rows, :] = (accp[rows, :] + dot(xe[rows, :], run.astype(BF16), 1, 1)).astype(BF16)
+        state = run.astype(BF16)
+        late = dot(xe[rows, :], state, 1, 1) + dot(xl[rows, :], state, 1, 1)
+        accw[rows, :] = (accp[rows, :] + late).astype(BF16)
         return totb[k] * run + hcb[k]
 
     lax.fori_loop(0, chunks, states_back, h_in[...].astype(F32))
     reduce_1(accw, 1, s_w1, r_w1)
-    for i in early[3:]:
-        weight_rows(i)
-
-    def finish(k, _):
+    def finish(i, run):
+        k = chunks - 1 - i
         rows = at_chunk(k)
         grad_y = dyb[rows, :]
-        run = hst[k]
         write = endb[rows, :] * sum(dot(b_ref[rows, :], part) for part in pieces(run, 2))
         gin[rows, :] = (skip_row * grad_y + dxi[rows, :] + write).astype(BF16)
         leaving = xb[rows, :].astype(F32) * write
@@ -687,16 +703,22 @@
         final = head_sums(jnp.broadcast_to(final, (8, width)))[0:1]
         whole = sum(dot(upper, part) for part in pieces(seg, 2)) + final
         sumd[k] = whole.T
-        return 0
-
-    lax.fori_loop(0, chunks // 2, finish, 0)
+        return totb[k] * run + hcb[k]
+
+    exchange_5(h_low, s_hl, r_hl)
+    run = lax.fori_loop(0, 3 * chunks // 4, finish, h_in[...].astype(F32) + h_low[...].astype(F32))
+    for i in batch(3, 5):
+        weight_rows(i)
+    for i in batch(6, 8):
+        weight_relay(i)
+
+    reduce_2(1, s_w1, r_w1, s_w2, r_w2)
     reduce_2(0, s_c1, r_c1, s_c2, r_c2)
-    back_steps(nz)
-    lax.fori_loop(chunks // 2, chunks, finish, 0)
+    lax.fori_loop(3 * chunks // 4, chunks, finish, run)
     for k in range(chunks):
         gdecay[:, k * L : (k + 1) * L] = sumd[k, 0:heads, :]
-    reduce_2(1, s_w1, r_w1, s_w2, r_w2)
-    for i in later[:-1]:
+    back_steps(nz)
+    for i in batch(5, 8)[:-1]:
         weight_rows(i)
     arrive(Z, slots(gz, nz), s_gz, r_gz)
     row = gz[0]
@@ -780,8 +802,8 @@
             pltpu.VMEM((nz, erows, width), F32),
             pltpu.VMEM((nz, erows, width), F32),
             pltpu.VMEM((nz, erows, width), F32),
-            pltpu.VMEM((nx, qrows, width), F32),
-            pltpu.VMEM((n, width), F32),
+            pltpu.VMEM((nx, qrows, width), kind),
+            pltpu.VMEM((n, width), kind),
         ]
 
     def sems(sends, lands):
@@ -797,6 +819,7 @@
         wide(),
         wide(),
         wide(BF16),
+        wide(BF16),
         pltpu.VMEM((tokens, n), F32),
         pltpu.VMEM((chunks, SLOT, L), F32),
         pltpu.VMEM((chunks, L, SLOT), F32),
@@ -806,13 +829,13 @@
         pltpu.VMEM((chunks, n, width), F32),
         pltpu.VMEM((chunks, n, width), F32),
         pltpu.VMEM((chunks, n, width), F32),
-        pltpu.VMEM((chunks, n, width), F32),
         pltpu.VMEM((chunks, SLOT, L), F32),
         pltpu.VMEM((chunks, SLOT, L), F32),
         pltpu.VMEM((chunks, L, SLOT), F32),
         wide(),
         *exchange(F32),
         *exchange(BF16),
+        *exchange(BF16)[-2:],
         pltpu.VMEM((qrows, width), F32),
         pltpu.VMEM((nx, 1, width), F32),
         pltpu.VMEM((nz, 1, width), F32),
@@ -828,11 +851,11 @@
         pltpu.VMEM((tokens, n), BF16),
         pltpu.VMEM((tokens, n), BF16),
         pltpu.VMEM((2, ntp, share, n), BF16),
-        pltpu.VMEM((2, ntp, share, n), F32),
+        pltpu.VMEM((2, ntp, share, n), BF16),
         pltpu.SemaphoreType.DMA((3,)),
         *sems(1, 10),
         *(sems(1, 1) * 2),
-        *(sems(1, 1) * 8),
+        *(sems(1, 1) * 9),
         *(sems(1, 1) * 3),
         pltpu.SemaphoreType.DMA((3,)),
         pltpu.SemaphoreType.DMA((3, nz)),

time: 77.1 us -> 73.4 us (0.952)
  Pallas kernels: 76.3 us -> 72.7 us
    pallas_call x1, Pallas kernels: 74.4 us -> 70.7 us  [on_device(): pl.pallas_call(functools.partial(core, nx, nz, ntp), out_shape=(pltpu.VME...]
where the time goes in v6:
time: 73.4 us; the launch traced here: 73.3 us
  Pallas kernels  72.7 us (99%)
    pallas_call x1, Pallas kernels, on_device(): pl.pallas_call(functools.partial(core, nx, nz, ntp), out_shape=(pltpu.VME...  70.7 us
    pallas_call x1, Pallas kernels, hand_out(): pl.pallas_call(copy_out, out_shape=shapes, in_specs=[vmem] * 8, out_specs...  1.95 us

profile of v6, /device:TPU:1, one launch (start us, length us, event | category | flops | bytes accessed | tf_op | source)
XLA Modules:
  0.0 73.3 jit_solution(7682945348772034624)
XLA Ops:
  0.6 70.7 %layer_backward.1 = (bf16[512,640]{1,0:T(8,128)(2,1)S(1)}, bf16[512,640]{1,0:T(8,128)(2,1)S(1)}, f32[512,128]{1,0:T(8,128)S(1)}, f32[512,128]{1,0:T(8,128)S(1)},...) custom-call(s32[64,640]{1,0:T(8,128)} %packed.1, s32[5,512]{1,0:T(8,128)} %expo.1, ...), custom_call_target="tpu_custom_call" | custom-call | tf_op jit(solution)/shard_map/layer_backward/pallas_call | solution.py:867
  71.3 1.9 %hand_out.1 = (bf16[512,640]{1,0:T(8,128)(2,1)}, bf16[512,640]{1,0:T(8,128)(2,1)}, f32[512,128]{1,0:T(8,128)}, f32[512,128]{1,0:T(8,128)}, f32[10,512]{1,0:T(8,1...) custom-call(bf16[512,640]{1,0:T(8,128)(2,1)S(1)} %get-tuple-element.24.refs_0_, ...), custom_call_target="tpu_custom_call" | custom-call | tf_op jit(solution)/shard_map/hand_out/pallas_call | solution.py:770

commit v7 on v6

--- a/solution.py
+++ b/solution.py
@@ -42,9 +42,9 @@
     )
 
 
-def core(nx, nz, ntp, packed, expo, gate_hbm, b_ref, c_ref, ld_ref, skip_ref, gain_ref, w_hbm, cot_hbm,
+def core(nx, nz, ntp, packed_hbm, expo_hbm, gate_hbm, b_hbm, c_hbm, ld_hbm, skip_hbm, gain_hbm, w_hbm, cot_hbm,
          gin, ggate, gwrite, gread, gdecay, gskip, ggain, gow, *scratch):
-    (gate_v, w_v, cot, xb, yb, gvb, mixb, dyb, rsb, endb, startb,
+    (packed, expo, b_ref, c_ref, ld_ref, skip_ref, gain_ref, gate_v, w_v, cot, xb, yb, gvb, mixb, dyb, rsb, endb, startb,
      normed, act, gvg, xe, xl, accp, csr, csc, totb, dec, cross, gb, stb, hcb, sumd, segr, segc, dxi,
      sloc, lb, tb, ub, qs, qb, vs, s_in,
      rloc, lb2, tb2, ub2, qs2, qb2, vs2, h_in, vl2, h_low,
@@ -101,6 +101,23 @@
     load_cot = pltpu.make_async_copy(cot_hbm, cot_rows(t), cp_sem.at[0])
     load_gate = pltpu.make_async_copy(gate_hbm, gate_v, cp_sem.at[1])
     load_w = pltpu.make_async_copy(w_hbm, w_v, cp_sem.at[2])
+    small = [
+        pltpu.make_async_copy(source, target, cp_sem.at[3 + i])
+        for i, (source, target) in enumerate(
+            (
+                (ld_hbm, ld_ref),
+                (packed_hbm, packed),
+                (expo_hbm, expo),
+                (b_hbm, b_ref),
+                (c_hbm, c_ref),
+                (skip_hbm, skip_ref),
+                (gain_hbm, gain_ref),
+            )
+        )
+    ]
+    load_ld, load_packed, load_expo, *load_rest = small
+    for load in small:
+        load.start()
     load_cot.start()
     load_gate.start()
     load_w.start()
@@ -126,6 +143,7 @@
 
     csr[...] = jnp.zeros_like(csr)
     segr[...] = jnp.zeros_like(segr)
+    load_ld.wait()
     for k in range(chunks):
         csr[k, 0:heads, :] = ld_ref[:, k * L : (k + 1) * L]
     rows = csr[...].reshape(chunks * SLOT, L)
@@ -143,6 +161,8 @@
         startb[k * L : (k + 1) * L, :] = jnp.exp(logs)
     dxs[x] = jnp.exp(log_total)
 
+    load_packed.wait()
+    load_expo.wait()
     powers = lax.shift_left(jnp.ones_like(expo[...]), expo[...] + 5).astype(F32) * (1.0 / 32.0)
     nibble = 4 * iota((8, width), 0)
     for k in range(chunks):
@@ -169,6 +189,8 @@
         )
         xb[k * L : (k + 1) * L, :] = (fields.astype(F32) * wide).astype(BF16)
 
+    for load in load_rest:
+        load.wait()
     run = jnp.zeros((128, width), F32)
     for k in range(chunks):
         rows = slice(k * L, (k + 1) * L)
@@ -688,6 +710,7 @@
 
     lax.fori_loop(0, chunks, states_back, h_in[...].astype(F32))
     reduce_1(accw, 1, s_w1, r_w1)
+    reduce_2(0, s_c1, r_c1, s_c2, r_c2)
     def finish(i, run):
         k = chunks - 1 - i
         rows = at_chunk(k)
@@ -713,7 +736,6 @@
         weight_relay(i)
 
     reduce_2(1, s_w1, r_w1, s_w2, r_w2)
-    reduce_2(0, s_c1, r_c1, s_c2, r_c2)
     lax.fori_loop(3 * chunks // 4, chunks, finish, run)
     for k in range(chunks):
         gdecay[:, k * L : (k + 1) * L] = sumd[k, 0:heads, :]
@@ -810,6 +832,9 @@
         return [pltpu.SemaphoreType.DMA((sends,)), pltpu.SemaphoreType.DMA((lands,))]
 
     scratch = [
+        *[pltpu.VMEM(a.shape, a.dtype) for a in (packed, expo, write, read, decay)],
+        pltpu.SMEM((1, heads), F32),
+        pltpu.VMEM((width,), F32),
         pltpu.VMEM((tokens, width), BF16),
         pltpu.VMEM((width, model), BF16),
         pltpu.VMEM((model, tokens), BF16),
@@ -852,7 +877,7 @@
         pltpu.VMEM((tokens, n), BF16),
         pltpu.VMEM((2, ntp, share, n), BF16),
         pltpu.VMEM((2, ntp, share, n), BF16),
-        pltpu.SemaphoreType.DMA((3,)),
+        pltpu.SemaphoreType.DMA((10,)),
         *sems(1, 10),
         *(sems(1, 1) * 2),
         *(sems(1, 1) * 9),
@@ -876,7 +901,7 @@
             pltpu.VMEM((1, width), F32),
             pltpu.VMEM((columns, width), F32),
         ),
-        in_specs=[vmem, vmem, hbm, vmem, vmem, vmem, pl.BlockSpec(memory_space=pltpu.SMEM), vmem, hbm, hbm],
+        in_specs=[hbm] * 10,
         out_specs=(vmem,) * 8,
         scratch_shapes=scratch,
         compiler_params=pltpu.CompilerParams(

time: 73.4 us -> 71.2 us (0.970)
  Pallas kernels: 72.7 us -> 70.1 us
    pallas_call x1, Pallas kernels: 70.7 us -> 68.1 us  [on_device(): pl.pallas_call(functools.partial(core, nx, nz, ntp), out_shape=(pltpu.VME...]
where the time goes in v7:
time: 71.2 us; the launch traced here: 70.7 us
  Pallas kernels  70.1 us (98%)
    pallas_call x1, Pallas kernels, on_device(): pl.pallas_call(functools.partial(core, nx, nz, ntp), out_shape=(pltpu.VME...  68.1 us
    pallas_call x1, Pallas kernels, hand_out(): pl.pallas_call(copy_out, out_shape=shapes, in_specs=[vmem] * 8, out_specs...  1.95 us

profile of v7, /device:TPU:1, one launch (start us, length us, event | category | flops | bytes accessed | tf_op | source)
XLA Modules:
  0.0 70.7 jit_solution(12802493453930217729)
XLA Ops:
  0.6 68.1 %layer_backward.1 = (bf16[512,640]{1,0:T(8,128)(2,1)S(1)}, bf16[512,640]{1,0:T(8,128)(2,1)S(1)}, f32[512,128]{1,0:T(8,128)S(1)}, f32[512,128]{1,0:T(8,128)S(1)},...) custom-call(s32[64,640]{1,0:T(8,128)} %packed_hbm.1, ...), custom_call_target="tpu_custom_call" | custom-call | tf_op jit(solution)/shard_map/layer_backward/pallas_call | solution.py:892
  68.8 1.9 %hand_out.1 = (bf16[512,640]{1,0:T(8,128)(2,1)}, bf16[512,640]{1,0:T(8,128)(2,1)}, f32[512,128]{1,0:T(8,128)}, f32[512,128]{1,0:T(8,128)}, f32[10,512]{1,0:T(8,1...) custom-call(bf16[512,640]{1,0:T(8,128)(2,1)S(1)} %get-tuple-element.24.refs_0_, ...), custom_call_target="tpu_custom_call" | custom-call | tf_op jit(solution)/shard_map/hand_out/pallas_call | solution.py:792
